TPU v7x, 512 devices: a whole 4x8x8 slice. The times are simulated.
512 devices in a mesh: depth: 256 (over z, y, x), chan: 2 (over core).
Axes of the slice: x: 4, y: 8, z: 8, core: 2. Of those that a mesh axis runs over, the one named last changes fastest.
Arguments:
- feats: bfloat16 [32, 512, 8, 128], P('chan', 'depth'), may hold values from -6 to 6
- weight_one: bfloat16 [32, 32, 27], replicated, may hold values from -0.21875 to 0.21875
- weight_two: bfloat16 [64, 32, 27], replicated, may hold values from -0.21875 to 0.21875
- cotangent: bfloat16 [64, 256, 4, 64], P('chan', 'depth'), may hold values from -6 to 6
Outputs:
- grad_feats: bfloat16 [32, 512, 8, 128], P('chan', 'depth')
- grad_weight_one: float32 [32, 32, 27], P(None, 'chan')
- grad_weight_two: float32 [64, 32, 27], P(None, 'chan')
All inputs are finite; a program needn't handle non-finite values.
Results may differ from a plain program's by a relative error of at most 0.013.
Values may be sent and summed in bfloat16 or wider, within the bound.
No kernel may reach another device: no remote copies, remote signals or barrier semaphores. Data moves between devices by JAX's collectives and lax.ppermute only.
A program may use at most 128 MiB of HBM per device.

v0:
```python
import functools

import jax
import jax.numpy as jnp
from jax import lax
from jax.sharding import Mesh
from jax.sharding import PartitionSpec as P

DEPTH = ("depth_0", "depth_1", "depth_2")


OFFSETS = [
    (first, second, third) for first in range(3) for second in range(3) for third in range(3)
]


def padded_2(block, sides, width):
    for axis, dim in sides:
        count = lax.axis_size(axis)
        forward = [(i, i + 1) for i in range(count - 1)]
        backward = [(target, source) for source, target in forward]
        low = lax.ppermute(
            lax.slice_in_dim(block, block.shape[dim] - width, None, axis=dim), axis, forward
        )
        high = lax.ppermute(lax.slice_in_dim(block, 0, width, axis=dim), axis, backward)
        block = jnp.concatenate([low, block, high], axis=dim)
    return block


def split_up(x, dim, count):
    before, after = (x.shape[:dim], x.shape[dim + 1 :])
    return jnp.moveaxis(x.reshape(*before, count, -1, *after), dim, 0)


def summed_on_arrival(x, axis, dim):
    count = lax.axis_size(axis)
    pieces = lax.all_to_all(split_up(x, dim, count), axis, 0, 0, tiled=True)
    return jnp.sum(pieces.astype(jnp.float32), axis=0)


def joined_along(pieces, dim):
    pieces = jnp.moveaxis(pieces, 0, dim)
    shape = pieces.shape
    return pieces.reshape(*shape[:dim], shape[dim] * shape[dim + 1], *shape[dim + 2 :])


def from_everyone(x, axis):
    copies = jnp.broadcast_to(x, (lax.axis_size(axis), *x.shape))
    return lax.all_to_all(copies, axis, split_axis=0, concat_axis=0, tiled=True)


def gather_directly(x, axis, dim):
    return joined_along(from_everyone(x, axis), dim)


def one_axis_at_a_time(x, axes):
    return functools.reduce(lax.psum, axes, x)


def pad_plane(haloed):
    return jnp.pad(haloed, ((0, 0), (0, 0), (1, 1), (1, 1)))


def cut_edges(haloed, lower_keep, upper_keep):
    count = haloed.shape[1]
    position = lax.iota(jnp.int32, count)
    keep = jnp.where(position == 0, lower_keep, jnp.where(position == count - 1, upper_keep, True))
    return jnp.where(keep[None, :, None, None], haloed, jnp.zeros((), haloed.dtype))


def patch_rows(haloed):
    chans = haloed.shape[0]
    planes = haloed.shape[1] - 2
    height = haloed.shape[2]
    across = haloed.shape[3]
    padded = pad_plane(haloed)
    windows = [
        padded[:, first : first + planes, second : second + height, third : third + across]
        for first, second, third in OFFSETS
    ]
    return jnp.stack(windows, 0).reshape(27 * chans, planes * height * across)


def flat_weight(own):
    return jnp.transpose(own, (0, 2, 1)).reshape(own.shape[0], -1)


def flat_transposed(own):
    return jnp.transpose(own, (2, 1, 0)).reshape(-1, own.shape[0])


def weight_layout(weight_sum, chans):
    return jnp.transpose(weight_sum.reshape(weight_sum.shape[0], 27, chans), (0, 2, 1))


def slope(pre):
    sig = jax.nn.sigmoid(pre)
    return sig * (1.0 + pre * (1.0 - sig))


def grad_fold(transposed, patches, piece):
    count = piece.shape[0]
    padded = pad_plane(piece).reshape(count, -1)
    image_sum = jnp.dot(transposed, padded, preferred_element_type=jnp.float32)
    inner = piece[:, 1:-1].reshape(count, -1)
    rows_part = lax.dot_general(
        inner, patches, (((1,), (1,)), ((), ())), preferred_element_type=jnp.float32
    )
    return (image_sum, rows_part)


def shift_sum(image_sum, chans, planes, height, across):
    shaped = image_sum.reshape(27, chans, planes + 2, height + 2, across + 2)
    total = jnp.zeros((chans, planes, height, across), jnp.float32)
    for index, (first, second, third) in enumerate(OFFSETS):
        total = (
            total
            + shaped[
                index,
                :,
                2 - first : 2 - first + planes,
                2 - second : 2 - second + height,
                2 - third : 2 - third + across,
            ]
        )
    return total


def shards(feats, weight_one, weight_two, cotangent):
    groups = lax.axis_size("chan")
    member = lax.axis_index("chan")
    slabs = lax.axis_size(DEPTH)
    place = lax.axis_index(DEPTH)
    lower_keep = place % slabs != 0
    upper_keep = (place + 1) % slabs != 0
    in_chans, planes, height, across = feats.shape
    mid_chans = weight_one.shape[0] // groups
    out_chans = weight_two.shape[0] // groups
    feats_halo = cut_edges(padded_2(feats, ((DEPTH, 1),), 1), lower_keep, upper_keep)
    patches_one = patch_rows(feats_halo)
    own_one = lax.dynamic_slice_in_dim(weight_one, member * in_chans, in_chans, 1)
    partial_one = jnp.dot(flat_weight(own_one), patches_one, preferred_element_type=jnp.float32)
    pre_one = summed_on_arrival(partial_one.astype(jnp.bfloat16), "chan", 0)
    act_one = jax.nn.silu(pre_one).astype(jnp.bfloat16).reshape(mid_chans, planes, height, across)
    pooled = (
        act_one.astype(jnp.float32)
        .reshape(mid_chans, planes // 2, 2, height // 2, 2, across // 2, 2)
        .mean(axis=(2, 4, 6))
        .astype(jnp.bfloat16)
    )
    pooled_halo = cut_edges(padded_2(pooled, ((DEPTH, 1),), 1), lower_keep, upper_keep)
    patches_two = patch_rows(pooled_halo)
    own_two = lax.dynamic_slice_in_dim(weight_two, member * mid_chans, mid_chans, 1)
    partial_two = jnp.dot(flat_weight(own_two), patches_two, preferred_element_type=jnp.float32)
    pre_two = summed_on_arrival(partial_two.astype(jnp.bfloat16), "chan", 0)
    grad_two = (cotangent.astype(jnp.float32).reshape(out_chans, -1) * slope(pre_two)).astype(
        jnp.bfloat16
    )
    grad_two = grad_two.reshape(out_chans, planes // 2, height // 2, across // 2)
    grad_two_halo = cut_edges(padded_2(grad_two, ((DEPTH, 1),), 1), lower_keep, upper_keep)
    image_two, wsum_two = grad_fold(
        flat_transposed(own_two), patches_two, gather_directly(grad_two_halo, "chan", 0)
    )
    grad_weight_two = weight_layout(wsum_two, mid_chans)
    grad_weight_two = one_axis_at_a_time(grad_weight_two, DEPTH)
    back_pooled = shift_sum(image_two, mid_chans, planes // 2, height // 2, across // 2)
    spread = (
        jnp.broadcast_to(
            back_pooled[:, :, None, :, None, :, None],
            (mid_chans, planes // 2, 2, height // 2, 2, across // 2, 2),
        ).reshape(mid_chans, -1)
        * 0.125
    )
    grad_one = (
        (spread * slope(pre_one)).astype(jnp.bfloat16).reshape(mid_chans, planes, height, across)
    )
    grad_one_halo = cut_edges(padded_2(grad_one, ((DEPTH, 1),), 1), lower_keep, upper_keep)
    image_one, wsum_one = grad_fold(
        flat_transposed(own_one), patches_one, gather_directly(grad_one_halo, "chan", 0)
    )
    grad_weight_one = weight_layout(wsum_one, in_chans)
    grad_weight_one = one_axis_at_a_time(grad_weight_one, DEPTH)
    grad_feats = shift_sum(image_one, in_chans, planes, height, across).astype(jnp.bfloat16)
    return (grad_feats, grad_weight_one, grad_weight_two)


def solution(mesh):
    finer = Mesh(
        mesh.devices.reshape(8, 8, 4, mesh.shape["chan"]), ("depth_0", "depth_1", "depth_2", "chan")
    )
    in_specs = (P("chan", DEPTH, None, None), P(), P(), P("chan", DEPTH, None, None))
    out_specs = (P("chan", DEPTH, None, None), P(None, "chan", None), P(None, "chan", None))
    return jax.shard_map(
        shards, mesh=finer, in_specs=in_specs, out_specs=out_specs, check_vma=False
    )
```

profile of v0, /device:TPU:8, one launch (start us, length us, event | category | flops | bytes accessed | tf_op | source)
XLA Modules:
  0.0 344.0 jit_solution(2406383492196253577)
XLA Ops:
  7.2 0.8 fusion.81
  8.1 3.4 collective-permute-start
  11.5 4.6 %collective-permute-start.1 = (bf16[16,1,8,128]{3,2,1,0:T(8,128)(2,1)S(1)}, bf16[16,1,8,128]{3,2,1,0:T(8,128)(2,1)S(1)}, u32[]{:S(2)}, u32[]{:S(2)}) collective-permute-start(bf16[16,1,8,128]{3,2,1,0:T(8,128)(2,1)S(1)} %get-tuple-element.150), channel_id=1, source_target_pairs={{2,0},{4,2},{6,4},{8,6},{10,8},{12,10},{14,12},{16,14},{18,16},{20... | collective-permute-start | bytes 98312 | tf_op jit(solution)/shard_map/ppermute | solution.py:25
  16.7 1.1 constant_dynamic-slice_fusion.1
  18.0 1.0 maximum_select_fusion
  20.3 0.7 copy.2505
  21.1 0.8 copy.2480
  21.8 0.8 copy.2481
  22.6 0.7 copy.2482
  23.3 0.7 copy.2484
  24.1 0.8 copy.2485
  24.8 0.7 copy.2486
  25.6 0.7 copy.2487
  26.3 0.7 copy.2488
  27.0 0.7 copy.2489
  27.8 0.8 copy.2490
  28.5 0.7 copy.2491
  29.3 0.7 copy.2493
  30.0 0.8 copy.2494
  30.8 0.7 copy.2495
  31.5 0.7 copy.2496
  32.3 0.8 copy.2497
  33.0 0.8 copy.2498
  33.8 0.8 copy.2499
  34.5 10.8 %stack.195 = bf16[27,16,2,8,128]{4,0,3,1,2:T(8,128)(2,1)S(1)} concatenate(bf16[1,16,2,8,128]{4,0,3,1,2:T(2,128)(2,1)S(1)} %copy.2479, bf16[1,16,2,8,128]{4,0,3,1,2:T(2,128)(2,1)} %copy.2480, bf16[1,16,2,8,128]{4,0,3,1,2:T(2,128)(2,1)} %copy.2481, bf16[1,16,2,8,128]{4,0,3,1,2:T(2,128)(2,1)} %copy.2482, bf16[1,16,2,8,128]{4,0,3,1,2:T(2,128)(2,1)S(1)} %copy.2483, ...), dimensions={0} | concatenate | bytes 3538944 | tf_op jit(solution)/shard_map/stack | solution.py:81
  45.4 1.9 copy.2506
  47.3 3.8 %reshape.401 = bf16[432,2048]{1,0:T(8,128)(2,1)} reshape(bf16[27,16,2,8,128]{4,3,2,1,0:T(8,128)(2,1)} %copy.2506) | data formatting | bytes 3538944 | tf_op jit(solution)/shard_map/reshape | solution.py:81
  51.1 1.9 convolution_convert_fusion
  53.1 3.8 %all_to_all.20 = bf16[2,16,2048]{2,1,0:T(8,128)(2,1)S(1)} all-to-all(bf16[2,16,2048]{2,1,0:T(8,128)(2,1)S(1)} %bitcast.385), channel_id=1, replica_groups=mesh['depth_0'=8,'depth_1'=8,'depth_2'=4,'chan'=2] {'chan'}, dimensions={0} | all-to-all | bytes 262144 | tf_op jit(solution)/shard_map/all_to_all | solution.py:37
  57.3 1.1 copy.2509
  58.4 1.1 convert_reduce_fusion
  59.5 5.9 %collective-permute-start.3 = (bf16[16,1,4,64]{3,2,0,1:T(4,128)(2,1)S(1)}, bf16[16,1,4,64]{3,2,0,1:T(4,128)(2,1)S(1)}, u32[]{:S(2)}, u32[]{:S(2)}) collective-permute-start(bf16[16,1,4,64]{3,2,0,1:T(4,128)(2,1)S(1)} %bitcast.414), channel_id=1, source_target_pairs={{2,0},{4,2},{6,4},{8,6},{10,8},{12,10},{14,12},{16,14},{18,16},{20... | collective-permute-start | bytes 24584 | tf_op jit(solution)/shard_map/ppermute | solution.py:25
  65.4 1.9 collective-permute-start.2
  67.4 5.8 %collective-permute-done.2 = bf16[16,1,4,64]{3,2,0,1:T(4,128)(2,1)S(1)} collective-permute-done((bf16[16,1,4,64]{3,2,0,1:T(4,128)(2,1)S(1)}, bf16[16,1,4,64]{3,2,0,1:T(4,128)(2,1)S(1)}, u32[]{:S(2)}, u32[]{:S(2)}) %collective-permute-start.2) | collective-permute-done | bytes 8224 | tf_op jit(solution)/shard_map/ppermute | solution.py:22
  75.7 3.7 %all_to_all.21 = bf16[2,32,256]{2,1,0:T(8,128)(2,1)S(1)} all-to-all(bf16[2,32,256]{2,1,0:T(8,128)(2,1)S(1)} %bitcast.413), channel_id=1, replica_groups=mesh['depth_0'=8,'depth_1'=8,'depth_2'=4,'chan'=2] {'chan'}, dimensions={0} | all-to-all | bytes 65536 | tf_op jit(solution)/shard_map/all_to_all | solution.py:37
  79.7 1.9 collective-permute-start.5
  81.6 3.9 %collective-permute-start.4 = (bf16[32,1,4,64]{3,2,1,0:T(4,128)(2,1)S(1)}, bf16[32,1,4,64]{3,2,1,0:T(4,128)(2,1)S(1)}, u32[]{:S(2)}, u32[]{:S(2)}) collective-permute-start(bf16[32,1,4,64]{3,2,1,0:T(4,128)(2,1)S(1)} %multiply_convert_fusion.2), channel_id=1, source_target_pairs={{0,2},{2,4},{4,6},{6,8},{8,10},{10,12},{12,14},{14,16},{16,18},{18... | collective-permute-start | bytes 49160 | tf_op jit(solution)/shard_map/ppermute | solution.py:22
  85.5 0.7 copy.2590
  86.2 3.3 collective-permute-done.4
  89.9 3.8 %all_to_all.22 = bf16[2,2,12288]{2,1,0:T(2,128)(2,1)S(1)} all-to-all(bf16[2,2,12288]{2,1,0:T(2,128)(2,1)S(1)} %reshape.443), channel_id=1, replica_groups=mesh['depth_0'=8,'depth_1'=8,'depth_2'=4,'chan'=2] {'chan'}, dimensions={0} | all-to-all | bytes 196608 | tf_op jit(solution)/shard_map/all_to_all | solution.py:49
  94.3 0.9 reshape.406
  95.2 1.3 dot_general.29
  96.5 0.8 fusion.4
  97.7 1.0 fusion.78
  98.8 0.8 copy.2542
  99.6 1.0 broadcast_in_dim.101
  100.8 1.0 multiply_convert_fusion.1
  101.8 1.9 collective-permute-start.6
  103.7 6.0 %collective-permute-start.7 = (bf16[16,1,8,128]{3,2,1,0:T(8,128)(2,1)S(1)}, bf16[16,1,8,128]{3,2,1,0:T(8,128)(2,1)S(1)}, u32[]{:S(2)}, u32[]{:S(2)}) collective-permute-start(bf16[16,1,8,128]{3,2,1,0:T(8,128)(2,1)S(1)} %get-tuple-element.148), channel_id=1, source_target_pairs={{2,0},{4,2},{6,4},{8,6},{10,8},{12,10},{14,12},{16,14},{18,16},{20... | collective-permute-start | bytes 98312 | tf_op jit(solution)/shard_map/ppermute | solution.py:25
  109.8 1.1 convolution_bitcast_fusion
  111.5 3.9 %all_to_all.23 = bf16[2,16,4,8,128]{4,1,3,2,0:T(8,128)(2,1)S(1)} all-to-all(bf16[2,16,4,8,128]{4,1,3,2,0:T(8,128)(2,1)S(1)} %broadcast_in_dim.103), channel_id=1, replica_groups=mesh['depth_0'=8,'depth_1'=8,'depth_2'=4,'chan'=2] {'chan'}, dimensions={0} | all-to-all | bytes 524288 | tf_op jit(solution)/shard_map/all_to_all | solution.py:49
  115.5 0.7 copy-done.1
  116.9 1.6 reshape.408
  118.5 2.8 dot_general.32
  121.4 2.5 fusion
  124.5 79.0 %all-reduce.8.cloned.1.call-done = f32[64,16,27]{0,2,1:T(8,128)} async-done(((f32[64,16,27]{0,2,1:T(8,128)}), f32[64,16,27]{0,2,1:T(8,128)}) %all-reduce.8.cloned.1.call-update) | async-done | bytes 110608 | tf_op jit(solution)/shard_map/psum | solution.py:57
  203.6 1.7 convolution_bitcast_fusion.1
  205.3 32.0 %psum.42 = f32[32,16,27]{2,0,1:T(8,128)S(1)} all-reduce(f32[32,16,27]{2,0,1:T(8,128)S(1)} %convolution_bitcast_fusion.1), channel_id=1, replica_groups=mesh['depth_0'=8,'depth_1'=8,'depth_2'=4,'chan'=2] {'depth_0'}, use_global_device_ids=true, to_apply=%region_3.4 | all-reduce | flops 13824 | bytes 110592 | tf_op jit(solution)/shard_map/psum | solution.py:57
  237.3 44.8 %all-reduce.10.cloned.1.call-done = f32[64,16,27]{0,2,1:T(8,128)} async-done(((f32[64,16,27]{0,2,1:T(8,128)}), f32[64,16,27]{0,2,1:T(8,128)}) %all-reduce.10.cloned.1.call-update) | async-done | bytes 110608 | tf_op jit(solution)/shard_map/psum | solution.py:57
  282.1 29.2 %psum.43 = f32[32,16,27]{2,0,1:T(8,128)S(1)} all-reduce(f32[32,16,27]{2,0,1:T(8,128)S(1)} %psum.42), channel_id=1, replica_groups=mesh['depth_0'=8,'depth_1'=8,'depth_2'=4,'chan'=2] {'depth_1'}, use_global_device_ids=true, to_apply=%region_4.5 | all-reduce | flops 13824 | bytes 110592 | tf_op jit(solution)/shard_map/psum | solution.py:57
  311.2 20.1 %psum.44 = f32[32,16,27]{2,0,1:T(8,128)S(1)} all-reduce(f32[32,16,27]{2,0,1:T(8,128)S(1)} %psum.43), channel_id=1, replica_groups=mesh['depth_0'=8,'depth_1'=8,'depth_2'=4,'chan'=2] {'depth_2'}, use_global_device_ids=true, to_apply=%region_5.6 | all-reduce | flops 13824 | bytes 110592 | tf_op jit(solution)/shard_map/psum | solution.py:57
  331.3 0.9 copy.2550
  332.8 2.8 all-reduce.12.cloned.1.call-done
  335.7 1.8 copy.2551
  (96 shorter events, 9.7 us)
Async XLA Ops:
  7.2 8.9 %copy-start = (bf16[64,32,27]{0,1,2:T(8,128)(2,1)S(1)}, bf16[64,32,27]{0,1,2:T(8,128)(2,1)}, u32[]{:S(2)}) copy-start(bf16[64,32,27]{0,1,2:T(8,128)(2,1)} %param.6) | copy-start | bytes 331780
  7.2 196.3 %all-reduce.8.cloned.1.call-start = ((), (), s32[]{:S(2)}) async-start(), calls=%async_computation.4 | async-start | bytes 524288 | tf_op jit(solution)/shard_map/psum | solution.py:57
  8.1 9.9 %collective-permute-start = (bf16[16,1,8,128]{3,2,1,0:T(8,128)(2,1)S(1)}, bf16[16,1,8,128]{3,2,1,0:T(8,128)(2,1)S(1)}, u32[]{:S(2)}, u32[]{:S(2)}) collective-permute-start(bf16[16,1,8,128]{3,2,1,0:T(8,128)(2,1)S(1)} %get-tuple-element.149), channel_id=1, source_target_pairs={{0,2},{2,4},{4,6},{6,8},{8,10},{10,12},{12,14},{14,16},{16,18},{18... | collective-permute-start | bytes 98312 | tf_op jit(solution)/shard_map/ppermute | solution.py:22
  11.5 6.5 %collective-permute-start.1 = (bf16[16,1,8,128]{3,2,1,0:T(8,128)(2,1)S(1)}, bf16[16,1,8,128]{3,2,1,0:T(8,128)(2,1)S(1)}, u32[]{:S(2)}, u32[]{:S(2)}) collective-permute-start(bf16[16,1,8,128]{3,2,1,0:T(8,128)(2,1)S(1)} %get-tuple-element.150), channel_id=1, source_target_pairs={{2,0},{4,2},{6,4},{8,6},{10,8},{12,10},{14,12},{16,14},{18,16},{20... | collective-permute-start | bytes 98312 | tf_op jit(solution)/shard_map/ppermute | solution.py:25
  17.9 33.2 %copy-start.4 = (bf16[32,16,27]{0,1,2:T(8,128)(2,1)}, bf16[32,16,27]{0,1,2:T(8,128)(2,1)S(1)}, u32[]{:S(2)}) copy-start(bf16[32,16,27]{0,1,2:T(8,128)(2,1)S(1)} %copy.2558) | copy-start | bytes 82948
  57.3 22.3 %copy-start.6 = (bf16[32,1,4,64]{3,2,1,0:T(4,128)(2,1)S(1)}, bf16[32,1,4,64]{3,2,1,0:T(4,128)(2,1)}, u32[]{:S(2)}) copy-start(bf16[32,1,4,64]{3,2,1,0:T(4,128)(2,1)} %param.7) | copy-start | bytes 49156
  58.4 17.1 %copy-start.3 = (bf16[64,16,27]{0,1,2:T(8,128)(2,1)S(1)}, bf16[64,16,27]{0,1,2:T(8,128)(2,1)}, u32[]{:S(2)}) copy-start(bf16[64,16,27]{0,1,2:T(8,128)(2,1)} %constant_dynamic-slice_fusion) | copy-start | bytes 165892
  59.5 7.9 %collective-permute-start.3 = (bf16[16,1,4,64]{3,2,0,1:T(4,128)(2,1)S(1)}, bf16[16,1,4,64]{3,2,0,1:T(4,128)(2,1)S(1)}, u32[]{:S(2)}, u32[]{:S(2)}) collective-permute-start(bf16[16,1,4,64]{3,2,0,1:T(4,128)(2,1)S(1)} %bitcast.414), channel_id=1, source_target_pairs={{2,0},{4,2},{6,4},{8,6},{10,8},{12,10},{14,12},{16,14},{18,16},{20... | collective-permute-start | bytes 24584 | tf_op jit(solution)/shard_map/ppermute | solution.py:25
  65.4 7.7 %collective-permute-start.2 = (bf16[16,1,4,64]{3,2,0,1:T(4,128)(2,1)S(1)}, bf16[16,1,4,64]{3,2,0,1:T(4,128)(2,1)S(1)}, u32[]{:S(2)}, u32[]{:S(2)}) collective-permute-start(bf16[16,1,4,64]{3,2,0,1:T(4,128)(2,1)S(1)} %bitcast.415), channel_id=1, source_target_pairs={{0,2},{2,4},{4,6},{6,8},{8,10},{10,12},{12,14},{14,16},{16,18},{18... | collective-permute-start | bytes 24584 | tf_op jit(solution)/shard_map/ppermute | solution.py:22
  79.7 6.5 %collective-permute-start.5 = (bf16[32,1,4,64]{3,2,1,0:T(4,128)(2,1)S(1)}, bf16[32,1,4,64]{3,2,1,0:T(4,128)(2,1)S(1)}, u32[]{:S(2)}, u32[]{:S(2)}) collective-permute-start(bf16[32,1,4,64]{3,2,1,0:T(4,128)(2,1)S(1)} %multiply_convert_fusion.2), channel_id=1, source_target_pairs={{2,0},{4,2},{6,4},{8,6},{10,8},{12,10},{14,12},{16,14},{18,16},{20... | collective-permute-start | bytes 49160 | tf_op jit(solution)/shard_map/ppermute | solution.py:25
  81.6 7.9 %collective-permute-start.4 = (bf16[32,1,4,64]{3,2,1,0:T(4,128)(2,1)S(1)}, bf16[32,1,4,64]{3,2,1,0:T(4,128)(2,1)S(1)}, u32[]{:S(2)}, u32[]{:S(2)}) collective-permute-start(bf16[32,1,4,64]{3,2,1,0:T(4,128)(2,1)S(1)} %multiply_convert_fusion.2), channel_id=1, source_target_pairs={{0,2},{2,4},{4,6},{6,8},{8,10},{10,12},{12,14},{14,16},{16,18},{18... | collective-permute-start | bytes 49160 | tf_op jit(solution)/shard_map/ppermute | solution.py:22
  101.8 9.1 %collective-permute-start.6 = (bf16[16,1,8,128]{3,2,1,0:T(8,128)(2,1)S(1)}, bf16[16,1,8,128]{3,2,1,0:T(8,128)(2,1)S(1)}, u32[]{:S(2)}, u32[]{:S(2)}) collective-permute-start(bf16[16,1,8,128]{3,2,1,0:T(8,128)(2,1)S(1)} %get-tuple-element.147), channel_id=1, source_target_pairs={{0,2},{2,4},{4,6},{6,8},{8,10},{10,12},{12,14},{14,16},{16,18},{18... | collective-permute-start | bytes 98312 | tf_op jit(solution)/shard_map/ppermute | solution.py:22
  103.7 7.6 %collective-permute-start.7 = (bf16[16,1,8,128]{3,2,1,0:T(8,128)(2,1)S(1)}, bf16[16,1,8,128]{3,2,1,0:T(8,128)(2,1)S(1)}, u32[]{:S(2)}, u32[]{:S(2)}) collective-permute-start(bf16[16,1,8,128]{3,2,1,0:T(8,128)(2,1)S(1)} %get-tuple-element.148), channel_id=1, source_target_pairs={{2,0},{4,2},{6,4},{8,6},{10,8},{12,10},{14,12},{16,14},{18,16},{20... | collective-permute-start | bytes 98312 | tf_op jit(solution)/shard_map/ppermute | solution.py:25
  110.9 171.2 %all-reduce.10.cloned.1.call-start = ((), (), s32[]{:S(2)}) async-start(), calls=%async_computation.5 | async-start | bytes 524288 | tf_op jit(solution)/shard_map/psum | solution.py:57
  115.5 0.7 copy-start.1
  116.3 5.1 %copy-start.5 = (bf16[32,16,27]{0,1,2:T(8,128)(2,1)S(1)}, bf16[32,16,27]{0,1,2:T(8,128)(2,1)}, u32[]{:S(2)}) copy-start(bf16[32,16,27]{0,1,2:T(8,128)(2,1)} %copy-done.4) | copy-start | bytes 82948
  123.8 79.7 %copy-start.2 = (bf16[2,16,4,8,128]{4,1,0,3,2:T(8,128)(2,1)S(1)}, bf16[2,16,4,8,128]{4,1,0,3,2:T(8,128)(2,1)}, u32[]{:S(2)}) copy-start(bf16[2,16,4,8,128]{4,1,0,3,2:T(8,128)(2,1)} %copy-done.1) | copy-start | bytes 786436
  203.5 132.2 %all-reduce.12.cloned.1.call-start = ((), (), s32[]{:S(2)}) async-start(), calls=%async_computation.6 | async-start | bytes 524288 | tf_op jit(solution)/shard_map/psum | solution.py:57
Sparse Core Ops, SparseCore 0:
  111.0 92.4 all-reduce.7
  205.8 76.2 all-reduce.9
  284.4 51.2 all-reduce.11
where the time goes:
time: 346 us; the launch traced here: 344 us
  waiting for transfers between devices  136 us (39%)
  blocking collectives  96.5 us (28%)
  local copies, waits for them, and re-layouts  55 us (16%)
  starting transfers between devices  29.7 us (9%)
  between operations  14.3 us (4%)
  matrix products  8.1 us (2%)
  other arithmetic  4.18 us (1%)
    psum x3, waiting for transfers between devices, one_axis_at_a_time(): return functools.reduce(lax.psum, axes, x)  127 us
    psum x3, blocking collectives, one_axis_at_a_time(): return functools.reduce(lax.psum, axes, x)  81.2 us
    another operation x32, local copies, waits for them, and re-layouts, patch_rows(): return jnp.stack(windows, 0).reshape(27 * chans, planes * height * across)  28.4 us
    ppermute x4, starting transfers between devices, padded_2(): lax.ppermute(lax.slice_in_dim(block, 0, width, axis=dim), axis, backward)  18.4 us
    ppermute x4, starting transfers between devices, padded_2(): lax.ppermute(lax.slice_in_dim(block, block.shape[dim] - width, None, axis...  11.2 us
    ppermute x4, waiting for transfers between devices, padded_2(): lax.ppermute(lax.slice_in_dim(block, block.shape[dim] - width, None, axis...  9.1 us
    all_to_all x2, blocking collectives, from_everyone(): return lax.all_to_all(copies, axis, split_axis=0, concat_axis=0, tiled=True)  7.74 us
    all_to_all x2, blocking collectives, summed_on_arrival(): pieces = lax.all_to_all(split_up(x, dim, count), axis, 0, 0, tiled=True)  7.59 us
  transfers between devices with their start and end apart: 11, of which 6 were waited for; matrix products, arithmetic and copies ran while one was open for 4% of the time, Pallas kernels for 0%

commit v1 on v0

v1 whole, which is shorter than its diff:
```python
import functools

import jax
import jax.numpy as jnp
from jax import lax
from jax.experimental import pallas as pl
from jax.experimental.pallas import tpu as pltpu
from jax.sharding import Mesh
from jax.sharding import PartitionSpec as P

DEPTH = ("z", "y_high", "y_low", "x")
NEAR = ("y_low", "x")
FAR = ("z", "y_high")
SLABS = 256
ROW = 4
BF16 = jnp.bfloat16
F32 = jnp.float32


def depth_shift(block, steps):
    pairs = [(i, i + steps) for i in range(SLABS) if 0 <= i + steps < SLABS]
    return lax.ppermute(block, DEPTH, pairs)


def slope(pre):
    sig = jax.nn.sigmoid(pre)
    return sig * (1.0 + pre * (1.0 - sig))


def pick(rows, lanes, width, step):
    row = lax.broadcasted_iota(jnp.int32, (rows, lanes), 0)
    lane = lax.broadcasted_iota(jnp.int32, (rows, lanes), 1)
    target = step(row // width) * width + row % width
    return jnp.where(lane == target, 1.0, 0.0).astype(BF16)


def band_kernel(w1, w1t, w2, w2t, t1, t1t, t2, t2t):
    def fill(weights, out, height, rows, width, lanes, sign):
        for h in range(height):
            marks = pick(3 * width, lanes, width, lambda b: h + sign * (b - 1))
            bands = jnp.dot(weights[...], marks, preferred_element_type=F32).astype(BF16)
            for tap in range(9):
                out[h * rows : (h + 1) * rows, tap * lanes : (tap + 1) * lanes] = bands[
                    tap * rows : (tap + 1) * rows
                ]

    fill(w1, t1, 8, 32, 32, 256, 1)
    fill(w2, t2, 4, 64, 32, 128, 1)
    fill(w2t, t2t, 4, 32, 64, 256, -1)
    fill(w1t, t1t, 8, 16, 32, 256, -1)


def shifted(value, step):
    lanes = value.shape[-1]
    lane = lax.broadcasted_iota(jnp.int32, value.shape, 1)
    low = jnp.where(lane < step, 0.0, pltpu.roll(value, step, 1))
    high = jnp.where(lane >= lanes - step, 0.0, pltpu.roll(value, lanes - step, 1))
    return low.astype(BF16), value.astype(BF16), high.astype(BF16)


def main_kernel(
    scalars, own, oth, t1, t1t, t2, t2t, gf, wg, XP, PS, SL, QP, GP, HP, CT, FS, FP, G1, G2
):
    member = scalars[0]
    place = scalars[1]
    x = scalars[2]
    half = pl.multiple_of(member * 16, 16)

    def slot(delta):
        return lax.rem(x + delta + 4, 4)

    planes = [(slot(0), 0)]
    planes += [(slot(delta), 8 * p) for delta in (-3, -2, -1) for p in range(2)]
    planes += [(slot(0), 12), (slot(0), 20)]
    planes += [(slot(delta), 20 + 8 * p) for delta in (1, 2, 3) for p in range(2)]
    planes += [(slot(0), 32)]
    for j, (at, start) in enumerate(planes):
        plane = jnp.concatenate(
            [own[at, start : start + 8], oth[at, start : start + 8]], axis=1
        ).reshape(256, 128)
        for c, part in enumerate(shifted(plane.astype(F32), 1)):
            if j <= 8:
                XP[j, c, :, :128] = part
            if j >= 7:
                XP[j - 7, c, :, 128:] = part

    for k in range(7):
        pre = jnp.dot(t1[...], XP[k : k + 3].reshape(2304, 256), preferred_element_type=F32)
        act = (pre * jax.nn.sigmoid(pre)).astype(BF16).astype(F32).reshape(4, 2, 32, 256)
        rows = (act[:, 0] + act[:, 1]).reshape(128, 256)
        PS[k] = rows[:, :128]
        PS[k + 7] = rows[:, 128:]
        if k >= 5:
            SL[k - 5] = slope(pre[:, :128])
        if k <= 1:
            SL[k + 2] = slope(pre[:, 128:])

    lane = lax.broadcasted_iota(jnp.int32, (128, 128), 1)
    even = lane % 2 == 0
    for c in range(3):
        QP[4, c, :, 128:] = jnp.zeros((128, 128), BF16)
    for j in range(7):
        total = PS[2 * j] + PS[2 * j + 1]
        total = total + jnp.where(even, pltpu.roll(total, 127, 1), pltpu.roll(total, 1, 1))
        at = place + (j - 3)
        factor = jnp.where((at >= 0) & (at < SLABS), 0.125, 0.0)
        pooled = (total * factor).astype(BF16).astype(F32)
        for c, part in enumerate(shifted(pooled, 2)):
            if j <= 4:
                QP[j, c, :, :128] = part
            if j >= 3:
                QP[j - 3, c, :, 128:] = part

    cots = [(slot(-2), 16), (slot(-1), 16), (slot(0), 28), (slot(1), 36), (slot(2), 36)]
    own_o = pl.multiple_of(member * 32, 32)
    oth_o = pl.multiple_of(32 - member * 32, 32)
    for e, (at, start) in enumerate(cots):
        for high in range(2):
            here = start + 2 * high
            CT[e, high, pl.ds(own_o, 32), :] = own[at, here : here + 2].reshape(32, 128)
            CT[e, high, pl.ds(oth_o, 32), :] = oth[at, here : here + 2].reshape(32, 128)
    row = lax.broadcasted_iota(jnp.int32, (128, 256), 0)
    col = lax.broadcasted_iota(jnp.int32, (128, 256), 1)
    spread = jnp.where(row == (col // 128) * 64 + (col % 128) // 2, 1.0, 0.0).astype(BF16)
    cot = jnp.dot(CT[...].reshape(640, 128), spread, preferred_element_type=F32)

    for e in range(3):
        pre_two = jnp.dot(t2[...], QP[e : e + 3].reshape(1152, 256), preferred_element_type=F32)
        slopes = slope(pre_two)
        for plane in (e, e + 3):
            if plane > 4:
                continue
            side = slopes[:, :128] if plane == e else slopes[:, 128:]
            base = plane * 128
            cots_of = jnp.concatenate(
                [
                    cot[base : base + 64, :128],
                    cot[base : base + 64, 128:],
                    cot[base + 64 : base + 128, :128],
                    cot[base + 64 : base + 128, 128:],
                ],
                axis=0,
            )
            grad = (cots_of * side).astype(BF16).astype(F32)
            for c, part in enumerate(shifted(grad, 2)):
                for m in range(3):
                    n = plane - m
                    if 0 <= n <= 2:
                        GP[m, c, :, n * 128 : (n + 1) * 128] = part
            if plane == 2:
                lanes = lax.broadcasted_iota(jnp.int32, (256, 128), 1)
                kept = jnp.where(lanes % 2 == 0, grad, 0.0).astype(BF16)
                G2[...] = jnp.zeros(G2.shape, BF16)
                for h in range(4):
                    G2[32:96, h * 128 : (h + 1) * 128] = kept[h * 64 : (h + 1) * 64]

    back = jnp.dot(t2t[...], GP[...].reshape(2304, 384), preferred_element_type=F32)
    G1[...] = jnp.zeros(G1.shape, BF16)
    for q, f in enumerate((0, 1, 1, 2)):
        at = place + (f - 1)
        factor = jnp.where((at >= 0) & (at < SLABS), 0.125, 0.0)
        part = (back[:, f * 128 : (f + 1) * 128] * factor).reshape(4, 1, 32, 128)
        wide = jnp.concatenate([part, part], axis=1).reshape(256, 128)
        grad = (wide * SL[q]).astype(BF16).astype(F32)
        for c, piece in enumerate(shifted(grad, 1)):
            if q <= 2:
                HP[q, c, :, :128] = piece
            if q >= 1:
                HP[q - 1, c, :, 128:] = piece
            if c == 1 and q in (1, 2):
                for h in range(8):
                    to = ((q - 1) * 8 + h) * 128
                    G1[0:32, to : to + 128] = piece[h * 32 : (h + 1) * 32]

    nothing = jnp.zeros((16, 128), BF16)
    for a in range(3):
        for b in range(3):
            for c in range(3):
                tap = (a * 3 + b) * 3 + c
                to = slice(tap * 16, tap * 16 + 16)
                for q in range(2):
                    j = 6 + a + q
                    m, side = (j, 0) if j <= 8 else (j - 7, 128)
                    for h in range(8):
                        at = h + b - 1
                        lanes = slice((q * 8 + h) * 128, (q * 8 + h + 1) * 128)
                        if 0 <= at < 8:
                            FS[to, lanes] = XP[m, c, at * 32 : at * 32 + 16, side : side + 128]
                        else:
                            FS[to, lanes] = nothing
                for h in range(4):
                    at = h + b - 1
                    lanes = slice(h * 128, (h + 1) * 128)
                    if 0 <= at < 4:
                        FP[to, lanes] = QP[2 + a, c, pl.ds(at * 32 + half, 16), :128]
                    else:
                        FP[to, lanes] = nothing
    along = (((1,), (1,)), ((), ()))
    wg[0:432] = lax.dot_general(
        FS[...], G1[...], along, preferred_element_type=F32
    ) + lax.dot_general(FP[...], G2[...], along, preferred_element_type=F32)
    wg[432:] = jnp.zeros((80, 128), F32)

    out = jnp.dot(t1t[...], HP[...].reshape(2304, 256), preferred_element_type=F32)
    gf[0] = out[:, :128].astype(BF16)
    gf[1] = out[:, 128:].astype(BF16)


def band_weights(w1, w1t, w2, w2t):
    shapes = [(256, 2304), (128, 2304), (256, 1152), (128, 2304)]
    return pl.pallas_call(
        band_kernel,
        out_shape=[jax.ShapeDtypeStruct(shape, BF16) for shape in shapes],
        cost_estimate=pl.CostEstimate(flops=10**9, bytes_accessed=4 * 10**6, transcendentals=0),
        name="bands",
    )(w1, w1t, w2, w2t)


def levels(scalars, own, oth, bands):
    vmem = pl.BlockSpec(memory_space=pltpu.VMEM)
    scratch = [
        ((9, 3, 256, 256), BF16),
        ((14, 128, 128), F32),
        ((4, 256, 128), F32),
        ((5, 3, 128, 256), BF16),
        ((3, 3, 256, 384), BF16),
        ((3, 3, 256, 256), BF16),
        ((5, 2, 64, 128), BF16),
        ((432, 2048), BF16),
        ((432, 512), BF16),
        ((128, 2048), BF16),
        ((128, 512), BF16),
    ]
    return pl.pallas_call(
        main_kernel,
        in_specs=[pl.BlockSpec(memory_space=pltpu.SMEM)] + [vmem] * 6,
        out_specs=[vmem, vmem],
        out_shape=[
            jax.ShapeDtypeStruct((2, 128, 128), BF16),
            jax.ShapeDtypeStruct((512, 128), F32),
        ],
        scratch_shapes=[pltpu.VMEM(shape, dtype) for shape, dtype in scratch],
        cost_estimate=pl.CostEstimate(
            flops=10**10, bytes_accessed=8 * 10**6, transcendentals=10**6
        ),
        name="levels",
    )(scalars, own, oth, *bands)


def total_over_depth(part):
    pieces = lax.all_to_all(part.reshape(16, 32, 128), NEAR, 0, 0, tiled=True)
    near = jnp.sum(pieces, axis=0)
    copies = jnp.broadcast_to(near, (16, 32, 128))
    pieces = lax.all_to_all(copies, FAR, 0, 0, tiled=True)
    whole = jnp.sum(pieces, axis=0)
    copies = jnp.broadcast_to(whole, (16, 32, 128))
    return lax.all_to_all(copies, NEAR, 0, 0, tiled=True).reshape(512, 128)


def shards(feats, weight_one, weight_two, cotangent):
    member = lax.axis_index("chan")
    place = lax.axis_index(DEPTH)
    x = lax.axis_index("x")
    fields = jnp.transpose(feats, (1, 2, 0, 3)).reshape(16, 16, 128)
    cot = jnp.transpose(cotangent.reshape(32, 2, 2, 64), (1, 0, 2, 3)).reshape(4, 16, 128)
    block = jnp.concatenate([fields, cot], axis=0)
    up = depth_shift(block, ROW)
    down = depth_shift(block, -ROW)

    w1 = weight_one.reshape(32, 32, 3, 3, 3)
    w2 = weight_two.reshape(64, 32, 3, 3, 3)
    own_one = lax.dynamic_slice_in_dim(w1, member * 16, 16, 1)
    other_one = lax.dynamic_slice_in_dim(w1, 16 - member * 16, 16, 1)
    ordered = jnp.concatenate([own_one, other_one], axis=1)
    bands = band_weights(
        jnp.transpose(ordered, (2, 4, 0, 3, 1)).reshape(288, 96),
        jnp.transpose(own_one[:, :, ::-1, :, ::-1], (2, 4, 1, 3, 0)).reshape(144, 96),
        jnp.transpose(w2, (2, 4, 0, 3, 1)).reshape(576, 96),
        jnp.transpose(w2[:, :, ::-1, :, ::-1], (2, 4, 1, 3, 0)).reshape(288, 192),
    )

    three = jnp.concatenate([up, block, down], axis=0)
    slots = [
        lax.dynamic_slice_in_dim(
            three, jnp.where(x > t, 0, jnp.where(x == t, 8, 20)).astype(jnp.int32), 40, 0
        )
        for t in range(4)
    ]
    own = lax.all_to_all(jnp.stack(slots, 0), "x", 0, 0, tiled=True)
    oth = lax.ppermute(own, "chan", [(0, 1), (1, 0)])
    scalars = jnp.stack([member, place, x]).astype(jnp.int32)
    grad_feats, part = levels(scalars, own, oth, bands)
    total = total_over_depth(part)[:432]
    grad_weight_one = jnp.transpose(total[:, :32].reshape(27, 16, 32), (2, 1, 0))
    grad_weight_two = jnp.transpose(total[:, 32:96].reshape(27, 16, 64), (2, 1, 0))
    grad_feats = jnp.transpose(grad_feats.reshape(2, 8, 16, 128), (2, 0, 1, 3))
    return (grad_feats, grad_weight_one, grad_weight_two)


def solution(mesh):
    finer = Mesh(
        mesh.devices.reshape(8, 2, 4, 4, mesh.shape["chan"]), DEPTH + ("chan",)
    )
    in_specs = (P("chan", DEPTH, None, None), P(), P(), P("chan", DEPTH, None, None))
    out_specs = (P("chan", DEPTH, None, None), P(None, "chan", None), P(None, "chan", None))
    return jax.shard_map(
        shards, mesh=finer, in_specs=in_specs, out_specs=out_specs, check_vma=False
    )
```

time: 346 us -> 109 us (0.32)
  the two profiles are of different devices: /device:TPU:8 before, /device:TPU:2 now
where the time goes in v1:
time: 109 us; the launch traced here: 108 us
  blocking collectives  43.3 us (40%)
  starting transfers between devices  20.3 us (19%)
  waiting for transfers between devices  19.1 us (18%)
  Pallas kernels  11.7 us (11%)
  local copies, waits for them, and re-layouts  11.2 us (10%)
  other arithmetic  1.8 us (2%)
    all_to_all x1, blocking collectives, total_over_depth(): pieces = lax.all_to_all(copies, FAR, 0, 0, tiled=True)  25.5 us
    all_to_all x1, blocking collectives, total_over_depth(): pieces = lax.all_to_all(part.reshape(16, 32, 128), NEAR, 0, 0, tiled=True)  17.7 us
    pallas_call x1, Pallas kernels, levels(): pl.pallas_call(main_kernel, in_specs=[pl.BlockSpec(memory_space=pltpu.SME...  8.54 us
    all_to_all x1, waiting for transfers between devices, total_over_depth(): return lax.all_to_all(copies, NEAR, 0, 0, tiled=True).reshape(512, 128)  7.97 us
    all_to_all x1, starting transfers between devices, shards(): own = lax.all_to_all(jnp.stack(slots, 0), 'x', 0, 0, tiled=True)  7.27 us
    all_to_all x1, waiting for transfers between devices, shards(): own = lax.all_to_all(jnp.stack(slots, 0), 'x', 0, 0, tiled=True)  7.01 us
    all_to_all x1, starting transfers between devices, total_over_depth(): return lax.all_to_all(copies, NEAR, 0, 0, tiled=True).reshape(512, 128)  6.36 us
    ppermute x2, starting transfers between devices, depth_shift(): return lax.ppermute(block, DEPTH, pairs)  4.78 us
  transfers between devices with their start and end apart: 5, of which 4 were waited for; matrix products, arithmetic and copies ran while one was open for 6% of the time, Pallas kernels for 3%

profile of v1, /device:TPU:2, one launch (start us, length us, event | category | flops | bytes accessed | tf_op | source)
XLA Modules:
  0.0 108.2 jit_solution(17803008681596030931)
XLA Ops:
  0.6 0.9 copy_dynamic-update-slice_fusion.1
  1.5 0.8 copy.26
  2.3 0.1 reshape.50
  2.4 3.5 %collective-permute-start = (bf16[20,16,128]{2,1,0:T(8,128)(2,1)S(1)}, bf16[20,16,128]{2,1,0:T(8,128)(2,1)S(1)}, u32[]{:S(2)}, u32[]{:S(2)}) collective-permute-start(bf16[20,16,128]{2,1,0:T(8,128)(2,1)S(1)} %constant_dynamic-update-slice_fusion), channel_id=1, source_target_pairs={{0,8},{2,10},{4,12},{6,14},{8,16},{10,18},{12,20},{14,22},{16,24},... | collective-permute-start | bytes 245768 | tf_op jit(solution)/shard_map/ppermute | solution.py:22
  5.9 1.3 %collective-permute-start.1 = (bf16[20,16,128]{2,1,0:T(8,128)(2,1)S(1)}, bf16[20,16,128]{2,1,0:T(8,128)(2,1)S(1)}, u32[]{:S(2)}, u32[]{:S(2)}) collective-permute-start(bf16[20,16,128]{2,1,0:T(8,128)(2,1)S(1)} %constant_dynamic-update-slice_fusion), channel_id=1, source_target_pairs={{8,0},{10,2},{12,4},{14,6},{16,8},{18,10},{20,12},{22,14},{24,16},... | collective-permute-start | bytes 245768 | tf_op jit(solution)/shard_map/ppermute | solution.py:22
  7.2 0.7 collective-permute-done
  7.9 0.9 copy_dynamic-update-slice_fusion
  8.8 3.4 %collective-permute-done.1 = bf16[20,16,128]{2,1,0:T(8,128)(2,1)S(1)} collective-permute-done((bf16[20,16,128]{2,1,0:T(8,128)(2,1)S(1)}, bf16[20,16,128]{2,1,0:T(8,128)(2,1)S(1)}, u32[]{:S(2)}, u32[]{:S(2)}) %collective-permute-start.1) | collective-permute-done | bytes 81952 | tf_op jit(solution)/shard_map/ppermute | solution.py:22
  12.2 0.1 dynamic-slice_bitcast_fusion.3
  12.4 0.0 copy-start
  12.4 0.9 pad_maximum_fusion
  13.3 0.0 copy-start.1
  13.3 7.3 %all-to-all-start = ((bf16[4,40,16,128]{3,2,1,0:T(8,128)(2,1)}), bf16[4,40,16,128]{3,2,1,0:T(8,128)(2,1)S(1)}, u32[]{:S(2)}, u32[]{:S(2)}) async-start(bf16[4,40,16,128]{3,2,1,0:T(8,128)(2,1)} %pad_maximum_fusion), calls=%async_computation | async-start | bytes 1310720 | tf_op jit(solution)/shard_map/all_to_all | solution.py:289
  20.6 0.0 copy-done
  20.6 0.2 copy.33
  20.7 0.2 copy.42
  20.9 7.0 %all-to-all-done.own = bf16[4,40,16,128]{3,2,1,0:T(8,128)(2,1)S(1)} async-done(((bf16[4,40,16,128]{3,2,1,0:T(8,128)(2,1)}), bf16[4,40,16,128]{3,2,1,0:T(8,128)(2,1)S(1)}, u32[]{:S(2)}, u32[]{:S(2)}) %all-to-all-start) | async-done | bytes 655392 | tf_op jit(solution)/shard_map/all_to_all | solution.py:289
  27.9 0.0 copy-start.2
  27.9 1.9 %collective-permute-start.2 = (bf16[4,40,16,128]{3,2,1,0:T(8,128)(2,1)S(1)}, bf16[4,40,16,128]{3,2,1,0:T(8,128)(2,1)S(1)}, u32[]{:S(2)}, u32[]{:S(2)}) collective-permute-start(bf16[4,40,16,128]{3,2,1,0:T(8,128)(2,1)S(1)} %all-to-all-done.own), channel_id=1, source_target_pairs={{0,1},{1,0},{2,3},{3,2},{4,5},{5,4},{6,7},{7,6},{8,9},{9,8},{10,11... | collective-permute-start | bytes 1966088 | tf_op jit(solution)/shard_map/ppermute | solution.py:290
  29.8 0.0 copy-done.1
  29.8 0.2 constant_dynamic-slice_fusion.1
  30.0 0.2 copy.36
  30.2 0.2 copy.37
  30.4 0.2 maximum_bitcast_fusion
  30.7 0.2 copy.31
  30.9 0.0 copy-done.2
  30.9 0.8 reshape.52.w1
  31.7 0.1 reverse_bitcast_fusion.1
  31.8 0.7 reshape.53.w1t
  32.5 0.1 reverse_bitcast_fusion
  32.6 0.9 reshape.56.w2t
  33.5 0.2 reshape.55
  33.7 0.8 copy.34.w2
  34.5 3.1 %bands.1 = (bf16[256,2304]{1,0:T(8,128)(2,1)}, bf16[128,2304]{1,0:T(8,128)(2,1)}, bf16[256,1152]{1,0:T(8,128)(2,1)}, bf16[128,2304]{1,0:T(8,128)(2,1)}) custom-call(bf16[288,96]{1,0:T(8,128)(2,1)} %reshape.52.w1, bf16[144,96]{1,0:T(8,128)(2,1)} %reshape.53.w1t, bf16[576,96]{1,0:T(8,128)(2,1)} %copy.34.w2, bf16[288,192]{1,0:T(8,128)(2,1)} %reshape.56.w2t), custom_call_target="tpu_custom_call" | custom-call | flops 1000000000 | bytes 4000000 | tf_op jit(solution)/shard_map/bands/pallas_call | solution.py:211
  37.6 0.6 pad_add_fusion.scalars
  38.2 0.0 collective-permute-done.2.oth
  38.2 0.0 copy-start.4
  38.2 0.8 copy-done.4
  39.1 8.5 %levels.1 = (bf16[2,128,128]{2,1,0:T(8,128)(2,1)}, f32[512,128]{1,0:T(8,128)}) custom-call(s32[3]{0:T(128)} %pad_add_fusion.scalars, bf16[4,40,16,128]{3,2,1,0:T(8,128)(2,1)} %copy-done.2, bf16[4,40,16,128]{3,2,1,0:T(8,128)(2,1)} %copy-done.4, bf16[256,2304]{1,0:T(8,128)(2,1)} %get-tuple-element.9.t1, bf16[128,2304]{1,0:T(8,128)(2,1)} %get-tuple-element.10.t1t, ...), custom_call_target="tpu_custom_call" | custom-call | flops 10000000000 | bytes 8000000 | tf_op jit(solution)/shard_map/levels/pallas_call | solution.py:234
  47.6 17.7 %all_to_all.20 = f32[16,32,128]{2,1,0:T(8,128)S(1)} all-to-all(f32[16,32,128]{2,1,0:T(8,128)} %bitcast.48), channel_id=1, replica_groups=mesh['z'=8,'y_high'=2,'y_low'=4,'x'=4,'chan'=2] {'y_low','x'}, dimensions={0} | all-to-all | bytes 524288 | tf_op jit(solution)/shard_map/all_to_all | solution.py:251
  65.3 0.0 copy-start.3
  65.4 25.5 %all_to_all.21 = f32[16,32,128]{2,1,0:T(8,128)S(1)} all-to-all(f32[16,32,128]{2,1,0:T(8,128)S(1)} %broadcast_in_dim.6), channel_id=1, replica_groups=mesh['z'=8,'y_high'=2,'y_low'=4,'x'=4,'chan'=2] {'z','y_high'}, dimensions={0} | all-to-all | bytes 524288 | tf_op jit(solution)/shard_map/all_to_all | solution.py:254
  90.9 0.7 broadcast_in_dim.7
  91.7 6.4 %all-to-all-start.3 = ((f32[16,32,128]{2,1,0:T(8,128)}), f32[16,32,128]{2,1,0:T(8,128)S(1)}, u32[]{:S(2)}, u32[]{:S(2)}) async-start(f32[16,32,128]{2,1,0:T(8,128)} %broadcast_in_dim.7), calls=%async_computation.3 | async-start | bytes 524288 | tf_op jit(solution)/shard_map/all_to_all | solution.py:257
  98.0 0.0 copy-done.3
  98.1 0.6 copy.43
  98.7 8.0 %all-to-all-done.3 = f32[16,32,128]{2,1,0:T(8,128)S(1)} async-done(((f32[16,32,128]{2,1,0:T(8,128)}), f32[16,32,128]{2,1,0:T(8,128)S(1)}, u32[]{:S(2)}, u32[]{:S(2)}) %all-to-all-start.3) | async-done | bytes 262176 | tf_op jit(solution)/shard_map/all_to_all | solution.py:257
  106.7 0.7 slice.11
  107.4 0.8 slice.12
  (7 shorter events, 0.1 us)
Async XLA Ops:
  2.4 5.5 %collective-permute-start = (bf16[20,16,128]{2,1,0:T(8,128)(2,1)S(1)}, bf16[20,16,128]{2,1,0:T(8,128)(2,1)S(1)}, u32[]{:S(2)}, u32[]{:S(2)}) collective-permute-start(bf16[20,16,128]{2,1,0:T(8,128)(2,1)S(1)} %constant_dynamic-update-slice_fusion), channel_id=1, source_target_pairs={{0,8},{2,10},{4,12},{6,14},{8,16},{10,18},{12,20},{14,22},{16,24},... | collective-permute-start | bytes 245768 | tf_op jit(solution)/shard_map/ppermute | solution.py:22
  5.9 6.3 %collective-permute-start.1 = (bf16[20,16,128]{2,1,0:T(8,128)(2,1)S(1)}, bf16[20,16,128]{2,1,0:T(8,128)(2,1)S(1)}, u32[]{:S(2)}, u32[]{:S(2)}) collective-permute-start(bf16[20,16,128]{2,1,0:T(8,128)(2,1)S(1)} %constant_dynamic-update-slice_fusion), channel_id=1, source_target_pairs={{8,0},{10,2},{12,4},{14,6},{16,8},{18,10},{20,12},{22,14},{24,16},... | collective-permute-start | bytes 245768 | tf_op jit(solution)/shard_map/ppermute | solution.py:22
  12.4 8.2 %copy-start = (bf16[64,32,27]{0,1,2:T(8,128)(2,1)S(1)}, bf16[64,32,27]{0,1,2:T(8,128)(2,1)}, u32[]{:S(2)}) copy-start(bf16[64,32,27]{0,1,2:T(8,128)(2,1)} %param.6) | copy-start | bytes 331780
  13.3 16.5 %copy-start.1 = (bf16[32,32,27]{1,0,2:T(8,128)(2,1)S(1)}, bf16[32,32,27]{1,0,2:T(8,128)(2,1)}, u32[]{:S(2)}) copy-start(bf16[32,32,27]{1,0,2:T(8,128)(2,1)} %param.5) | copy-start | bytes 165892
  13.3 14.6 %all-to-all-start = ((bf16[4,40,16,128]{3,2,1,0:T(8,128)(2,1)}), bf16[4,40,16,128]{3,2,1,0:T(8,128)(2,1)S(1)}, u32[]{:S(2)}, u32[]{:S(2)}) async-start(bf16[4,40,16,128]{3,2,1,0:T(8,128)(2,1)} %pad_maximum_fusion), calls=%async_computation | async-start | bytes 1310720 | tf_op jit(solution)/shard_map/all_to_all | solution.py:289
  27.9 3.0 %copy-start.2 = (bf16[4,40,16,128]{3,2,1,0:T(8,128)(2,1)}, bf16[4,40,16,128]{3,2,1,0:T(8,128)(2,1)S(1)}, u32[]{:S(2)}) copy-start(bf16[4,40,16,128]{3,2,1,0:T(8,128)(2,1)S(1)} %all-to-all-done.own) | copy-start | bytes 1966084
  27.9 10.3 %collective-permute-start.2 = (bf16[4,40,16,128]{3,2,1,0:T(8,128)(2,1)S(1)}, bf16[4,40,16,128]{3,2,1,0:T(8,128)(2,1)S(1)}, u32[]{:S(2)}, u32[]{:S(2)}) collective-permute-start(bf16[4,40,16,128]{3,2,1,0:T(8,128)(2,1)S(1)} %all-to-all-done.own), channel_id=1, source_target_pairs={{0,1},{1,0},{2,3},{3,2},{4,5},{5,4},{6,7},{7,6},{8,9},{9,8},{10,11... | collective-permute-start | bytes 1966088 | tf_op jit(solution)/shard_map/ppermute | solution.py:290
  38.2 0.8 copy-start.4
  65.3 32.7 %copy-start.3 = (bf16[2,128,128]{2,1,0:T(8,128)(2,1)S(1)}, bf16[2,128,128]{2,1,0:T(8,128)(2,1)}, u32[]{:S(2)}) copy-start(bf16[2,128,128]{2,1,0:T(8,128)(2,1)} %get-tuple-element.13) | copy-start | bytes 196612
  91.7 15.0 %all-to-all-start.3 = ((f32[16,32,128]{2,1,0:T(8,128)}), f32[16,32,128]{2,1,0:T(8,128)S(1)}, u32[]{:S(2)}, u32[]{:S(2)}) async-start(f32[16,32,128]{2,1,0:T(8,128)} %broadcast_in_dim.7), calls=%async_computation.3 | async-start | bytes 524288 | tf_op jit(solution)/shard_map/all_to_all | solution.py:257

commit v2 on v1

--- a/solution.py
+++ b/solution.py
@@ -1,5 +1,3 @@
-import functools
-
 import jax
 import jax.numpy as jnp
 from jax import lax
@@ -8,9 +6,8 @@
 from jax.sharding import Mesh
 from jax.sharding import PartitionSpec as P
 
-DEPTH = ("z", "y_high", "y_low", "x")
-NEAR = ("y_low", "x")
-FAR = ("z", "y_high")
+
+DEPTH = ("z", "y", "x")
 SLABS = 256
 ROW = 4
 BF16 = jnp.bfloat16
@@ -27,27 +24,55 @@
     return sig * (1.0 + pre * (1.0 - sig))
 
 
-def pick(rows, lanes, width, step):
-    row = lax.broadcasted_iota(jnp.int32, (rows, lanes), 0)
-    lane = lax.broadcasted_iota(jnp.int32, (rows, lanes), 1)
-    target = step(row // width) * width + row % width
-    return jnp.where(lane == target, 1.0, 0.0).astype(BF16)
-
-
-def band_kernel(w1, w1t, w2, w2t, t1, t1t, t2, t2t):
-    def fill(weights, out, height, rows, width, lanes, sign):
+def near_groups():
+    far_class = [0, 1, 0, 1, 1, 0, 1, 0]
+    groups = {}
+    for place in range(SLABS):
+        z, y, x = place // 32, place // 4 % 8, place % 4
+        rank = (x * 2 + far_class[y]) * 2 + far_class[z]
+        groups.setdefault((z // 2, y // 2), {})[rank] = place
+    near = [[block[rank] for rank in range(16)] for block in groups.values()]
+    far = [[block[rank] for block in groups.values()] for rank in range(16)]
+    return near, far
+
+
+NEAR, FAR = near_groups()
+
+
+def band_kernel(scalars, w1, w1t, w2, w2t, t1, t1t, t2, t2t):
+    turn = scalars[0] * 16
+    half = pl.multiple_of(turn, 16)
+
+    def fill(weights, out, height, rows, width, lanes, sign, turn):
+        row = lax.broadcasted_iota(jnp.int32, (3 * width, lanes), 0)
+        lane = lax.broadcasted_iota(jnp.int32, (3 * width, lanes), 1)
+        base = lane - (sign * (row // width - 1) * width + (row + turn) % width)
         for h in range(height):
-            marks = pick(3 * width, lanes, width, lambda b: h + sign * (b - 1))
-            bands = jnp.dot(weights[...], marks, preferred_element_type=F32).astype(BF16)
+            marks = jnp.where(base == h * width, 1.0, 0.0).astype(BF16)
+            bands = jnp.dot(weights, marks, preferred_element_type=F32).astype(BF16)
             for tap in range(9):
                 out[h * rows : (h + 1) * rows, tap * lanes : (tap + 1) * lanes] = bands[
                     tap * rows : (tap + 1) * rows
                 ]
 
-    fill(w1, t1, 8, 32, 32, 256, 1)
-    fill(w2, t2, 4, 64, 32, 128, 1)
-    fill(w2t, t2t, 4, 32, 64, 256, -1)
-    fill(w1t, t1t, 8, 16, 32, 256, -1)
+    def forward(ref):
+        parts = [
+            jnp.concatenate([ref[9 * a + 3 * b + c] for a in range(3) for c in range(3)], axis=0)
+            for b in range(3)
+        ]
+        return jnp.concatenate(parts, axis=1)
+
+    def backward(load):
+        taps = [(2 - a, 2 - c) for a in range(3) for c in range(3)]
+        parts = [
+            jnp.concatenate([load(9 * a + 3 * b + c) for a, c in taps], axis=0) for b in range(3)
+        ]
+        return jnp.concatenate(parts, axis=1)
+
+    fill(forward(w1), t1, 8, 32, 32, 256, 1, turn)
+    fill(forward(w2), t2, 4, 64, 32, 128, 1, 0)
+    fill(backward(lambda t: w2t[t]), t2t, 4, 32, 64, 256, -1, 0)
+    fill(backward(lambda t: w1t[t, pl.ds(half, 16), :]), t1t, 8, 16, 32, 256, -1, 0)
 
 
 def shifted(value, step):
@@ -206,14 +231,18 @@
     gf[1] = out[:, 128:].astype(BF16)
 
 
-def band_weights(w1, w1t, w2, w2t):
+def band_weights(scalars, w1, w1t, w2, w2t):
+    vmem = pl.BlockSpec(memory_space=pltpu.VMEM)
     shapes = [(256, 2304), (128, 2304), (256, 1152), (128, 2304)]
     return pl.pallas_call(
         band_kernel,
+        in_specs=[pl.BlockSpec(memory_space=pltpu.SMEM)] + [vmem] * 4,
+        out_specs=[vmem] * 4,
         out_shape=[jax.ShapeDtypeStruct(shape, BF16) for shape in shapes],
         cost_estimate=pl.CostEstimate(flops=10**9, bytes_accessed=4 * 10**6, transcendentals=0),
+        compiler_params=pltpu.CompilerParams(vmem_limit_bytes=16 * 2**20),
         name="bands",
-    )(w1, w1t, w2, w2t)
+    )(scalars, w1, w1t, w2, w2t)
 
 
 def levels(scalars, own, oth, bands):
@@ -243,18 +272,20 @@
         cost_estimate=pl.CostEstimate(
             flops=10**10, bytes_accessed=8 * 10**6, transcendentals=10**6
         ),
+        compiler_params=pltpu.CompilerParams(vmem_limit_bytes=28 * 2**20),
         name="levels",
     )(scalars, own, oth, *bands)
 
 
+def exchange(pieces, groups):
+    return lax.all_to_all(pieces, DEPTH, 0, 0, axis_index_groups=groups, tiled=True)
+
+
 def total_over_depth(part):
-    pieces = lax.all_to_all(part.reshape(16, 32, 128), NEAR, 0, 0, tiled=True)
-    near = jnp.sum(pieces, axis=0)
-    copies = jnp.broadcast_to(near, (16, 32, 128))
-    pieces = lax.all_to_all(copies, FAR, 0, 0, tiled=True)
-    whole = jnp.sum(pieces, axis=0)
-    copies = jnp.broadcast_to(whole, (16, 32, 128))
-    return lax.all_to_all(copies, NEAR, 0, 0, tiled=True).reshape(512, 128)
+    near = jnp.sum(exchange(part.reshape(16, 32, 128), NEAR), axis=0)
+    whole = jnp.sum(exchange(jnp.broadcast_to(near, (16, 32, 128)), FAR), axis=0)
+    copies = jnp.broadcast_to(whole.astype(BF16), (16, 32, 128))
+    return exchange(copies, NEAR).reshape(512, 128).astype(F32)
 
 
 def shards(feats, weight_one, weight_two, cotangent):
@@ -267,16 +298,13 @@
     up = depth_shift(block, ROW)
     down = depth_shift(block, -ROW)
 
-    w1 = weight_one.reshape(32, 32, 3, 3, 3)
-    w2 = weight_two.reshape(64, 32, 3, 3, 3)
-    own_one = lax.dynamic_slice_in_dim(w1, member * 16, 16, 1)
-    other_one = lax.dynamic_slice_in_dim(w1, 16 - member * 16, 16, 1)
-    ordered = jnp.concatenate([own_one, other_one], axis=1)
+    scalars = jnp.stack([member, place, x]).astype(jnp.int32)
     bands = band_weights(
-        jnp.transpose(ordered, (2, 4, 0, 3, 1)).reshape(288, 96),
-        jnp.transpose(own_one[:, :, ::-1, :, ::-1], (2, 4, 1, 3, 0)).reshape(144, 96),
-        jnp.transpose(w2, (2, 4, 0, 3, 1)).reshape(576, 96),
-        jnp.transpose(w2[:, :, ::-1, :, ::-1], (2, 4, 1, 3, 0)).reshape(288, 192),
+        scalars,
+        jnp.transpose(weight_one, (2, 0, 1)),
+        jnp.transpose(weight_one, (2, 1, 0)),
+        jnp.transpose(weight_two, (2, 0, 1)),
+        jnp.transpose(weight_two, (2, 1, 0)),
     )
 
     three = jnp.concatenate([up, block, down], axis=0)
@@ -288,7 +316,6 @@
     ]
     own = lax.all_to_all(jnp.stack(slots, 0), "x", 0, 0, tiled=True)
     oth = lax.ppermute(own, "chan", [(0, 1), (1, 0)])
-    scalars = jnp.stack([member, place, x]).astype(jnp.int32)
     grad_feats, part = levels(scalars, own, oth, bands)
     total = total_over_depth(part)[:432]
     grad_weight_one = jnp.transpose(total[:, :32].reshape(27, 16, 32), (2, 1, 0))
@@ -299,10 +326,11 @@
 
 def solution(mesh):
     finer = Mesh(
-        mesh.devices.reshape(8, 2, 4, 4, mesh.shape["chan"]), DEPTH + ("chan",)
+        mesh.devices.reshape(8, 8, 4, mesh.shape["chan"]), DEPTH + ("chan",)
     )
     in_specs = (P("chan", DEPTH, None, None), P(), P(), P("chan", DEPTH, None, None))
     out_specs = (P("chan", DEPTH, None, None), P(None, "chan", None), P(None, "chan", None))
+
     return jax.shard_map(
         shards, mesh=finer, in_specs=in_specs, out_specs=out_specs, check_vma=False
     )

time: 109 us -> 90.5 us (0.83)
  the two profiles are of different devices: /device:TPU:2 before, /device:TPU:8 now
where the time goes in v2:
time: 90.5 us; the launch traced here: 90 us
  blocking collectives  50.3 us (56%)
  starting transfers between devices  18.2 us (20%)
  Pallas kernels  7.73 us (9%)
  waiting for transfers between devices  6.7 us (7%)
  local copies, waits for them, and re-layouts  6.04 us (7%)
    all_to_all x2, blocking collectives, exchange(): lax.all_to_all(pieces, DEPTH, 0, 0, axis_index_groups=groups, tiled=True)  37.8 us
    all_to_all x1, blocking collectives, shards(): own = lax.all_to_all(jnp.stack(slots, 0), 'x', 0, 0, tiled=True)  12.5 us
    ppermute x2, starting transfers between devices, depth_shift(): return lax.ppermute(block, DEPTH, pairs)  9 us
    all_to_all x1, starting transfers between devices, exchange(): lax.all_to_all(pieces, DEPTH, 0, 0, axis_index_groups=groups, tiled=True)  7.3 us
    pallas_call x1, Pallas kernels, levels(): pl.pallas_call(main_kernel, in_specs=[pl.BlockSpec(memory_space=pltpu.SME...  6.2 us
    all_to_all x1, waiting for transfers between devices, exchange(): lax.all_to_all(pieces, DEPTH, 0, 0, axis_index_groups=groups, tiled=True)  5.58 us
    unnamed x10, local copies, waits for them, and re-layouts  2.17 us
    ppermute x1, starting transfers between devices, shards(): oth = lax.ppermute(own, 'chan', [(0, 1), (1, 0)])  1.91 us
  transfers between devices with their start and end apart: 4, of which 3 were waited for; matrix products, arithmetic and copies ran while one was open for 2% of the time, Pallas kernels for 2%

profile of v2, /device:TPU:8, one launch (start us, length us, event | category | flops | bytes accessed | tf_op | source)
XLA Modules:
  0.0 90.0 jit_solution(15451954486189015499)
XLA Ops:
  0.6 0.8 copy.13
  1.4 0.1 reshape.32
  1.5 0.9 copy_dynamic-update-slice_fusion.1
  2.4 3.5 %collective-permute-start = (bf16[20,16,128]{2,1,0:T(8,128)(2,1)S(1)}, bf16[20,16,128]{2,1,0:T(8,128)(2,1)S(1)}, u32[]{:S(2)}, u32[]{:S(2)}) collective-permute-start(bf16[20,16,128]{2,1,0:T(8,128)(2,1)S(1)} %constant_dynamic-update-slice_fusion), channel_id=1, source_target_pairs={{0,8},{2,10},{4,12},{6,14},{8,16},{10,18},{12,20},{14,22},{16,24},... | collective-permute-start | bytes 245768 | tf_op jit(solution)/shard_map/ppermute | solution.py:19
  5.9 5.5 %collective-permute-start.1 = (bf16[20,16,128]{2,1,0:T(8,128)(2,1)S(1)}, bf16[20,16,128]{2,1,0:T(8,128)(2,1)S(1)}, u32[]{:S(2)}, u32[]{:S(2)}) collective-permute-start(bf16[20,16,128]{2,1,0:T(8,128)(2,1)S(1)} %constant_dynamic-update-slice_fusion), channel_id=1, source_target_pairs={{8,0},{10,2},{12,4},{14,6},{16,8},{18,10},{20,12},{22,14},{24,16},... | collective-permute-start | bytes 245768 | tf_op jit(solution)/shard_map/ppermute | solution.py:19
  11.4 0.4 collective-permute-done
  11.9 0.9 copy_dynamic-update-slice_fusion
  12.8 0.7 collective-permute-done.1
  13.4 0.1 dynamic-slice_bitcast_fusion.3
  13.6 0.0 copy-start
  13.6 0.1 pad_maximum_fusion
  13.7 0.0 copy-start.1
  13.7 12.5 %all_to_all.20.own = bf16[4,40,16,128]{3,2,1,0:T(8,128)(2,1)S(1)} all-to-all(bf16[4,40,16,128]{3,2,1,0:T(8,128)(2,1)S(1)} %pad_maximum_fusion), channel_id=1, replica_groups=mesh['z'=8,'y'=8,'x'=4,'chan'=2] {'x'}, dimensions={0} | all-to-all | bytes 1310720 | tf_op jit(solution)/shard_map/all_to_all | solution.py:317
  26.2 1.9 %collective-permute-start.2 = (bf16[4,40,16,128]{3,2,1,0:T(8,128)(2,1)S(1)}, bf16[4,40,16,128]{3,2,1,0:T(8,128)(2,1)S(1)}, u32[]{:S(2)}, u32[]{:S(2)}) collective-permute-start(bf16[4,40,16,128]{3,2,1,0:T(8,128)(2,1)S(1)} %all_to_all.20.own), channel_id=1, source_target_pairs={{0,1},{1,0},{2,3},{3,2},{4,5},{5,4},{6,7},{7,6},{8,9},{9,8},{10,11... | collective-permute-start | bytes 1966088 | tf_op jit(solution)/shard_map/ppermute | solution.py:318
  28.1 0.0 copy-done
  28.1 0.2 copy.16
  28.3 0.0 copy-done.1
  28.3 0.3 copy.17
  28.5 0.1 pad_add_fusion.scalars
  28.6 1.5 %bands.1 = (bf16[256,2304]{1,0:T(8,128)(2,1)S(1)}, bf16[128,2304]{1,0:T(8,128)(2,1)S(1)}, bf16[256,1152]{1,0:T(8,128)(2,1)S(1)}, bf16[128,2304]{1,0:T(8,128)(2,1)S(1)}) custom-call(s32[3]{0:T(128)S(1)} %pad_add_fusion.scalars, bf16[27,32,32]{2,1,0:T(8,128)(2,1)S(1)} %bitcast.37, bf16[27,32,32]{2,1,0:T(8,128)(2,1)S(1)} %bitcast.38, ...), custom_call_target="tpu_custom_call" | custom-call | flops 1000000000 | bytes 4000000 | tf_op jit(solution)/shard_map/bands/pallas_call | solution.py:237
  30.1 0.0 collective-permute-done.2.oth
  30.2 6.2 %levels.1 = (bf16[2,128,128]{2,1,0:T(8,128)(2,1)S(1)}, f32[512,128]{1,0:T(8,128)S(1)}) custom-call(s32[3]{0:T(128)S(1)} %pad_add_fusion.scalars, bf16[4,40,16,128]{3,2,1,0:T(8,128)(2,1)S(1)} %all_to_all.20.own, bf16[4,40,16,128]{3,2,1,0:T(8,128)(2,1)S(1)} %collective-permute-done.2.oth, bf16[256,2304]{1,0:T(8,128)(2,1)S(1)} %get-tuple-element.9.t1, ...), custom_call_target="tpu_custom_call" | custom-call | flops 10000000000 | bytes 8000000 | tf_op jit(solution)/shard_map/levels/pallas_call | solution.py:263
  36.4 12.8 %all_to_all.21 = f32[16,32,128]{2,1,0:T(8,128)S(1)} all-to-all(f32[16,32,128]{2,1,0:T(8,128)S(1)} %bitcast.36), channel_id=1, replica_groups={{0,64,8,72,2,66,10,74,4,68,12,76,6,70,14,78},{16,80,24,88,18,82,26,90,2..., dimensions={0} | all-to-all | bytes 524288 | tf_op jit(solution)/shard_map/all_to_all | solution.py:281
  49.3 25.0 %all_to_all.22 = f32[16,32,128]{2,1,0:T(8,128)S(1)} all-to-all(f32[16,32,128]{2,1,0:T(8,128)S(1)} %broadcast_in_dim.6), channel_id=1, replica_groups={{0,16,40,56,128,144,168,184,320,336,360,376,448,464,488,504},{64,80,104..., dimensions={0} | all-to-all | bytes 524288 | tf_op jit(solution)/shard_map/all_to_all | solution.py:281
  74.3 0.7 broadcast_in_dim.7
  74.9 7.3 %all-to-all-start.3 = ((bf16[16,32,128]{2,1,0:T(8,128)(2,1)}), bf16[16,32,128]{2,1,0:T(8,128)(2,1)S(1)}, u32[]{:S(2)}, u32[]{:S(2)}) async-start(bf16[16,32,128]{2,1,0:T(8,128)(2,1)} %broadcast_in_dim.7), calls=%async_computation.3 | async-start | bytes 262144 | tf_op jit(solution)/shard_map/all_to_all | solution.py:281
  82.2 0.6 copy.22
  82.9 5.6 %all-to-all-done.3 = bf16[16,32,128]{2,1,0:T(8,128)(2,1)S(1)} async-done(((bf16[16,32,128]{2,1,0:T(8,128)(2,1)}), bf16[16,32,128]{2,1,0:T(8,128)(2,1)S(1)}, u32[]{:S(2)}, u32[]{:S(2)}) %all-to-all-start.3) | async-done | bytes 131104 | tf_op jit(solution)/shard_map/all_to_all | solution.py:281
  88.5 0.8 slice.12
  89.3 0.7 slice.11
  (8 shorter events, 0.1 us)
Async XLA Ops:
  2.4 9.5 %collective-permute-start = (bf16[20,16,128]{2,1,0:T(8,128)(2,1)S(1)}, bf16[20,16,128]{2,1,0:T(8,128)(2,1)S(1)}, u32[]{:S(2)}, u32[]{:S(2)}) collective-permute-start(bf16[20,16,128]{2,1,0:T(8,128)(2,1)S(1)} %constant_dynamic-update-slice_fusion), channel_id=1, source_target_pairs={{0,8},{2,10},{4,12},{6,14},{8,16},{10,18},{12,20},{14,22},{16,24},... | collective-permute-start | bytes 245768 | tf_op jit(solution)/shard_map/ppermute | solution.py:19
  5.9 7.6 %collective-permute-start.1 = (bf16[20,16,128]{2,1,0:T(8,128)(2,1)S(1)}, bf16[20,16,128]{2,1,0:T(8,128)(2,1)S(1)}, u32[]{:S(2)}, u32[]{:S(2)}) collective-permute-start(bf16[20,16,128]{2,1,0:T(8,128)(2,1)S(1)} %constant_dynamic-update-slice_fusion), channel_id=1, source_target_pairs={{8,0},{10,2},{12,4},{14,6},{16,8},{18,10},{20,12},{22,14},{24,16},... | collective-permute-start | bytes 245768 | tf_op jit(solution)/shard_map/ppermute | solution.py:19
  13.6 14.5 %copy-start = (bf16[32,32,27]{1,0,2:T(8,128)(2,1)S(1)}, bf16[32,32,27]{1,0,2:T(8,128)(2,1)}, u32[]{:S(2)}) copy-start(bf16[32,32,27]{1,0,2:T(8,128)(2,1)} %param.5) | copy-start | bytes 165892
  13.7 14.6 %copy-start.1 = (bf16[64,32,27]{0,1,2:T(8,128)(2,1)S(1)}, bf16[64,32,27]{0,1,2:T(8,128)(2,1)}, u32[]{:S(2)}) copy-start(bf16[64,32,27]{0,1,2:T(8,128)(2,1)} %param.6) | copy-start | bytes 331780
  26.2 4.0 %collective-permute-start.2 = (bf16[4,40,16,128]{3,2,1,0:T(8,128)(2,1)S(1)}, bf16[4,40,16,128]{3,2,1,0:T(8,128)(2,1)S(1)}, u32[]{:S(2)}, u32[]{:S(2)}) collective-permute-start(bf16[4,40,16,128]{3,2,1,0:T(8,128)(2,1)S(1)} %all_to_all.20.own), channel_id=1, source_target_pairs={{0,1},{1,0},{2,3},{3,2},{4,5},{5,4},{6,7},{7,6},{8,9},{9,8},{10,11... | collective-permute-start | bytes 1966088 | tf_op jit(solution)/shard_map/ppermute | solution.py:318
  74.9 13.5 %all-to-all-start.3 = ((bf16[16,32,128]{2,1,0:T(8,128)(2,1)}), bf16[16,32,128]{2,1,0:T(8,128)(2,1)S(1)}, u32[]{:S(2)}, u32[]{:S(2)}) async-start(bf16[16,32,128]{2,1,0:T(8,128)(2,1)} %broadcast_in_dim.7), calls=%async_computation.3 | async-start | bytes 262144 | tf_op jit(solution)/shard_map/all_to_all | solution.py:281

commit v3 on v2

--- a/solution.py
+++ b/solution.py
@@ -39,40 +39,56 @@
 NEAR, FAR = near_groups()
 
 
-def band_kernel(scalars, w1, w1t, w2, w2t, t1, t1t, t2, t2t):
+def band_kernel(scalars, w1, w2, t1, t1t, t2, t2t, rows_one):
     turn = scalars[0] * 16
     half = pl.multiple_of(turn, 16)
 
-    def fill(weights, out, height, rows, width, lanes, sign, turn):
+    def marks_of(width, lanes, sign, turn):
         row = lax.broadcasted_iota(jnp.int32, (3 * width, lanes), 0)
         lane = lax.broadcasted_iota(jnp.int32, (3 * width, lanes), 1)
         base = lane - (sign * (row // width - 1) * width + (row + turn) % width)
+        return lambda h: jnp.where(base == h * width, 1.0, 0.0).astype(BF16)
+
+    def taps_of(ref, flip):
+        order = [(2 - a, 2 - c) if flip else (a, c) for a in range(3) for c in range(3)]
+        return [[ref[9 * a + 3 * b + c] for b in range(3)] for a, c in order]
+
+    def straight(ref, flip, marks, height, put):
+        taps = taps_of(ref, flip)
+        parts = [jnp.concatenate([tap[b] for tap in taps], axis=0) for b in range(3)]
+        weights = jnp.concatenate(parts, axis=1)
         for h in range(height):
-            marks = jnp.where(base == h * width, 1.0, 0.0).astype(BF16)
-            bands = jnp.dot(weights, marks, preferred_element_type=F32).astype(BF16)
+            put(h, jnp.dot(weights, marks(h), preferred_element_type=F32).astype(BF16))
+
+    def crossed(ref, flip, marks, height, put):
+        parts = [jnp.concatenate(tap, axis=0) for tap in taps_of(ref, flip)]
+        weights = jnp.concatenate(parts, axis=1)
+        for h in range(height):
+            bands = lax.dot_general(
+                weights, marks(h), (((0,), (0,)), ((), ())), preferred_element_type=F32
+            )
+            put(h, bands.astype(BF16))
+
+    def into(out, rows, lanes):
+        def put(h, bands):
             for tap in range(9):
                 out[h * rows : (h + 1) * rows, tap * lanes : (tap + 1) * lanes] = bands[
                     tap * rows : (tap + 1) * rows
                 ]
 
-    def forward(ref):
-        parts = [
-            jnp.concatenate([ref[9 * a + 3 * b + c] for a in range(3) for c in range(3)], axis=0)
-            for b in range(3)
-        ]
-        return jnp.concatenate(parts, axis=1)
-
-    def backward(load):
-        taps = [(2 - a, 2 - c) for a in range(3) for c in range(3)]
-        parts = [
-            jnp.concatenate([load(9 * a + 3 * b + c) for a, c in taps], axis=0) for b in range(3)
-        ]
-        return jnp.concatenate(parts, axis=1)
-
-    fill(forward(w1), t1, 8, 32, 32, 256, 1, turn)
-    fill(forward(w2), t2, 4, 64, 32, 128, 1, 0)
-    fill(backward(lambda t: w2t[t]), t2t, 4, 32, 64, 256, -1, 0)
-    fill(backward(lambda t: w1t[t, pl.ds(half, 16), :]), t1t, 8, 16, 32, 256, -1, 0)
+        return put
+
+    def put_half(h, bands):
+        rows_one[h] = bands
+        for tap in range(9):
+            t1t[h * 16 : (h + 1) * 16, tap * 256 : (tap + 1) * 256] = rows_one[
+                h, pl.ds(tap * 32 + half, 16), :
+            ]
+
+    straight(w1, False, marks_of(32, 256, 1, turn), 8, into(t1, 32, 256))
+    crossed(w1, True, marks_of(32, 256, -1, 0), 8, put_half)
+    crossed(w2, False, marks_of(32, 128, 1, 0), 4, into(t2, 64, 128))
+    straight(w2, True, marks_of(64, 256, -1, 0), 4, into(t2t, 32, 256))
 
 
 def shifted(value, step):
@@ -99,7 +115,9 @@
     planes += [(slot(0), 12), (slot(0), 20)]
     planes += [(slot(delta), 20 + 8 * p) for delta in (1, 2, 3) for p in range(2)]
     planes += [(slot(0), 32)]
-    for j, (at, start) in enumerate(planes):
+
+    def load_plane(j):
+        at, start = planes[j]
         plane = jnp.concatenate(
             [own[at, start : start + 8], oth[at, start : start + 8]], axis=1
         ).reshape(256, 128)
@@ -109,7 +127,13 @@
             if j >= 7:
                 XP[j - 7, c, :, 128:] = part
 
+    for j in (0, 1, 7, 8):
+        load_plane(j)
+
     for k in range(7):
+        for j in (k + 2, k + 9):
+            if j not in (7, 8) and j < 16:
+                load_plane(j)
         pre = jnp.dot(t1[...], XP[k : k + 3].reshape(2304, 256), preferred_element_type=F32)
         act = (pre * jax.nn.sigmoid(pre)).astype(BF16).astype(F32).reshape(4, 2, 32, 256)
         rows = (act[:, 0] + act[:, 1]).reshape(128, 256)
@@ -227,22 +251,24 @@
     wg[432:] = jnp.zeros((80, 128), F32)
 
     out = jnp.dot(t1t[...], HP[...].reshape(2304, 256), preferred_element_type=F32)
-    gf[0] = out[:, :128].astype(BF16)
-    gf[1] = out[:, 128:].astype(BF16)
-
-
-def band_weights(scalars, w1, w1t, w2, w2t):
+    for p in range(2):
+        side = out[:, p * 128 : (p + 1) * 128].reshape(8, 16, 128)
+        gf[:, p] = jnp.transpose(side, (1, 0, 2)).astype(BF16)
+
+
+def band_weights(scalars, w1, w2):
     vmem = pl.BlockSpec(memory_space=pltpu.VMEM)
     shapes = [(256, 2304), (128, 2304), (256, 1152), (128, 2304)]
     return pl.pallas_call(
         band_kernel,
-        in_specs=[pl.BlockSpec(memory_space=pltpu.SMEM)] + [vmem] * 4,
+        in_specs=[pl.BlockSpec(memory_space=pltpu.SMEM)] + [vmem] * 2,
         out_specs=[vmem] * 4,
+        scratch_shapes=[pltpu.VMEM((8, 288, 256), BF16)],
         out_shape=[jax.ShapeDtypeStruct(shape, BF16) for shape in shapes],
         cost_estimate=pl.CostEstimate(flops=10**9, bytes_accessed=4 * 10**6, transcendentals=0),
         compiler_params=pltpu.CompilerParams(vmem_limit_bytes=16 * 2**20),
         name="bands",
-    )(scalars, w1, w1t, w2, w2t)
+    )(scalars, w1, w2)
 
 
 def levels(scalars, own, oth, bands):
@@ -265,7 +291,7 @@
         in_specs=[pl.BlockSpec(memory_space=pltpu.SMEM)] + [vmem] * 6,
         out_specs=[vmem, vmem],
         out_shape=[
-            jax.ShapeDtypeStruct((2, 128, 128), BF16),
+            jax.ShapeDtypeStruct((16, 2, 8, 128), BF16),
             jax.ShapeDtypeStruct((512, 128), F32),
         ],
         scratch_shapes=[pltpu.VMEM(shape, dtype) for shape, dtype in scratch],
@@ -285,7 +311,28 @@
     near = jnp.sum(exchange(part.reshape(16, 32, 128), NEAR), axis=0)
     whole = jnp.sum(exchange(jnp.broadcast_to(near, (16, 32, 128)), FAR), axis=0)
     copies = jnp.broadcast_to(whole.astype(BF16), (16, 32, 128))
-    return exchange(copies, NEAR).reshape(512, 128).astype(F32)
+    return exchange(copies, NEAR)
+
+
+def split_kernel(total, one, two):
+    rows = total[...].reshape(512, 128)[:432].astype(F32)
+    one[...] = rows[:, :32]
+    two[...] = rows[:, 32:96]
+
+
+def split_total(total):
+    vmem = pl.BlockSpec(memory_space=pltpu.VMEM)
+    return pl.pallas_call(
+        split_kernel,
+        in_specs=[vmem],
+        out_specs=[vmem, vmem],
+        out_shape=[
+            jax.ShapeDtypeStruct((432, 32), F32),
+            jax.ShapeDtypeStruct((432, 64), F32),
+        ],
+        compiler_params=pltpu.CompilerParams(vmem_limit_bytes=4 * 2**20),
+        name="split",
+    )(total)
 
 
 def shards(feats, weight_one, weight_two, cotangent):
@@ -302,8 +349,6 @@
     bands = band_weights(
         scalars,
         jnp.transpose(weight_one, (2, 0, 1)),
-        jnp.transpose(weight_one, (2, 1, 0)),
-        jnp.transpose(weight_two, (2, 0, 1)),
         jnp.transpose(weight_two, (2, 1, 0)),
     )
 
@@ -317,10 +362,9 @@
     own = lax.all_to_all(jnp.stack(slots, 0), "x", 0, 0, tiled=True)
     oth = lax.ppermute(own, "chan", [(0, 1), (1, 0)])
     grad_feats, part = levels(scalars, own, oth, bands)
-    total = total_over_depth(part)[:432]
-    grad_weight_one = jnp.transpose(total[:, :32].reshape(27, 16, 32), (2, 1, 0))
-    grad_weight_two = jnp.transpose(total[:, 32:96].reshape(27, 16, 64), (2, 1, 0))
-    grad_feats = jnp.transpose(grad_feats.reshape(2, 8, 16, 128), (2, 0, 1, 3))
+    one, two = split_total(total_over_depth(part))
+    grad_weight_one = jnp.transpose(one.reshape(27, 16, 32), (2, 1, 0))
+    grad_weight_two = jnp.transpose(two.reshape(27, 16, 64), (2, 1, 0))
     return (grad_feats, grad_weight_one, grad_weight_two)
 
 

time: 90.5 us -> 89 us (0.983)
  blocking collectives: 50.3 us -> 63.4 us
  starting transfers between devices: 18.2 us -> 10.9 us
  waiting for transfers between devices: 6.7 us -> 1.36 us
  local copies, waits for them, and re-layouts: 6.04 us -> 2.82 us
  Pallas kernels: 7.73 us -> 9.04 us
    all_to_all x2 -> x3, blocking collectives: 37.8 us -> 50.9 us  [exchange(): lax.all_to_all(pieces, DEPTH, 0, 0, axis_index_groups=groups, tiled=True)]
    all_to_all x1 -> x0, starting transfers between devices: 7.3 us -> none  [exchange(): lax.all_to_all(pieces, DEPTH, 0, 0, axis_index_groups=groups, tiled=True)]
    all_to_all x1 -> x0, waiting for transfers between devices: 5.58 us -> none  [exchange(): lax.all_to_all(pieces, DEPTH, 0, 0, axis_index_groups=groups, tiled=True)]
    slice x2 -> x0, local copies, waits for them, and re-layouts: 1.51 us -> none  [the longest x1 0.81 us: shards(): total[:, 32:96].reshape(27, 16, 64)]
    unnamed x10 -> x8, local copies, waits for them, and re-layouts: 2.17 us -> 1.75 us
  transfers between devices with their start and end apart: 4 -> 3, of which waited for: 3 -> 3; matrix products, arithmetic and copies ran while one was open for 2% -> 1% of each run, Pallas kernels for 2% -> 2%
where the time goes in v3:
time: 89 us; the launch traced here: 88.5 us
  blocking collectives  63.4 us (71%)
  starting transfers between devices  10.9 us (12%)
  Pallas kernels  9.04 us (10%)
  local copies, waits for them, and re-layouts  2.82 us (3%)
  waiting for transfers between devices  1.36 us (2%)
    all_to_all x3, blocking collectives, exchange(): lax.all_to_all(pieces, DEPTH, 0, 0, axis_index_groups=groups, tiled=True)  50.9 us
    all_to_all x1, blocking collectives, shards(): own = lax.all_to_all(jnp.stack(slots, 0), 'x', 0, 0, tiled=True)  12.5 us
    ppermute x2, starting transfers between devices, depth_shift(): return lax.ppermute(block, DEPTH, pairs)  9 us
    pallas_call x1, Pallas kernels, levels(): pl.pallas_call(main_kernel, in_specs=[pl.BlockSpec(memory_space=pltpu.SME...  6.53 us
    ppermute x1, starting transfers between devices, shards(): oth = lax.ppermute(own, 'chan', [(0, 1), (1, 0)])  1.91 us
  transfers between devices with their start and end apart: 3, of which 3 were waited for; matrix products, arithmetic and copies ran while one was open for 1% of the time, Pallas kernels for 2%

profile of v3, /device:TPU:8, one launch (start us, length us, event | category | flops | bytes accessed | tf_op | source)
XLA Modules:
  0.0 88.5 jit_solution(2409747996568984349)
XLA Ops:
  0.6 0.8 copy.10
  1.4 0.1 reshape.26
  1.5 0.9 copy_dynamic-update-slice_fusion.1
  2.4 3.5 %collective-permute-start = (bf16[20,16,128]{2,1,0:T(8,128)(2,1)S(1)}, bf16[20,16,128]{2,1,0:T(8,128)(2,1)S(1)}, u32[]{:S(2)}, u32[]{:S(2)}) collective-permute-start(bf16[20,16,128]{2,1,0:T(8,128)(2,1)S(1)} %constant_dynamic-update-slice_fusion), channel_id=1, source_target_pairs={{0,8},{2,10},{4,12},{6,14},{8,16},{10,18},{12,20},{14,22},{16,24},... | collective-permute-start | bytes 245768 | tf_op jit(solution)/shard_map/ppermute | solution.py:19
  5.9 5.5 %collective-permute-start.1 = (bf16[20,16,128]{2,1,0:T(8,128)(2,1)S(1)}, bf16[20,16,128]{2,1,0:T(8,128)(2,1)S(1)}, u32[]{:S(2)}, u32[]{:S(2)}) collective-permute-start(bf16[20,16,128]{2,1,0:T(8,128)(2,1)S(1)} %constant_dynamic-update-slice_fusion), channel_id=1, source_target_pairs={{8,0},{10,2},{12,4},{14,6},{16,8},{18,10},{20,12},{22,14},{24,16},... | collective-permute-start | bytes 245768 | tf_op jit(solution)/shard_map/ppermute | solution.py:19
  11.4 0.4 collective-permute-done
  11.9 0.9 copy_dynamic-update-slice_fusion
  12.8 0.7 collective-permute-done.1
  13.4 0.1 dynamic-slice_bitcast_fusion.3
  13.6 0.0 copy-start
  13.6 0.0 copy-start.1
  13.6 0.1 pad_maximum_fusion
  13.7 12.5 %all_to_all.20.own = bf16[4,40,16,128]{3,2,1,0:T(8,128)(2,1)S(1)} all-to-all(bf16[4,40,16,128]{3,2,1,0:T(8,128)(2,1)S(1)} %pad_maximum_fusion), channel_id=1, replica_groups=mesh['z'=8,'y'=8,'x'=4,'chan'=2] {'x'}, dimensions={0} | all-to-all | bytes 1310720 | tf_op jit(solution)/shard_map/all_to_all | solution.py:362
  26.2 1.9 %collective-permute-start.2 = (bf16[4,40,16,128]{3,2,1,0:T(8,128)(2,1)S(1)}, bf16[4,40,16,128]{3,2,1,0:T(8,128)(2,1)S(1)}, u32[]{:S(2)}, u32[]{:S(2)}) collective-permute-start(bf16[4,40,16,128]{3,2,1,0:T(8,128)(2,1)S(1)} %all_to_all.20.own), channel_id=1, source_target_pairs={{0,1},{1,0},{2,3},{3,2},{4,5},{5,4},{6,7},{7,6},{8,9},{9,8},{10,11... | collective-permute-start | bytes 1966088 | tf_op jit(solution)/shard_map/ppermute | solution.py:363
  28.1 0.1 pad_add_fusion.scalars
  28.2 0.0 copy-done
  28.2 0.0 copy-done.1
  28.2 1.7 %bands.1 = (bf16[256,2304]{1,0:T(8,128)(2,1)S(1)}, bf16[128,2304]{1,0:T(8,128)(2,1)S(1)}, bf16[256,1152]{1,0:T(8,128)(2,1)S(1)}, bf16[128,2304]{1,0:T(8,128)(2,1)S(1)}) custom-call(s32[3]{0:T(128)S(1)} %pad_add_fusion.scalars, bf16[27,32,32]{2,1,0:T(8,128)(2,1)S(1)} %bitcast.27, bf16[27,32,64]{2,1,0:T(8,128)(2,1)S(1)} %bitcast.28), custom_call_target="tpu_custom_call" | custom-call | flops 1000000000 | bytes 4000000 | tf_op jit(solution)/shard_map/bands/pallas_call | solution.py:262
  29.9 0.2 collective-permute-done.2.oth
  30.1 6.5 %levels.1 = (bf16[16,2,8,128]{3,2,1,0:T(8,128)(2,1)}, f32[512,128]{1,0:T(8,128)S(1)}) custom-call(s32[3]{0:T(128)S(1)} %pad_add_fusion.scalars, bf16[4,40,16,128]{3,2,1,0:T(8,128)(2,1)S(1)} %all_to_all.20.own, bf16[4,40,16,128]{3,2,1,0:T(8,128)(2,1)S(1)} %collective-permute-done.2.oth, bf16[256,2304]{1,0:T(8,128)(2,1)S(1)} %get-tuple-element.11.t1, ...), custom_call_target="tpu_custom_call" | custom-call | flops 10000000000 | bytes 8000000 | tf_op jit(solution)/shard_map/levels/pallas_call | solution.py:289
  36.7 12.7 %all_to_all.21 = f32[16,32,128]{2,1,0:T(8,128)S(1)} all-to-all(f32[16,32,128]{2,1,0:T(8,128)S(1)} %bitcast.26), channel_id=1, replica_groups={{0,64,8,72,2,66,10,74,4,68,12,76,6,70,14,78},{16,80,24,88,18,82,26,90,2..., dimensions={0} | all-to-all | bytes 524288 | tf_op jit(solution)/shard_map/all_to_all | solution.py:307
  49.4 24.6 %all_to_all.22 = f32[16,32,128]{2,1,0:T(8,128)S(1)} all-to-all(f32[16,32,128]{2,1,0:T(8,128)S(1)} %broadcast_in_dim.6), channel_id=1, replica_groups={{0,16,40,56,128,144,168,184,320,336,360,376,448,464,488,504},{64,80,104..., dimensions={0} | all-to-all | bytes 524288 | tf_op jit(solution)/shard_map/all_to_all | solution.py:307
  74.1 13.6 %all_to_all.23.total = bf16[16,32,128]{2,1,0:T(8,128)(2,1)S(1)} all-to-all(bf16[16,32,128]{2,1,0:T(8,128)(2,1)S(1)} %broadcast_in_dim.7), channel_id=1, replica_groups={{0,64,8,72,2,66,10,74,4,68,12,76,6,70,14,78},{16,80,24,88,18,82,26,90,2..., dimensions={0} | all-to-all | bytes 262144 | tf_op jit(solution)/shard_map/all_to_all | solution.py:307
  87.7 0.8 split.1
  (8 shorter events, 0.1 us)
Async XLA Ops:
  2.4 9.5 %collective-permute-start = (bf16[20,16,128]{2,1,0:T(8,128)(2,1)S(1)}, bf16[20,16,128]{2,1,0:T(8,128)(2,1)S(1)}, u32[]{:S(2)}, u32[]{:S(2)}) collective-permute-start(bf16[20,16,128]{2,1,0:T(8,128)(2,1)S(1)} %constant_dynamic-update-slice_fusion), channel_id=1, source_target_pairs={{0,8},{2,10},{4,12},{6,14},{8,16},{10,18},{12,20},{14,22},{16,24},... | collective-permute-start | bytes 245768 | tf_op jit(solution)/shard_map/ppermute | solution.py:19
  5.9 7.6 %collective-permute-start.1 = (bf16[20,16,128]{2,1,0:T(8,128)(2,1)S(1)}, bf16[20,16,128]{2,1,0:T(8,128)(2,1)S(1)}, u32[]{:S(2)}, u32[]{:S(2)}) collective-permute-start(bf16[20,16,128]{2,1,0:T(8,128)(2,1)S(1)} %constant_dynamic-update-slice_fusion), channel_id=1, source_target_pairs={{8,0},{10,2},{12,4},{14,6},{16,8},{18,10},{20,12},{22,14},{24,16},... | collective-permute-start | bytes 245768 | tf_op jit(solution)/shard_map/ppermute | solution.py:19
  13.6 14.6 %copy-start = (bf16[32,32,27]{1,0,2:T(8,128)(2,1)S(1)}, bf16[32,32,27]{1,0,2:T(8,128)(2,1)}, u32[]{:S(2)}) copy-start(bf16[32,32,27]{1,0,2:T(8,128)(2,1)} %param.5) | copy-start | bytes 165892
  13.6 14.6 %copy-start.1 = (bf16[64,32,27]{0,1,2:T(8,128)(2,1)S(1)}, bf16[64,32,27]{0,1,2:T(8,128)(2,1)}, u32[]{:S(2)}) copy-start(bf16[64,32,27]{0,1,2:T(8,128)(2,1)} %param.6) | copy-start | bytes 331780
  26.2 4.0 %collective-permute-start.2 = (bf16[4,40,16,128]{3,2,1,0:T(8,128)(2,1)S(1)}, bf16[4,40,16,128]{3,2,1,0:T(8,128)(2,1)S(1)}, u32[]{:S(2)}, u32[]{:S(2)}) collective-permute-start(bf16[4,40,16,128]{3,2,1,0:T(8,128)(2,1)S(1)} %all_to_all.20.own), channel_id=1, source_target_pairs={{0,1},{1,0},{2,3},{3,2},{4,5},{5,4},{6,7},{7,6},{8,9},{9,8},{10,11... | collective-permute-start | bytes 1966088 | tf_op jit(solution)/shard_map/ppermute | solution.py:363

commit v4 on v3

--- a/solution.py
+++ b/solution.py
@@ -39,8 +39,34 @@
 NEAR, FAR = near_groups()
 
 
-def band_kernel(scalars, w1, w2, t1, t1t, t2, t2t, rows_one):
-    turn = scalars[0] * 16
+def position():
+    place = (lax.axis_index("z") * 8 + lax.axis_index("y")) * 4 + lax.axis_index("x")
+    return lax.axis_index("chan"), place
+
+
+def gather_kernel(feats_far, cot_far, w1, w2, block, w1_near, w2_near, feats, cot, sems):
+    pairs = ((feats_far, feats), (cot_far, cot), (w1, w1_near), (w2, w2_near))
+    copies = [
+        pltpu.make_async_copy(source, target, sems.at[index])
+        for index, (source, target) in enumerate(pairs)
+    ]
+    for copy in copies:
+        copy.start()
+    copies[0].wait()
+    for p in range(2):
+        plane = jnp.transpose(feats[:, p].astype(F32), (1, 0, 2))
+        block[p * 8 : (p + 1) * 8] = plane.astype(BF16)
+    copies[1].wait()
+    rows = jnp.transpose(cot[...].reshape(32, 4, 64).astype(F32), (1, 0, 2))
+    for high in range(2):
+        pair = jnp.concatenate([rows[2 * high], rows[2 * high + 1]], axis=1)
+        block[16 + 2 * high : 18 + 2 * high] = pair.astype(BF16).reshape(2, 16, 128)
+    for copy in copies[2:]:
+        copy.wait()
+
+
+def band_kernel(w1, w2, t1, t1t, t2, t2t, rows_one):
+    turn = position()[0] * 16
     half = pl.multiple_of(turn, 16)
 
     def marks_of(width, lanes, sign, turn):
@@ -100,11 +126,10 @@
 
 
 def main_kernel(
-    scalars, own, oth, t1, t1t, t2, t2t, gf, wg, XP, PS, SL, QP, GP, HP, CT, FS, FP, G1, G2
+    own, oth, t1, t1t, t2, t2t, gf, wg, XP, PS, SL, QP, GP, HP, CT, FS, FP, G1, G2, GF, sem
 ):
-    member = scalars[0]
-    place = scalars[1]
-    x = scalars[2]
+    member, place = position()
+    x = lax.rem(place, 4)
     half = pl.multiple_of(member * 16, 16)
 
     def slot(delta):
@@ -221,6 +246,13 @@
                     to = ((q - 1) * 8 + h) * 128
                     G1[0:32, to : to + 128] = piece[h * 32 : (h + 1) * 32]
 
+    out = jnp.dot(t1t[...], HP[...].reshape(2304, 256), preferred_element_type=F32)
+    for p in range(2):
+        side = out[:, p * 128 : (p + 1) * 128].reshape(8, 16, 128)
+        GF[:, p] = jnp.transpose(side, (1, 0, 2)).astype(BF16)
+    away = pltpu.make_async_copy(GF, gf, sem)
+    away.start()
+
     nothing = jnp.zeros((16, 128), BF16)
     for a in range(3):
         for b in range(3):
@@ -249,29 +281,47 @@
         FS[...], G1[...], along, preferred_element_type=F32
     ) + lax.dot_general(FP[...], G2[...], along, preferred_element_type=F32)
     wg[432:] = jnp.zeros((80, 128), F32)
-
-    out = jnp.dot(t1t[...], HP[...].reshape(2304, 256), preferred_element_type=F32)
-    for p in range(2):
-        side = out[:, p * 128 : (p + 1) * 128].reshape(8, 16, 128)
-        gf[:, p] = jnp.transpose(side, (1, 0, 2)).astype(BF16)
-
-
-def band_weights(scalars, w1, w2):
+    away.wait()
+
+
+def own_block(feats, cot, w1, w2):
+    vmem = pl.BlockSpec(memory_space=pltpu.VMEM)
+    hbm = pl.BlockSpec(memory_space=pltpu.MemorySpace.HBM)
+    return pl.pallas_call(
+        gather_kernel,
+        in_specs=[hbm] * 4,
+        out_specs=[vmem] * 3,
+        out_shape=[
+            jax.ShapeDtypeStruct((20, 16, 128), BF16),
+            jax.ShapeDtypeStruct(w1.shape, BF16),
+            jax.ShapeDtypeStruct(w2.shape, BF16),
+        ],
+        scratch_shapes=[
+            pltpu.VMEM(feats.shape, BF16),
+            pltpu.VMEM(cot.shape, BF16),
+            pltpu.SemaphoreType.DMA((4,)),
+        ],
+        compiler_params=pltpu.CompilerParams(vmem_limit_bytes=4 * 2**20),
+        name="gather",
+    )(*[pltpu.with_memory_space_constraint(array, pltpu.HBM) for array in (feats, cot, w1, w2)])
+
+
+def band_weights(w1, w2):
     vmem = pl.BlockSpec(memory_space=pltpu.VMEM)
     shapes = [(256, 2304), (128, 2304), (256, 1152), (128, 2304)]
     return pl.pallas_call(
         band_kernel,
-        in_specs=[pl.BlockSpec(memory_space=pltpu.SMEM)] + [vmem] * 2,
+        in_specs=[vmem] * 2,
         out_specs=[vmem] * 4,
         scratch_shapes=[pltpu.VMEM((8, 288, 256), BF16)],
         out_shape=[jax.ShapeDtypeStruct(shape, BF16) for shape in shapes],
         cost_estimate=pl.CostEstimate(flops=10**9, bytes_accessed=4 * 10**6, transcendentals=0),
         compiler_params=pltpu.CompilerParams(vmem_limit_bytes=16 * 2**20),
         name="bands",
-    )(scalars, w1, w2)
-
-
-def levels(scalars, own, oth, bands):
+    )(w1, w2)
+
+
+def levels(own, oth, bands):
     vmem = pl.BlockSpec(memory_space=pltpu.VMEM)
     scratch = [
         ((9, 3, 256, 256), BF16),
@@ -285,22 +335,24 @@
         ((432, 512), BF16),
         ((128, 2048), BF16),
         ((128, 512), BF16),
+        ((16, 2, 8, 128), BF16),
     ]
     return pl.pallas_call(
         main_kernel,
-        in_specs=[pl.BlockSpec(memory_space=pltpu.SMEM)] + [vmem] * 6,
-        out_specs=[vmem, vmem],
+        in_specs=[vmem] * 6,
+        out_specs=[pl.BlockSpec(memory_space=pl.ANY), vmem],
         out_shape=[
             jax.ShapeDtypeStruct((16, 2, 8, 128), BF16),
             jax.ShapeDtypeStruct((512, 128), F32),
         ],
-        scratch_shapes=[pltpu.VMEM(shape, dtype) for shape, dtype in scratch],
+        scratch_shapes=[pltpu.VMEM(shape, dtype) for shape, dtype in scratch]
+        + [pltpu.SemaphoreType.DMA(())],
         cost_estimate=pl.CostEstimate(
             flops=10**10, bytes_accessed=8 * 10**6, transcendentals=10**6
         ),
         compiler_params=pltpu.CompilerParams(vmem_limit_bytes=28 * 2**20),
         name="levels",
-    )(scalars, own, oth, *bands)
+    )(own, oth, *bands)
 
 
 def exchange(pieces, groups):
@@ -336,21 +388,17 @@
 
 
 def shards(feats, weight_one, weight_two, cotangent):
-    member = lax.axis_index("chan")
-    place = lax.axis_index(DEPTH)
     x = lax.axis_index("x")
-    fields = jnp.transpose(feats, (1, 2, 0, 3)).reshape(16, 16, 128)
-    cot = jnp.transpose(cotangent.reshape(32, 2, 2, 64), (1, 0, 2, 3)).reshape(4, 16, 128)
-    block = jnp.concatenate([fields, cot], axis=0)
-    up = depth_shift(block, ROW)
-    down = depth_shift(block, -ROW)
-
-    scalars = jnp.stack([member, place, x]).astype(jnp.int32)
-    bands = band_weights(
-        scalars,
+    block, w1, w2 = own_block(
+        feats,
+        cotangent,
         jnp.transpose(weight_one, (2, 0, 1)),
         jnp.transpose(weight_two, (2, 1, 0)),
     )
+    up = depth_shift(block, ROW)
+    down = depth_shift(block, -ROW)
+
+    bands = band_weights(w1, w2)
 
     three = jnp.concatenate([up, block, down], axis=0)
     slots = [
@@ -361,7 +409,7 @@
     ]
     own = lax.all_to_all(jnp.stack(slots, 0), "x", 0, 0, tiled=True)
     oth = lax.ppermute(own, "chan", [(0, 1), (1, 0)])
-    grad_feats, part = levels(scalars, own, oth, bands)
+    grad_feats, part = levels(own, oth, bands)
     one, two = split_total(total_over_depth(part))
     grad_weight_one = jnp.transpose(one.reshape(27, 16, 32), (2, 1, 0))
     grad_weight_two = jnp.transpose(two.reshape(27, 16, 64), (2, 1, 0))

time: 89 us -> 87.1 us (0.979)
  local copies, waits for them, and re-layouts: 2.82 us -> 0.2 us
  waiting for transfers between devices: 1.36 us -> 2.79 us
    unnamed x8 -> x2, local copies, waits for them, and re-layouts: 1.75 us -> 0.02 us
    pallas_call x2 -> x3, Pallas kernels: 8.25 us -> 8.2 us  [the longest x1 5.81 us: levels(): pl.pallas_call(main_kernel, in_specs=[vmem] * 6, out_specs=[pl.BlockSpec(...]
  transfers between devices with their start and end apart: 3 -> 3, of which waited for: 3 -> 3; matrix products, arithmetic and copies ran while one was open for 1% -> 0% of each run, Pallas kernels for 2% -> 1%
where the time goes in v4:
time: 87.1 us; the launch traced here: 86.8 us
  blocking collectives  63 us (72%)
  starting transfers between devices  10.9 us (13%)
  Pallas kernels  8.98 us (10%)
  waiting for transfers between devices  2.79 us (3%)
    all_to_all x3, blocking collectives, exchange(): lax.all_to_all(pieces, DEPTH, 0, 0, axis_index_groups=groups, tiled=True)  50.7 us
    all_to_all x1, blocking collectives, shards(): own = lax.all_to_all(jnp.stack(slots, 0), 'x', 0, 0, tiled=True)  12.3 us
    ppermute x2, starting transfers between devices, depth_shift(): return lax.ppermute(block, DEPTH, pairs)  9 us
    pallas_call x1, Pallas kernels, levels(): pl.pallas_call(main_kernel, in_specs=[vmem] * 6, out_specs=[pl.BlockSpec(...  5.81 us
    ppermute x2, waiting for transfers between devices, depth_shift(): return lax.ppermute(block, DEPTH, pairs)  1.98 us
    ppermute x1, starting transfers between devices, shards(): oth = lax.ppermute(own, 'chan', [(0, 1), (1, 0)])  1.91 us
  transfers between devices with their start and end apart: 3, of which 3 were waited for; matrix products, arithmetic and copies ran while one was open for 0% of the time, Pallas kernels for 1%

profile of v4, /device:TPU:8, one launch (start us, length us, event | category | flops | bytes accessed | tf_op | source)
XLA Modules:
  0.0 86.8 jit_solution(10241475033204820173)
XLA Ops:
  0.6 1.1 %gather.1 = (bf16[20,16,128]{2,1,0:T(8,128)(2,1)S(1)}, bf16[27,32,32]{2,1,0:T(8,128)(2,1)S(1)}, bf16[27,32,64]{2,1,0:T(8,128)(2,1)S(1)}) custom-call(bf16[16,2,8,128]{3,2,1,0:T(8,128)(2,1)} %feats_far.1, bf16[32,1,4,64]{3,2,1,0:T(4,128)(2,1)} %cot_far.1, bf16[27,32,32]{2,1,0:T(8,128)(2,1)} %bitcast.18, bf16[27,32,64]{2,1,0:T(8,128)(2,1)} %bitcast.19), custom_call_target="tpu_custom_call" | custom-call | tf_op jit(solution)/shard_map/gather/pallas_call | solution.py:290
  1.8 3.5 %collective-permute-start = (bf16[20,16,128]{2,1,0:T(8,128)(2,1)S(1)}, bf16[20,16,128]{2,1,0:T(8,128)(2,1)S(1)}, u32[]{:S(2)}, u32[]{:S(2)}) collective-permute-start(bf16[20,16,128]{2,1,0:T(8,128)(2,1)S(1)} %get-tuple-element.14), channel_id=1, source_target_pairs={{0,8},{2,10},{4,12},{6,14},{8,16},{10,18},{12,20},{14,22},{16,24},... | collective-permute-start | bytes 245768 | tf_op jit(solution)/shard_map/ppermute | solution.py:19
  5.3 5.5 %collective-permute-start.1 = (bf16[20,16,128]{2,1,0:T(8,128)(2,1)S(1)}, bf16[20,16,128]{2,1,0:T(8,128)(2,1)S(1)}, u32[]{:S(2)}, u32[]{:S(2)}) collective-permute-start(bf16[20,16,128]{2,1,0:T(8,128)(2,1)S(1)} %get-tuple-element.14), channel_id=1, source_target_pairs={{8,0},{10,2},{12,4},{14,6},{16,8},{18,10},{20,12},{22,14},{24,16},... | collective-permute-start | bytes 245768 | tf_op jit(solution)/shard_map/ppermute | solution.py:19
  10.8 0.4 collective-permute-done
  11.3 1.5 %collective-permute-done.1 = bf16[20,16,128]{2,1,0:T(8,128)(2,1)S(1)} collective-permute-done((bf16[20,16,128]{2,1,0:T(8,128)(2,1)S(1)}, bf16[20,16,128]{2,1,0:T(8,128)(2,1)S(1)}, u32[]{:S(2)}, u32[]{:S(2)}) %collective-permute-start.1) | collective-permute-done | bytes 81952 | tf_op jit(solution)/shard_map/ppermute | solution.py:19
  12.8 0.1 dynamic-slice_bitcast_fusion.3
  13.0 0.1 pad_maximum_fusion
  13.1 12.3 %all_to_all.20.own = bf16[4,40,16,128]{3,2,1,0:T(8,128)(2,1)S(1)} all-to-all(bf16[4,40,16,128]{3,2,1,0:T(8,128)(2,1)S(1)} %pad_maximum_fusion), channel_id=1, replica_groups=mesh['z'=8,'y'=8,'x'=4,'chan'=2] {'x'}, dimensions={0} | all-to-all | bytes 1310720 | tf_op jit(solution)/shard_map/all_to_all | solution.py:410
  25.4 1.9 %collective-permute-start.2 = (bf16[4,40,16,128]{3,2,1,0:T(8,128)(2,1)S(1)}, bf16[4,40,16,128]{3,2,1,0:T(8,128)(2,1)S(1)}, u32[]{:S(2)}, u32[]{:S(2)}) collective-permute-start(bf16[4,40,16,128]{3,2,1,0:T(8,128)(2,1)S(1)} %all_to_all.20.own), channel_id=1, source_target_pairs={{0,1},{1,0},{2,3},{3,2},{4,5},{5,4},{6,7},{7,6},{8,9},{9,8},{10,11... | collective-permute-start | bytes 1966088 | tf_op jit(solution)/shard_map/ppermute | solution.py:411
  27.3 1.2 %bands.1 = (bf16[256,2304]{1,0:T(8,128)(2,1)S(1)}, bf16[128,2304]{1,0:T(8,128)(2,1)S(1)}, bf16[256,1152]{1,0:T(8,128)(2,1)S(1)}, bf16[128,2304]{1,0:T(8,128)(2,1)S(1)}) custom-call(bf16[27,32,32]{2,1,0:T(8,128)(2,1)S(1)} %get-tuple-element.15.w1, bf16[27,32,64]{2,1,0:T(8,128)(2,1)S(1)} %get-tuple-element.16.w2), custom_call_target="tpu_custom_call" | custom-call | flops 1000000000 | bytes 4000000 | tf_op jit(solution)/shard_map/bands/pallas_call | solution.py:312
  28.6 0.8 collective-permute-done.2.oth
  29.4 5.8 %levels.1 = (bf16[16,2,8,128]{3,2,1,0:T(8,128)(2,1)}, f32[512,128]{1,0:T(8,128)S(1)}) custom-call(bf16[4,40,16,128]{3,2,1,0:T(8,128)(2,1)S(1)} %all_to_all.20.own, bf16[4,40,16,128]{3,2,1,0:T(8,128)(2,1)S(1)} %collective-permute-done.2.oth, bf16[256,2304]{1,0:T(8,128)(2,1)S(1)} %get-tuple-element.17.t1, bf16[128,2304]{1,0:T(8,128)(2,1)S(1)} %get-tuple-element.18.t1t, ...), custom_call_target="tpu_custom_call" | custom-call | flops 10000000000 | bytes 8000000 | tf_op jit(solution)/shard_map/levels/pallas_call | solution.py:340
  35.2 12.6 %all_to_all.21 = f32[16,32,128]{2,1,0:T(8,128)S(1)} all-to-all(f32[16,32,128]{2,1,0:T(8,128)S(1)} %bitcast.17), channel_id=1, replica_groups={{0,64,8,72,2,66,10,74,4,68,12,76,6,70,14,78},{16,80,24,88,18,82,26,90,2..., dimensions={0} | all-to-all | bytes 524288 | tf_op jit(solution)/shard_map/all_to_all | solution.py:359
  47.8 24.7 %all_to_all.22 = f32[16,32,128]{2,1,0:T(8,128)S(1)} all-to-all(f32[16,32,128]{2,1,0:T(8,128)S(1)} %broadcast_in_dim.6), channel_id=1, replica_groups={{0,16,40,56,128,144,168,184,320,336,360,376,448,464,488,504},{64,80,104..., dimensions={0} | all-to-all | bytes 524288 | tf_op jit(solution)/shard_map/all_to_all | solution.py:359
  72.6 13.5 %all_to_all.23.total = bf16[16,32,128]{2,1,0:T(8,128)(2,1)S(1)} all-to-all(bf16[16,32,128]{2,1,0:T(8,128)(2,1)S(1)} %broadcast_in_dim.7), channel_id=1, replica_groups={{0,64,8,72,2,66,10,74,4,68,12,76,6,70,14,78},{16,80,24,88,18,82,26,90,2..., dimensions={0} | all-to-all | bytes 262144 | tf_op jit(solution)/shard_map/all_to_all | solution.py:359
  86.0 0.8 split.1
  (7 shorter events, 0.1 us)
Async XLA Ops:
  1.8 9.5 %collective-permute-start = (bf16[20,16,128]{2,1,0:T(8,128)(2,1)S(1)}, bf16[20,16,128]{2,1,0:T(8,128)(2,1)S(1)}, u32[]{:S(2)}, u32[]{:S(2)}) collective-permute-start(bf16[20,16,128]{2,1,0:T(8,128)(2,1)S(1)} %get-tuple-element.14), channel_id=1, source_target_pairs={{0,8},{2,10},{4,12},{6,14},{8,16},{10,18},{12,20},{14,22},{16,24},... | collective-permute-start | bytes 245768 | tf_op jit(solution)/shard_map/ppermute | solution.py:19
  5.3 7.6 %collective-permute-start.1 = (bf16[20,16,128]{2,1,0:T(8,128)(2,1)S(1)}, bf16[20,16,128]{2,1,0:T(8,128)(2,1)S(1)}, u32[]{:S(2)}, u32[]{:S(2)}) collective-permute-start(bf16[20,16,128]{2,1,0:T(8,128)(2,1)S(1)} %get-tuple-element.14), channel_id=1, source_target_pairs={{8,0},{10,2},{12,4},{14,6},{16,8},{18,10},{20,12},{22,14},{24,16},... | collective-permute-start | bytes 245768 | tf_op jit(solution)/shard_map/ppermute | solution.py:19
  25.4 4.0 %collective-permute-start.2 = (bf16[4,40,16,128]{3,2,1,0:T(8,128)(2,1)S(1)}, bf16[4,40,16,128]{3,2,1,0:T(8,128)(2,1)S(1)}, u32[]{:S(2)}, u32[]{:S(2)}) collective-permute-start(bf16[4,40,16,128]{3,2,1,0:T(8,128)(2,1)S(1)} %all_to_all.20.own), channel_id=1, source_target_pairs={{0,1},{1,0},{2,3},{3,2},{4,5},{5,4},{6,7},{7,6},{8,9},{9,8},{10,11... | collective-permute-start | bytes 1966088 | tf_op jit(solution)/shard_map/ppermute | solution.py:411

commit v5 on v4

--- a/solution.py
+++ b/solution.py
@@ -224,12 +224,15 @@
             if plane == 2:
                 lanes = lax.broadcasted_iota(jnp.int32, (256, 128), 1)
                 kept = jnp.where(lanes % 2 == 0, grad, 0.0).astype(BF16)
-                G2[...] = jnp.zeros(G2.shape, BF16)
-                for h in range(4):
-                    G2[32:96, h * 128 : (h + 1) * 128] = kept[h * 64 : (h + 1) * 64]
+                for b in range(3):
+                    for at in range(4):
+                        h = at + 1 - b
+                        here = jnp.zeros((64, 128), BF16)
+                        if 0 <= h < 4:
+                            here = kept[h * 64 : (h + 1) * 64]
+                        G2[b * 64 : (b + 1) * 64, at * 128 : (at + 1) * 128] = here
 
     back = jnp.dot(t2t[...], GP[...].reshape(2304, 384), preferred_element_type=F32)
-    G1[...] = jnp.zeros(G1.shape, BF16)
     for q, f in enumerate((0, 1, 1, 2)):
         at = place + (f - 1)
         factor = jnp.where((at >= 0) & (at < SLABS), 0.125, 0.0)
@@ -242,9 +245,16 @@
             if q >= 1:
                 HP[q - 1, c, :, 128:] = piece
             if c == 1 and q in (1, 2):
-                for h in range(8):
-                    to = ((q - 1) * 8 + h) * 128
-                    G1[0:32, to : to + 128] = piece[h * 32 : (h + 1) * 32]
+                for b in range(3):
+                    for at in range(8):
+                        h = at + 1 - b
+                        here = jnp.zeros((32, 128), BF16)
+                        if 0 <= h < 8:
+                            here = piece[h * 32 : (h + 1) * 32]
+                        to = (q - 1) * 128 + b * 32
+                        G1[to : to + 32, at * 128 : (at + 1) * 128] = here
+    for q in range(2):
+        G1[q * 128 + 96 : q * 128 + 128] = jnp.zeros((32, 1024), BF16)
 
     out = jnp.dot(t1t[...], HP[...].reshape(2304, 256), preferred_element_type=F32)
     for p in range(2):
@@ -253,33 +263,27 @@
     away = pltpu.make_async_copy(GF, gf, sem)
     away.start()
 
-    nothing = jnp.zeros((16, 128), BF16)
-    for a in range(3):
-        for b in range(3):
-            for c in range(3):
-                tap = (a * 3 + b) * 3 + c
-                to = slice(tap * 16, tap * 16 + 16)
-                for q in range(2):
-                    j = 6 + a + q
-                    m, side = (j, 0) if j <= 8 else (j - 7, 128)
-                    for h in range(8):
-                        at = h + b - 1
-                        lanes = slice((q * 8 + h) * 128, (q * 8 + h + 1) * 128)
-                        if 0 <= at < 8:
-                            FS[to, lanes] = XP[m, c, at * 32 : at * 32 + 16, side : side + 128]
-                        else:
-                            FS[to, lanes] = nothing
-                for h in range(4):
-                    at = h + b - 1
-                    lanes = slice(h * 128, (h + 1) * 128)
-                    if 0 <= at < 4:
-                        FP[to, lanes] = QP[2 + a, c, pl.ds(at * 32 + half, 16), :128]
-                    else:
-                        FP[to, lanes] = nothing
+    for c in range(3):
+        for j in range(4):
+            m, side = (j + 6, 0) if j <= 2 else (2, 128)
+            to = (j * 3 + c) * 16
+            for h in range(8):
+                FS[to : to + 16, h * 128 : (h + 1) * 128] = XP[
+                    m, c, h * 32 : h * 32 + 16, side : side + 128
+                ]
+        for a in range(3):
+            to = (a * 3 + c) * 16
+            for h in range(4):
+                FP[to : to + 16, h * 128 : (h + 1) * 128] = QP[
+                    2 + a, c, pl.ds(h * 32 + half, 16), :128
+                ]
     along = (((1,), (1,)), ((), ()))
-    wg[0:432] = lax.dot_general(
-        FS[...], G1[...], along, preferred_element_type=F32
-    ) + lax.dot_general(FP[...], G2[...], along, preferred_element_type=F32)
+    one = lax.dot_general(FS[...], G1[...], along, preferred_element_type=F32)
+    two = lax.dot_general(FP[...], G2[...], along, preferred_element_type=F32)
+    wg[0:144] = one[0:144, :128] + one[48:192, 128:]
+    wg[144:288] = two[:, :128]
+    wg[288:432, :64] = two[:, 128:]
+    wg[288:432, 64:] = jnp.zeros((144, 64), F32)
     wg[432:] = jnp.zeros((80, 128), F32)
     away.wait()
 
@@ -331,10 +335,10 @@
         ((3, 3, 256, 384), BF16),
         ((3, 3, 256, 256), BF16),
         ((5, 2, 64, 128), BF16),
-        ((432, 2048), BF16),
-        ((432, 512), BF16),
-        ((128, 2048), BF16),
-        ((128, 512), BF16),
+        ((192, 1024), BF16),
+        ((144, 512), BF16),
+        ((256, 1024), BF16),
+        ((192, 512), BF16),
         ((16, 2, 8, 128), BF16),
     ]
     return pl.pallas_call(
@@ -367,9 +371,18 @@
 
 
 def split_kernel(total, one, two):
-    rows = total[...].reshape(512, 128)[:432].astype(F32)
-    one[...] = rows[:, :32]
-    two[...] = rows[:, 32:96]
+    rows = total[...].reshape(512, 128).astype(F32)
+    for a in range(3):
+        for c in range(3):
+            at = (a * 3 + c) * 16
+            first = rows[at : at + 16]
+            second = jnp.concatenate(
+                [rows[144 + at : 160 + at], rows[288 + at : 304 + at]], axis=1
+            )
+            for b in range(3):
+                to = ((a * 3 + b) * 3 + c) * 16
+                one[to : to + 16] = first[:, b * 32 : (b + 1) * 32]
+                two[to : to + 16] = second[:, b * 64 : (b + 1) * 64]
 
 
 def split_total(total):

time: 87.1 us -> 87.1 us (level)
  no operation moved by 1% of the time
where the time goes in v5:
time: 87.1 us; the launch traced here: 86.8 us
  blocking collectives  63 us (72%)
  starting transfers between devices  10.9 us (13%)
  Pallas kernels  9.01 us (10%)
  waiting for transfers between devices  2.79 us (3%)
    all_to_all x3, blocking collectives, exchange(): lax.all_to_all(pieces, DEPTH, 0, 0, axis_index_groups=groups, tiled=True)  50.7 us
    all_to_all x1, blocking collectives, shards(): own = lax.all_to_all(jnp.stack(slots, 0), 'x', 0, 0, tiled=True)  12.3 us
    ppermute x2, starting transfers between devices, depth_shift(): return lax.ppermute(block, DEPTH, pairs)  9 us
    pallas_call x1, Pallas kernels, levels(): pl.pallas_call(main_kernel, in_specs=[vmem] * 6, out_specs=[pl.BlockSpec(...  5.77 us
    ppermute x2, waiting for transfers between devices, depth_shift(): return lax.ppermute(block, DEPTH, pairs)  1.98 us
    ppermute x1, starting transfers between devices, shards(): oth = lax.ppermute(own, 'chan', [(0, 1), (1, 0)])  1.91 us
  transfers between devices with their start and end apart: 3, of which 3 were waited for; matrix products, arithmetic and copies ran while one was open for 0% of the time, Pallas kernels for 1%

profile of v5, /device:TPU:8, one launch (start us, length us, event | category | flops | bytes accessed | tf_op | source)
XLA Modules:
  0.0 86.8 jit_solution(6545778244420996069)
XLA Ops:
  0.6 1.1 %gather.1 = (bf16[20,16,128]{2,1,0:T(8,128)(2,1)S(1)}, bf16[27,32,32]{2,1,0:T(8,128)(2,1)S(1)}, bf16[27,32,64]{2,1,0:T(8,128)(2,1)S(1)}) custom-call(bf16[16,2,8,128]{3,2,1,0:T(8,128)(2,1)} %feats_far.1, bf16[32,1,4,64]{3,2,1,0:T(4,128)(2,1)} %cot_far.1, bf16[27,32,32]{2,1,0:T(8,128)(2,1)} %bitcast.18, bf16[27,32,64]{2,1,0:T(8,128)(2,1)} %bitcast.19), custom_call_target="tpu_custom_call" | custom-call | tf_op jit(solution)/shard_map/gather/pallas_call | solution.py:294
  1.8 3.5 %collective-permute-start = (bf16[20,16,128]{2,1,0:T(8,128)(2,1)S(1)}, bf16[20,16,128]{2,1,0:T(8,128)(2,1)S(1)}, u32[]{:S(2)}, u32[]{:S(2)}) collective-permute-start(bf16[20,16,128]{2,1,0:T(8,128)(2,1)S(1)} %get-tuple-element.14), channel_id=1, source_target_pairs={{0,8},{2,10},{4,12},{6,14},{8,16},{10,18},{12,20},{14,22},{16,24},... | collective-permute-start | bytes 245768 | tf_op jit(solution)/shard_map/ppermute | solution.py:19
  5.3 5.5 %collective-permute-start.1 = (bf16[20,16,128]{2,1,0:T(8,128)(2,1)S(1)}, bf16[20,16,128]{2,1,0:T(8,128)(2,1)S(1)}, u32[]{:S(2)}, u32[]{:S(2)}) collective-permute-start(bf16[20,16,128]{2,1,0:T(8,128)(2,1)S(1)} %get-tuple-element.14), channel_id=1, source_target_pairs={{8,0},{10,2},{12,4},{14,6},{16,8},{18,10},{20,12},{22,14},{24,16},... | collective-permute-start | bytes 245768 | tf_op jit(solution)/shard_map/ppermute | solution.py:19
  10.8 0.4 collective-permute-done
  11.3 1.5 %collective-permute-done.1 = bf16[20,16,128]{2,1,0:T(8,128)(2,1)S(1)} collective-permute-done((bf16[20,16,128]{2,1,0:T(8,128)(2,1)S(1)}, bf16[20,16,128]{2,1,0:T(8,128)(2,1)S(1)}, u32[]{:S(2)}, u32[]{:S(2)}) %collective-permute-start.1) | collective-permute-done | bytes 81952 | tf_op jit(solution)/shard_map/ppermute | solution.py:19
  12.8 0.1 dynamic-slice_bitcast_fusion.3
  13.0 0.1 pad_maximum_fusion
  13.1 12.3 %all_to_all.20.own = bf16[4,40,16,128]{3,2,1,0:T(8,128)(2,1)S(1)} all-to-all(bf16[4,40,16,128]{3,2,1,0:T(8,128)(2,1)S(1)} %pad_maximum_fusion), channel_id=1, replica_groups=mesh['z'=8,'y'=8,'x'=4,'chan'=2] {'x'}, dimensions={0} | all-to-all | bytes 1310720 | tf_op jit(solution)/shard_map/all_to_all | solution.py:423
  25.4 1.9 %collective-permute-start.2 = (bf16[4,40,16,128]{3,2,1,0:T(8,128)(2,1)S(1)}, bf16[4,40,16,128]{3,2,1,0:T(8,128)(2,1)S(1)}, u32[]{:S(2)}, u32[]{:S(2)}) collective-permute-start(bf16[4,40,16,128]{3,2,1,0:T(8,128)(2,1)S(1)} %all_to_all.20.own), channel_id=1, source_target_pairs={{0,1},{1,0},{2,3},{3,2},{4,5},{5,4},{6,7},{7,6},{8,9},{9,8},{10,11... | collective-permute-start | bytes 1966088 | tf_op jit(solution)/shard_map/ppermute | solution.py:424
  27.3 1.2 %bands.1 = (bf16[256,2304]{1,0:T(8,128)(2,1)S(1)}, bf16[128,2304]{1,0:T(8,128)(2,1)S(1)}, bf16[256,1152]{1,0:T(8,128)(2,1)S(1)}, bf16[128,2304]{1,0:T(8,128)(2,1)S(1)}) custom-call(bf16[27,32,32]{2,1,0:T(8,128)(2,1)S(1)} %get-tuple-element.15.w1, bf16[27,32,64]{2,1,0:T(8,128)(2,1)S(1)} %get-tuple-element.16.w2), custom_call_target="tpu_custom_call" | custom-call | flops 1000000000 | bytes 4000000 | tf_op jit(solution)/shard_map/bands/pallas_call | solution.py:316
  28.6 0.8 collective-permute-done.2.oth
  29.4 5.8 %levels.1 = (bf16[16,2,8,128]{3,2,1,0:T(8,128)(2,1)}, f32[512,128]{1,0:T(8,128)S(1)}) custom-call(bf16[4,40,16,128]{3,2,1,0:T(8,128)(2,1)S(1)} %all_to_all.20.own, bf16[4,40,16,128]{3,2,1,0:T(8,128)(2,1)S(1)} %collective-permute-done.2.oth, bf16[256,2304]{1,0:T(8,128)(2,1)S(1)} %get-tuple-element.17.t1, bf16[128,2304]{1,0:T(8,128)(2,1)S(1)} %get-tuple-element.18.t1t, ...), custom_call_target="tpu_custom_call" | custom-call | flops 10000000000 | bytes 8000000 | tf_op jit(solution)/shard_map/levels/pallas_call | solution.py:344
  35.1 12.6 %all_to_all.21 = f32[16,32,128]{2,1,0:T(8,128)S(1)} all-to-all(f32[16,32,128]{2,1,0:T(8,128)S(1)} %bitcast.17), channel_id=1, replica_groups={{0,64,8,72,2,66,10,74,4,68,12,76,6,70,14,78},{16,80,24,88,18,82,26,90,2..., dimensions={0} | all-to-all | bytes 524288 | tf_op jit(solution)/shard_map/all_to_all | solution.py:363
  47.8 24.7 %all_to_all.22 = f32[16,32,128]{2,1,0:T(8,128)S(1)} all-to-all(f32[16,32,128]{2,1,0:T(8,128)S(1)} %broadcast_in_dim.6), channel_id=1, replica_groups={{0,16,40,56,128,144,168,184,320,336,360,376,448,464,488,504},{64,80,104..., dimensions={0} | all-to-all | bytes 524288 | tf_op jit(solution)/shard_map/all_to_all | solution.py:363
  72.5 13.5 %all_to_all.23.total = bf16[16,32,128]{2,1,0:T(8,128)(2,1)S(1)} all-to-all(bf16[16,32,128]{2,1,0:T(8,128)(2,1)S(1)} %broadcast_in_dim.7), channel_id=1, replica_groups={{0,64,8,72,2,66,10,74,4,68,12,76,6,70,14,78},{16,80,24,88,18,82,26,90,2..., dimensions={0} | all-to-all | bytes 262144 | tf_op jit(solution)/shard_map/all_to_all | solution.py:363
  86.0 0.9 split.1
  (7 shorter events, 0.1 us)
Async XLA Ops:
  1.8 9.5 %collective-permute-start = (bf16[20,16,128]{2,1,0:T(8,128)(2,1)S(1)}, bf16[20,16,128]{2,1,0:T(8,128)(2,1)S(1)}, u32[]{:S(2)}, u32[]{:S(2)}) collective-permute-start(bf16[20,16,128]{2,1,0:T(8,128)(2,1)S(1)} %get-tuple-element.14), channel_id=1, source_target_pairs={{0,8},{2,10},{4,12},{6,14},{8,16},{10,18},{12,20},{14,22},{16,24},... | collective-permute-start | bytes 245768 | tf_op jit(solution)/shard_map/ppermute | solution.py:19
  5.3 7.6 %collective-permute-start.1 = (bf16[20,16,128]{2,1,0:T(8,128)(2,1)S(1)}, bf16[20,16,128]{2,1,0:T(8,128)(2,1)S(1)}, u32[]{:S(2)}, u32[]{:S(2)}) collective-permute-start(bf16[20,16,128]{2,1,0:T(8,128)(2,1)S(1)} %get-tuple-element.14), channel_id=1, source_target_pairs={{8,0},{10,2},{12,4},{14,6},{16,8},{18,10},{20,12},{22,14},{24,16},... | collective-permute-start | bytes 245768 | tf_op jit(solution)/shard_map/ppermute | solution.py:19
  25.4 4.0 %collective-permute-start.2 = (bf16[4,40,16,128]{3,2,1,0:T(8,128)(2,1)S(1)}, bf16[4,40,16,128]{3,2,1,0:T(8,128)(2,1)S(1)}, u32[]{:S(2)}, u32[]{:S(2)}) collective-permute-start(bf16[4,40,16,128]{3,2,1,0:T(8,128)(2,1)S(1)} %all_to_all.20.own), channel_id=1, source_target_pairs={{0,1},{1,0},{2,3},{3,2},{4,5},{5,4},{6,7},{7,6},{8,9},{9,8},{10,11... | collective-permute-start | bytes 1966088 | tf_op jit(solution)/shard_map/ppermute | solution.py:424

commit v6 on v5

--- a/solution.py
+++ b/solution.py
@@ -126,7 +126,7 @@
 
 
 def main_kernel(
-    own, oth, t1, t1t, t2, t2t, gf, wg, XP, PS, SL, QP, GP, HP, CT, FS, FP, G1, G2, GF, sem
+    own, oth, t1, t1t, t2, t2t, gf, wg, XP, PS, SL, QP, GP, HP, CT, FS, FP, G1, G2
 ):
     member, place = position()
     x = lax.rem(place, 4)
@@ -251,17 +251,15 @@
                         here = jnp.zeros((32, 128), BF16)
                         if 0 <= h < 8:
                             here = piece[h * 32 : (h + 1) * 32]
-                        to = (q - 1) * 128 + b * 32
+                        to = (q - 1) * 128 + (64, 96, 0)[b]
                         G1[to : to + 32, at * 128 : (at + 1) * 128] = here
     for q in range(2):
-        G1[q * 128 + 96 : q * 128 + 128] = jnp.zeros((32, 1024), BF16)
+        G1[q * 128 + 32 : q * 128 + 64] = jnp.zeros((32, 1024), BF16)
 
     out = jnp.dot(t1t[...], HP[...].reshape(2304, 256), preferred_element_type=F32)
     for p in range(2):
         side = out[:, p * 128 : (p + 1) * 128].reshape(8, 16, 128)
-        GF[:, p] = jnp.transpose(side, (1, 0, 2)).astype(BF16)
-    away = pltpu.make_async_copy(GF, gf, sem)
-    away.start()
+        gf[:, p] = jnp.transpose(side, (1, 0, 2)).astype(BF16)
 
     for c in range(3):
         for j in range(4):
@@ -280,12 +278,12 @@
     along = (((1,), (1,)), ((), ()))
     one = lax.dot_general(FS[...], G1[...], along, preferred_element_type=F32)
     two = lax.dot_general(FP[...], G2[...], along, preferred_element_type=F32)
-    wg[0:144] = one[0:144, :128] + one[48:192, 128:]
+    one = one[0:144, :128] + one[48:192, 128:]
+    wg[0:144] = jnp.concatenate([two[:, 128:], one[:, 64:]], axis=1)
     wg[144:288] = two[:, :128]
-    wg[288:432, :64] = two[:, 128:]
-    wg[288:432, 64:] = jnp.zeros((144, 64), F32)
-    wg[432:] = jnp.zeros((80, 128), F32)
-    away.wait()
+    thirds = [one[at : at + 48, :32] for at in (0, 48, 96)]
+    wg[288:336] = jnp.concatenate(thirds + [jnp.zeros((48, 32), F32)], axis=1)
+    wg[336:] = jnp.zeros((48, 128), F32)
 
 
 def own_block(feats, cot, w1, w2):
@@ -339,18 +337,16 @@
         ((144, 512), BF16),
         ((256, 1024), BF16),
         ((192, 512), BF16),
-        ((16, 2, 8, 128), BF16),
     ]
     return pl.pallas_call(
         main_kernel,
         in_specs=[vmem] * 6,
-        out_specs=[pl.BlockSpec(memory_space=pl.ANY), vmem],
+        out_specs=[vmem, vmem],
         out_shape=[
             jax.ShapeDtypeStruct((16, 2, 8, 128), BF16),
-            jax.ShapeDtypeStruct((512, 128), F32),
+            jax.ShapeDtypeStruct((384, 128), F32),
         ],
-        scratch_shapes=[pltpu.VMEM(shape, dtype) for shape, dtype in scratch]
-        + [pltpu.SemaphoreType.DMA(())],
+        scratch_shapes=[pltpu.VMEM(shape, dtype) for shape, dtype in scratch],
         cost_estimate=pl.CostEstimate(
             flops=10**10, bytes_accessed=8 * 10**6, transcendentals=10**6
         ),
@@ -364,40 +360,46 @@
 
 
 def total_over_depth(part):
-    near = jnp.sum(exchange(part.reshape(16, 32, 128), NEAR), axis=0)
-    whole = jnp.sum(exchange(jnp.broadcast_to(near, (16, 32, 128)), FAR), axis=0)
-    copies = jnp.broadcast_to(whole.astype(BF16), (16, 32, 128))
+    near = jnp.sum(exchange(part.reshape(16, 24, 128), NEAR), axis=0)
+    whole = jnp.sum(exchange(jnp.broadcast_to(near, (16, 24, 128)), FAR), axis=0)
+    copies = jnp.broadcast_to(whole.astype(BF16), (16, 24, 128))
     return exchange(copies, NEAR)
 
 
-def split_kernel(total, one, two):
-    rows = total[...].reshape(512, 128).astype(F32)
+def split_kernel(total, gf, one, two, gf_out, sem):
+    away = pltpu.make_async_copy(gf, gf_out, sem)
+    away.start()
+    rows = total[...].reshape(384, 128).astype(F32)
     for a in range(3):
         for c in range(3):
             at = (a * 3 + c) * 16
-            first = rows[at : at + 16]
-            second = jnp.concatenate(
-                [rows[144 + at : 160 + at], rows[288 + at : 304 + at]], axis=1
-            )
+            first, second = rows[at : at + 16], rows[144 + at : 160 + at]
+            rest = rows[288 + at % 48 : 304 + at % 48]
+            third = at // 48 * 32
+            ones = (first[:, 64:96], first[:, 96:], rest[:, third : third + 32])
+            twos = (second[:, :64], second[:, 64:], first[:, :64])
             for b in range(3):
                 to = ((a * 3 + b) * 3 + c) * 16
-                one[to : to + 16] = first[:, b * 32 : (b + 1) * 32]
-                two[to : to + 16] = second[:, b * 64 : (b + 1) * 64]
-
-
-def split_total(total):
+                one[to : to + 16] = ones[b]
+                two[to : to + 16] = twos[b]
+    away.wait()
+
+
+def split_total(total, gf):
     vmem = pl.BlockSpec(memory_space=pltpu.VMEM)
     return pl.pallas_call(
         split_kernel,
-        in_specs=[vmem],
-        out_specs=[vmem, vmem],
+        in_specs=[vmem, vmem],
+        out_specs=[vmem, vmem, pl.BlockSpec(memory_space=pl.ANY)],
         out_shape=[
             jax.ShapeDtypeStruct((432, 32), F32),
             jax.ShapeDtypeStruct((432, 64), F32),
+            jax.ShapeDtypeStruct(gf.shape, BF16),
         ],
+        scratch_shapes=[pltpu.SemaphoreType.DMA(())],
         compiler_params=pltpu.CompilerParams(vmem_limit_bytes=4 * 2**20),
         name="split",
-    )(total)
+    )(total, gf)
 
 
 def shards(feats, weight_one, weight_two, cotangent):
@@ -423,7 +425,7 @@
     own = lax.all_to_all(jnp.stack(slots, 0), "x", 0, 0, tiled=True)
     oth = lax.ppermute(own, "chan", [(0, 1), (1, 0)])
     grad_feats, part = levels(own, oth, bands)
-    one, two = split_total(total_over_depth(part))
+    one, two, grad_feats = split_total(total_over_depth(part), grad_feats)
     grad_weight_one = jnp.transpose(one.reshape(27, 16, 32), (2, 1, 0))
     grad_weight_two = jnp.transpose(two.reshape(27, 16, 64), (2, 1, 0))
     return (grad_feats, grad_weight_one, grad_weight_two)

time: 87.1 us -> 84.8 us (0.974)
  blocking collectives: 63 us -> 60.9 us
    all_to_all x3, blocking collectives: 50.7 us -> 48.5 us  [exchange(): lax.all_to_all(pieces, DEPTH, 0, 0, axis_index_groups=groups, tiled=True)]
where the time goes in v6:
time: 84.8 us; the launch traced here: 84.5 us
  blocking collectives  60.9 us (72%)
  starting transfers between devices  10.9 us (13%)
  Pallas kernels  8.9 us (10%)
  waiting for transfers between devices  2.79 us (3%)
    all_to_all x3, blocking collectives, exchange(): lax.all_to_all(pieces, DEPTH, 0, 0, axis_index_groups=groups, tiled=True)  48.5 us
    all_to_all x1, blocking collectives, shards(): own = lax.all_to_all(jnp.stack(slots, 0), 'x', 0, 0, tiled=True)  12.3 us
    ppermute x2, starting transfers between devices, depth_shift(): return lax.ppermute(block, DEPTH, pairs)  9 us
    pallas_call x1, Pallas kernels, levels(): pl.pallas_call(main_kernel, in_specs=[vmem] * 6, out_specs=[vmem, vmem],...  5.12 us
    ppermute x2, waiting for transfers between devices, depth_shift(): return lax.ppermute(block, DEPTH, pairs)  1.98 us
    ppermute x1, starting transfers between devices, shards(): oth = lax.ppermute(own, 'chan', [(0, 1), (1, 0)])  1.91 us
  transfers between devices with their start and end apart: 3, of which 3 were waited for; matrix products, arithmetic and copies ran while one was open for 0% of the time, Pallas kernels for 1%

profile of v6, /device:TPU:8, one launch (start us, length us, event | category | flops | bytes accessed | tf_op | source)
XLA Modules:
  0.0 84.5 jit_solution(1650896574196510971)
XLA Ops:
  0.6 1.1 %gather.1 = (bf16[20,16,128]{2,1,0:T(8,128)(2,1)S(1)}, bf16[27,32,32]{2,1,0:T(8,128)(2,1)S(1)}, bf16[27,32,64]{2,1,0:T(8,128)(2,1)S(1)}) custom-call(bf16[16,2,8,128]{3,2,1,0:T(8,128)(2,1)} %feats_far.1, bf16[32,1,4,64]{3,2,1,0:T(4,128)(2,1)} %cot_far.1, bf16[27,32,32]{2,1,0:T(8,128)(2,1)} %bitcast.18, bf16[27,32,64]{2,1,0:T(8,128)(2,1)} %bitcast.19), custom_call_target="tpu_custom_call" | custom-call | tf_op jit(solution)/shard_map/gather/pallas_call | solution.py:292
  1.8 3.5 %collective-permute-start = (bf16[20,16,128]{2,1,0:T(8,128)(2,1)S(1)}, bf16[20,16,128]{2,1,0:T(8,128)(2,1)S(1)}, u32[]{:S(2)}, u32[]{:S(2)}) collective-permute-start(bf16[20,16,128]{2,1,0:T(8,128)(2,1)S(1)} %get-tuple-element.15), channel_id=1, source_target_pairs={{0,8},{2,10},{4,12},{6,14},{8,16},{10,18},{12,20},{14,22},{16,24},... | collective-permute-start | bytes 245768 | tf_op jit(solution)/shard_map/ppermute | solution.py:19
  5.3 5.5 %collective-permute-start.1 = (bf16[20,16,128]{2,1,0:T(8,128)(2,1)S(1)}, bf16[20,16,128]{2,1,0:T(8,128)(2,1)S(1)}, u32[]{:S(2)}, u32[]{:S(2)}) collective-permute-start(bf16[20,16,128]{2,1,0:T(8,128)(2,1)S(1)} %get-tuple-element.15), channel_id=1, source_target_pairs={{8,0},{10,2},{12,4},{14,6},{16,8},{18,10},{20,12},{22,14},{24,16},... | collective-permute-start | bytes 245768 | tf_op jit(solution)/shard_map/ppermute | solution.py:19
  10.8 0.4 collective-permute-done
  11.3 1.5 %collective-permute-done.1 = bf16[20,16,128]{2,1,0:T(8,128)(2,1)S(1)} collective-permute-done((bf16[20,16,128]{2,1,0:T(8,128)(2,1)S(1)}, bf16[20,16,128]{2,1,0:T(8,128)(2,1)S(1)}, u32[]{:S(2)}, u32[]{:S(2)}) %collective-permute-start.1) | collective-permute-done | bytes 81952 | tf_op jit(solution)/shard_map/ppermute | solution.py:19
  12.8 0.1 dynamic-slice_bitcast_fusion.3
  13.0 0.1 pad_maximum_fusion
  13.1 12.3 %all_to_all.20.own = bf16[4,40,16,128]{3,2,1,0:T(8,128)(2,1)S(1)} all-to-all(bf16[4,40,16,128]{3,2,1,0:T(8,128)(2,1)S(1)} %pad_maximum_fusion), channel_id=1, replica_groups=mesh['z'=8,'y'=8,'x'=4,'chan'=2] {'x'}, dimensions={0} | all-to-all | bytes 1310720 | tf_op jit(solution)/shard_map/all_to_all | solution.py:425
  25.4 1.9 %collective-permute-start.2 = (bf16[4,40,16,128]{3,2,1,0:T(8,128)(2,1)S(1)}, bf16[4,40,16,128]{3,2,1,0:T(8,128)(2,1)S(1)}, u32[]{:S(2)}, u32[]{:S(2)}) collective-permute-start(bf16[4,40,16,128]{3,2,1,0:T(8,128)(2,1)S(1)} %all_to_all.20.own), channel_id=1, source_target_pairs={{0,1},{1,0},{2,3},{3,2},{4,5},{5,4},{6,7},{7,6},{8,9},{9,8},{10,11... | collective-permute-start | bytes 1966088 | tf_op jit(solution)/shard_map/ppermute | solution.py:426
  27.3 1.2 %bands.1 = (bf16[256,2304]{1,0:T(8,128)(2,1)S(1)}, bf16[128,2304]{1,0:T(8,128)(2,1)S(1)}, bf16[256,1152]{1,0:T(8,128)(2,1)S(1)}, bf16[128,2304]{1,0:T(8,128)(2,1)S(1)}) custom-call(bf16[27,32,32]{2,1,0:T(8,128)(2,1)S(1)} %get-tuple-element.16.w1, bf16[27,32,64]{2,1,0:T(8,128)(2,1)S(1)} %get-tuple-element.17.w2), custom_call_target="tpu_custom_call" | custom-call | flops 1000000000 | bytes 4000000 | tf_op jit(solution)/shard_map/bands/pallas_call | solution.py:314
  28.6 0.8 collective-permute-done.2.oth
  29.4 5.1 %levels.1 = (bf16[16,2,8,128]{3,2,1,0:T(8,128)(2,1)S(1)}, f32[384,128]{1,0:T(8,128)S(1)}) custom-call(bf16[4,40,16,128]{3,2,1,0:T(8,128)(2,1)S(1)} %all_to_all.20.own, bf16[4,40,16,128]{3,2,1,0:T(8,128)(2,1)S(1)} %collective-permute-done.2.oth, bf16[256,2304]{1,0:T(8,128)(2,1)S(1)} %get-tuple-element.18.t1, bf16[128,2304]{1,0:T(8,128)(2,1)S(1)} %get-tuple-element.19.t1t, ...), custom_call_target="tpu_custom_call" | custom-call | flops 10000000000 | bytes 8000000 | tf_op jit(solution)/shard_map/levels/pallas_call | solution.py:341
  34.5 12.0 %all_to_all.21 = f32[16,24,128]{2,1,0:T(8,128)S(1)} all-to-all(f32[16,24,128]{2,1,0:T(8,128)S(1)} %bitcast.17), channel_id=1, replica_groups={{0,64,8,72,2,66,10,74,4,68,12,76,6,70,14,78},{16,80,24,88,18,82,26,90,2..., dimensions={0} | all-to-all | bytes 393216 | tf_op jit(solution)/shard_map/all_to_all | solution.py:359
  46.6 24.0 %all_to_all.22 = f32[16,24,128]{2,1,0:T(8,128)S(1)} all-to-all(f32[16,24,128]{2,1,0:T(8,128)S(1)} %broadcast_in_dim.6), channel_id=1, replica_groups={{0,16,40,56,128,144,168,184,320,336,360,376,448,464,488,504},{64,80,104..., dimensions={0} | all-to-all | bytes 393216 | tf_op jit(solution)/shard_map/all_to_all | solution.py:359
  70.6 12.5 %all_to_all.23.total = bf16[16,24,128]{2,1,0:T(8,128)(2,1)S(1)} all-to-all(bf16[16,24,128]{2,1,0:T(8,128)(2,1)S(1)} %broadcast_in_dim.7), channel_id=1, replica_groups={{0,64,8,72,2,66,10,74,4,68,12,76,6,70,14,78},{16,80,24,88,18,82,26,90,2..., dimensions={0} | all-to-all | bytes 196608 | tf_op jit(solution)/shard_map/all_to_all | solution.py:359
  83.1 1.4 %split.1 = (f32[432,32]{1,0:T(8,128)}, f32[432,64]{1,0:T(8,128)}, bf16[16,2,8,128]{3,2,1,0:T(8,128)(2,1)}) custom-call(bf16[16,24,128]{2,1,0:T(8,128)(2,1)S(1)} %all_to_all.23.total, bf16[16,2,8,128]{3,2,1,0:T(8,128)(2,1)S(1)} %get-tuple-element.23.gf), custom_call_target="tpu_custom_call" | custom-call | tf_op jit(solution)/shard_map/split/pallas_call | solution.py:390
  (7 shorter events, 0.1 us)
Async XLA Ops:
  1.8 9.5 %collective-permute-start = (bf16[20,16,128]{2,1,0:T(8,128)(2,1)S(1)}, bf16[20,16,128]{2,1,0:T(8,128)(2,1)S(1)}, u32[]{:S(2)}, u32[]{:S(2)}) collective-permute-start(bf16[20,16,128]{2,1,0:T(8,128)(2,1)S(1)} %get-tuple-element.15), channel_id=1, source_target_pairs={{0,8},{2,10},{4,12},{6,14},{8,16},{10,18},{12,20},{14,22},{16,24},... | collective-permute-start | bytes 245768 | tf_op jit(solution)/shard_map/ppermute | solution.py:19
  5.3 7.6 %collective-permute-start.1 = (bf16[20,16,128]{2,1,0:T(8,128)(2,1)S(1)}, bf16[20,16,128]{2,1,0:T(8,128)(2,1)S(1)}, u32[]{:S(2)}, u32[]{:S(2)}) collective-permute-start(bf16[20,16,128]{2,1,0:T(8,128)(2,1)S(1)} %get-tuple-element.15), channel_id=1, source_target_pairs={{8,0},{10,2},{12,4},{14,6},{16,8},{18,10},{20,12},{22,14},{24,16},... | collective-permute-start | bytes 245768 | tf_op jit(solution)/shard_map/ppermute | solution.py:19
  25.4 4.0 %collective-permute-start.2 = (bf16[4,40,16,128]{3,2,1,0:T(8,128)(2,1)S(1)}, bf16[4,40,16,128]{3,2,1,0:T(8,128)(2,1)S(1)}, u32[]{:S(2)}, u32[]{:S(2)}) collective-permute-start(bf16[4,40,16,128]{3,2,1,0:T(8,128)(2,1)S(1)} %all_to_all.20.own), channel_id=1, source_target_pairs={{0,1},{1,0},{2,3},{3,2},{4,5},{5,4},{6,7},{7,6},{8,9},{9,8},{10,11... | collective-permute-start | bytes 1966088 | tf_op jit(solution)/shard_map/ppermute | solution.py:426

commit v7 on v6

--- a/solution.py
+++ b/solution.py
@@ -366,37 +366,49 @@
     return exchange(copies, NEAR)
 
 
-def split_kernel(total, gf, one, two, gf_out, sem):
-    away = pltpu.make_async_copy(gf, gf_out, sem)
-    away.start()
+def split_kernel(total, gf, one_out, two_out, gf_out, one, two, sems):
+    pairs = ((gf, gf_out), (one, one_out), (two, two_out))
+    away = [
+        pltpu.make_async_copy(source, target, sems.at[index])
+        for index, (source, target) in enumerate(pairs)
+    ]
+    away[0].start()
     rows = total[...].reshape(384, 128).astype(F32)
     for a in range(3):
         for c in range(3):
             at = (a * 3 + c) * 16
-            first, second = rows[at : at + 16], rows[144 + at : 160 + at]
+            first = rows[at : at + 16]
             rest = rows[288 + at % 48 : 304 + at % 48]
             third = at // 48 * 32
             ones = (first[:, 64:96], first[:, 96:], rest[:, third : third + 32])
+            for b in range(3):
+                to = ((a * 3 + b) * 3 + c) * 16
+                one[to : to + 16] = ones[b]
+    away[1].start()
+    for a in range(3):
+        for c in range(3):
+            at = (a * 3 + c) * 16
+            first, second = rows[at : at + 16], rows[144 + at : 160 + at]
             twos = (second[:, :64], second[:, 64:], first[:, :64])
             for b in range(3):
                 to = ((a * 3 + b) * 3 + c) * 16
-                one[to : to + 16] = ones[b]
                 two[to : to + 16] = twos[b]
-    away.wait()
+    away[2].start()
+    for copy in away:
+        copy.wait()
 
 
 def split_total(total, gf):
     vmem = pl.BlockSpec(memory_space=pltpu.VMEM)
+    shapes = [(432, 32), (432, 64)]
     return pl.pallas_call(
         split_kernel,
         in_specs=[vmem, vmem],
-        out_specs=[vmem, vmem, pl.BlockSpec(memory_space=pl.ANY)],
-        out_shape=[
-            jax.ShapeDtypeStruct((432, 32), F32),
-            jax.ShapeDtypeStruct((432, 64), F32),
-            jax.ShapeDtypeStruct(gf.shape, BF16),
-        ],
-        scratch_shapes=[pltpu.SemaphoreType.DMA(())],
+        out_specs=[pl.BlockSpec(memory_space=pl.ANY)] * 3,
+        out_shape=[jax.ShapeDtypeStruct(shape, F32) for shape in shapes]
+        + [jax.ShapeDtypeStruct(gf.shape, BF16)],
+        scratch_shapes=[pltpu.VMEM(shape, F32) for shape in shapes]
+        + [pltpu.SemaphoreType.DMA((3,))],
         compiler_params=pltpu.CompilerParams(vmem_limit_bytes=4 * 2**20),
         name="split",
     )(total, gf)

time: 84.8 us -> 84.3 us (level)
  no operation moved by 1% of the time
where the time goes in v7:
time: 84.3 us; the launch traced here: 84 us
  blocking collectives  60.9 us (72%)
  starting transfers between devices  10.9 us (13%)
  Pallas kernels  8.38 us (10%)
  waiting for transfers between devices  2.79 us (3%)
    all_to_all x3, blocking collectives, exchange(): lax.all_to_all(pieces, DEPTH, 0, 0, axis_index_groups=groups, tiled=True)  48.5 us
    all_to_all x1, blocking collectives, shards(): own = lax.all_to_all(jnp.stack(slots, 0), 'x', 0, 0, tiled=True)  12.3 us
    ppermute x2, starting transfers between devices, depth_shift(): return lax.ppermute(block, DEPTH, pairs)  9 us
    pallas_call x1, Pallas kernels, levels(): pl.pallas_call(main_kernel, in_specs=[vmem] * 6, out_specs=[vmem, vmem],...  5.12 us
    ppermute x2, waiting for transfers between devices, depth_shift(): return lax.ppermute(block, DEPTH, pairs)  1.98 us
    ppermute x1, starting transfers between devices, shards(): oth = lax.ppermute(own, 'chan', [(0, 1), (1, 0)])  1.91 us
  transfers between devices with their start and end apart: 3, of which 3 were waited for; matrix products, arithmetic and copies ran while one was open for 0% of the time, Pallas kernels for 1%

profile of v7, /device:TPU:8, one launch (start us, length us, event | category | flops | bytes accessed | tf_op | source)
XLA Modules:
  0.0 84.0 jit_solution(11568046655714618305)
XLA Ops:
  0.6 1.1 %gather.1 = (bf16[20,16,128]{2,1,0:T(8,128)(2,1)S(1)}, bf16[27,32,32]{2,1,0:T(8,128)(2,1)S(1)}, bf16[27,32,64]{2,1,0:T(8,128)(2,1)S(1)}) custom-call(bf16[16,2,8,128]{3,2,1,0:T(8,128)(2,1)} %feats_far.1, bf16[32,1,4,64]{3,2,1,0:T(4,128)(2,1)} %cot_far.1, bf16[27,32,32]{2,1,0:T(8,128)(2,1)} %bitcast.18, bf16[27,32,64]{2,1,0:T(8,128)(2,1)} %bitcast.19), custom_call_target="tpu_custom_call" | custom-call | tf_op jit(solution)/shard_map/gather/pallas_call | solution.py:292
  1.8 3.5 %collective-permute-start = (bf16[20,16,128]{2,1,0:T(8,128)(2,1)S(1)}, bf16[20,16,128]{2,1,0:T(8,128)(2,1)S(1)}, u32[]{:S(2)}, u32[]{:S(2)}) collective-permute-start(bf16[20,16,128]{2,1,0:T(8,128)(2,1)S(1)} %get-tuple-element.15), channel_id=1, source_target_pairs={{0,8},{2,10},{4,12},{6,14},{8,16},{10,18},{12,20},{14,22},{16,24},... | collective-permute-start | bytes 245768 | tf_op jit(solution)/shard_map/ppermute | solution.py:19
  5.3 5.5 %collective-permute-start.1 = (bf16[20,16,128]{2,1,0:T(8,128)(2,1)S(1)}, bf16[20,16,128]{2,1,0:T(8,128)(2,1)S(1)}, u32[]{:S(2)}, u32[]{:S(2)}) collective-permute-start(bf16[20,16,128]{2,1,0:T(8,128)(2,1)S(1)} %get-tuple-element.15), channel_id=1, source_target_pairs={{8,0},{10,2},{12,4},{14,6},{16,8},{18,10},{20,12},{22,14},{24,16},... | collective-permute-start | bytes 245768 | tf_op jit(solution)/shard_map/ppermute | solution.py:19
  10.8 0.4 collective-permute-done
  11.3 1.5 %collective-permute-done.1 = bf16[20,16,128]{2,1,0:T(8,128)(2,1)S(1)} collective-permute-done((bf16[20,16,128]{2,1,0:T(8,128)(2,1)S(1)}, bf16[20,16,128]{2,1,0:T(8,128)(2,1)S(1)}, u32[]{:S(2)}, u32[]{:S(2)}) %collective-permute-start.1) | collective-permute-done | bytes 81952 | tf_op jit(solution)/shard_map/ppermute | solution.py:19
  12.8 0.1 dynamic-slice_bitcast_fusion.3
  13.0 0.1 pad_maximum_fusion
  13.1 12.3 %all_to_all.20.own = bf16[4,40,16,128]{3,2,1,0:T(8,128)(2,1)S(1)} all-to-all(bf16[4,40,16,128]{3,2,1,0:T(8,128)(2,1)S(1)} %pad_maximum_fusion), channel_id=1, replica_groups=mesh['z'=8,'y'=8,'x'=4,'chan'=2] {'x'}, dimensions={0} | all-to-all | bytes 1310720 | tf_op jit(solution)/shard_map/all_to_all | solution.py:437
  25.4 1.9 %collective-permute-start.2 = (bf16[4,40,16,128]{3,2,1,0:T(8,128)(2,1)S(1)}, bf16[4,40,16,128]{3,2,1,0:T(8,128)(2,1)S(1)}, u32[]{:S(2)}, u32[]{:S(2)}) collective-permute-start(bf16[4,40,16,128]{3,2,1,0:T(8,128)(2,1)S(1)} %all_to_all.20.own), channel_id=1, source_target_pairs={{0,1},{1,0},{2,3},{3,2},{4,5},{5,4},{6,7},{7,6},{8,9},{9,8},{10,11... | collective-permute-start | bytes 1966088 | tf_op jit(solution)/shard_map/ppermute | solution.py:438
  27.3 1.2 %bands.1 = (bf16[256,2304]{1,0:T(8,128)(2,1)S(1)}, bf16[128,2304]{1,0:T(8,128)(2,1)S(1)}, bf16[256,1152]{1,0:T(8,128)(2,1)S(1)}, bf16[128,2304]{1,0:T(8,128)(2,1)S(1)}) custom-call(bf16[27,32,32]{2,1,0:T(8,128)(2,1)S(1)} %get-tuple-element.16.w1, bf16[27,32,64]{2,1,0:T(8,128)(2,1)S(1)} %get-tuple-element.17.w2), custom_call_target="tpu_custom_call" | custom-call | flops 1000000000 | bytes 4000000 | tf_op jit(solution)/shard_map/bands/pallas_call | solution.py:314
  28.6 0.8 collective-permute-done.2.oth
  29.4 5.1 %levels.1 = (bf16[16,2,8,128]{3,2,1,0:T(8,128)(2,1)S(1)}, f32[384,128]{1,0:T(8,128)S(1)}) custom-call(bf16[4,40,16,128]{3,2,1,0:T(8,128)(2,1)S(1)} %all_to_all.20.own, bf16[4,40,16,128]{3,2,1,0:T(8,128)(2,1)S(1)} %collective-permute-done.2.oth, bf16[256,2304]{1,0:T(8,128)(2,1)S(1)} %get-tuple-element.18.t1, bf16[128,2304]{1,0:T(8,128)(2,1)S(1)} %get-tuple-element.19.t1t, ...), custom_call_target="tpu_custom_call" | custom-call | flops 10000000000 | bytes 8000000 | tf_op jit(solution)/shard_map/levels/pallas_call | solution.py:341
  34.5 12.0 %all_to_all.21 = f32[16,24,128]{2,1,0:T(8,128)S(1)} all-to-all(f32[16,24,128]{2,1,0:T(8,128)S(1)} %bitcast.17), channel_id=1, replica_groups={{0,64,8,72,2,66,10,74,4,68,12,76,6,70,14,78},{16,80,24,88,18,82,26,90,2..., dimensions={0} | all-to-all | bytes 393216 | tf_op jit(solution)/shard_map/all_to_all | solution.py:359
  46.6 24.0 %all_to_all.22 = f32[16,24,128]{2,1,0:T(8,128)S(1)} all-to-all(f32[16,24,128]{2,1,0:T(8,128)S(1)} %broadcast_in_dim.6), channel_id=1, replica_groups={{0,16,40,56,128,144,168,184,320,336,360,376,448,464,488,504},{64,80,104..., dimensions={0} | all-to-all | bytes 393216 | tf_op jit(solution)/shard_map/all_to_all | solution.py:359
  70.6 12.5 %all_to_all.23.total = bf16[16,24,128]{2,1,0:T(8,128)(2,1)S(1)} all-to-all(bf16[16,24,128]{2,1,0:T(8,128)(2,1)S(1)} %broadcast_in_dim.7), channel_id=1, replica_groups={{0,64,8,72,2,66,10,74,4,68,12,76,6,70,14,78},{16,80,24,88,18,82,26,90,2..., dimensions={0} | all-to-all | bytes 196608 | tf_op jit(solution)/shard_map/all_to_all | solution.py:359
  83.1 0.9 %split.1 = (f32[432,32]{1,0:T(8,128)}, f32[432,64]{1,0:T(8,128)}, bf16[16,2,8,128]{3,2,1,0:T(8,128)(2,1)}) custom-call(bf16[16,24,128]{2,1,0:T(8,128)(2,1)S(1)} %all_to_all.23.total, bf16[16,2,8,128]{3,2,1,0:T(8,128)(2,1)S(1)} %get-tuple-element.23.gf), custom_call_target="tpu_custom_call" | custom-call | tf_op jit(solution)/shard_map/split/pallas_call | solution.py:404
  (7 shorter events, 0.1 us)
Async XLA Ops:
  1.8 9.5 %collective-permute-start = (bf16[20,16,128]{2,1,0:T(8,128)(2,1)S(1)}, bf16[20,16,128]{2,1,0:T(8,128)(2,1)S(1)}, u32[]{:S(2)}, u32[]{:S(2)}) collective-permute-start(bf16[20,16,128]{2,1,0:T(8,128)(2,1)S(1)} %get-tuple-element.15), channel_id=1, source_target_pairs={{0,8},{2,10},{4,12},{6,14},{8,16},{10,18},{12,20},{14,22},{16,24},... | collective-permute-start | bytes 245768 | tf_op jit(solution)/shard_map/ppermute | solution.py:19
  5.3 7.6 %collective-permute-start.1 = (bf16[20,16,128]{2,1,0:T(8,128)(2,1)S(1)}, bf16[20,16,128]{2,1,0:T(8,128)(2,1)S(1)}, u32[]{:S(2)}, u32[]{:S(2)}) collective-permute-start(bf16[20,16,128]{2,1,0:T(8,128)(2,1)S(1)} %get-tuple-element.15), channel_id=1, source_target_pairs={{8,0},{10,2},{12,4},{14,6},{16,8},{18,10},{20,12},{22,14},{24,16},... | collective-permute-start | bytes 245768 | tf_op jit(solution)/shard_map/ppermute | solution.py:19
  25.4 4.0 %collective-permute-start.2 = (bf16[4,40,16,128]{3,2,1,0:T(8,128)(2,1)S(1)}, bf16[4,40,16,128]{3,2,1,0:T(8,128)(2,1)S(1)}, u32[]{:S(2)}, u32[]{:S(2)}) collective-permute-start(bf16[4,40,16,128]{3,2,1,0:T(8,128)(2,1)S(1)} %all_to_all.20.own), channel_id=1, source_target_pairs={{0,1},{1,0},{2,3},{3,2},{4,5},{5,4},{6,7},{7,6},{8,9},{9,8},{10,11... | collective-permute-start | bytes 1966088 | tf_op jit(solution)/shard_map/ppermute | solution.py:438

commit v8 on v7

--- a/solution.py
+++ b/solution.py
@@ -279,11 +279,12 @@
     one = lax.dot_general(FS[...], G1[...], along, preferred_element_type=F32)
     two = lax.dot_general(FP[...], G2[...], along, preferred_element_type=F32)
     one = one[0:144, :128] + one[48:192, 128:]
-    wg[0:144] = jnp.concatenate([two[:, 128:], one[:, 64:]], axis=1)
-    wg[144:288] = two[:, :128]
+    wg[0:144] = jnp.concatenate([two[:, 128:], one[:, 64:]], axis=1).astype(BF16)
+    wg[144:288] = two[:, :128].astype(BF16)
     thirds = [one[at : at + 48, :32] for at in (0, 48, 96)]
-    wg[288:336] = jnp.concatenate(thirds + [jnp.zeros((48, 32), F32)], axis=1)
-    wg[336:] = jnp.zeros((48, 128), F32)
+    rest = jnp.concatenate(thirds + [jnp.zeros((48, 32), F32)], axis=1)
+    wg[288:336] = rest.astype(BF16)
+    wg[336:] = jnp.zeros((48, 128), BF16)
 
 
 def own_block(feats, cot, w1, w2):
@@ -344,7 +345,7 @@
         out_specs=[vmem, vmem],
         out_shape=[
             jax.ShapeDtypeStruct((16, 2, 8, 128), BF16),
-            jax.ShapeDtypeStruct((384, 128), F32),
+            jax.ShapeDtypeStruct((384, 128), BF16),
         ],
         scratch_shapes=[pltpu.VMEM(shape, dtype) for shape, dtype in scratch],
         cost_estimate=pl.CostEstimate(
@@ -360,10 +361,11 @@
 
 
 def total_over_depth(part):
-    near = jnp.sum(exchange(part.reshape(16, 24, 128), NEAR), axis=0)
-    whole = jnp.sum(exchange(jnp.broadcast_to(near, (16, 24, 128)), FAR), axis=0)
-    copies = jnp.broadcast_to(whole.astype(BF16), (16, 24, 128))
-    return exchange(copies, NEAR)
+    pieces = exchange(part.reshape(16, 24, 128), NEAR)
+    for groups in (FAR, NEAR):
+        total = jnp.sum(pieces.astype(F32), axis=0).astype(BF16)
+        pieces = exchange(jnp.broadcast_to(total, (16, 24, 128)), groups)
+    return pieces
 
 
 def split_kernel(total, gf, one_out, two_out, gf_out, one, two, sems):

time: 84.3 us -> 82.5 us (0.979)
  blocking collectives: 60.9 us -> 59.1 us
    all_to_all x3, blocking collectives: 48.5 us -> 46.7 us  [exchange(): lax.all_to_all(pieces, DEPTH, 0, 0, axis_index_groups=groups, tiled=True)]
  transfers between devices with their start and end apart: 3 -> 3, of which waited for: 3 -> 3; matrix products, arithmetic and copies ran while one was open for 0% -> 0% of each run, Pallas kernels for 1% -> 2%
where the time goes in v8:
time: 82.5 us; the launch traced here: 82.2 us
  blocking collectives  59.1 us (72%)
  starting transfers between devices  10.9 us (13%)
  Pallas kernels  8.38 us (10%)
  waiting for transfers between devices  2.79 us (3%)
    all_to_all x3, blocking collectives, exchange(): lax.all_to_all(pieces, DEPTH, 0, 0, axis_index_groups=groups, tiled=True)  46.7 us
    all_to_all x1, blocking collectives, shards(): own = lax.all_to_all(jnp.stack(slots, 0), 'x', 0, 0, tiled=True)  12.3 us
    ppermute x2, starting transfers between devices, depth_shift(): return lax.ppermute(block, DEPTH, pairs)  9 us
    pallas_call x1, Pallas kernels, levels(): pl.pallas_call(main_kernel, in_specs=[vmem] * 6, out_specs=[vmem, vmem],...  5.12 us
    ppermute x2, waiting for transfers between devices, depth_shift(): return lax.ppermute(block, DEPTH, pairs)  1.98 us
    ppermute x1, starting transfers between devices, shards(): oth = lax.ppermute(own, 'chan', [(0, 1), (1, 0)])  1.91 us
  transfers between devices with their start and end apart: 3, of which 3 were waited for; matrix products, arithmetic and copies ran while one was open for 0% of the time, Pallas kernels for 2%

profile of v8, /device:TPU:8, one launch (start us, length us, event | category | flops | bytes accessed | tf_op | source)
XLA Modules:
  0.0 82.2 jit_solution(14694788287576899868)
XLA Ops:
  0.6 1.1 %gather.1 = (bf16[20,16,128]{2,1,0:T(8,128)(2,1)S(1)}, bf16[27,32,32]{2,1,0:T(8,128)(2,1)S(1)}, bf16[27,32,64]{2,1,0:T(8,128)(2,1)S(1)}) custom-call(bf16[16,2,8,128]{3,2,1,0:T(8,128)(2,1)} %feats_far.1, bf16[32,1,4,64]{3,2,1,0:T(4,128)(2,1)} %cot_far.1, bf16[27,32,32]{2,1,0:T(8,128)(2,1)} %bitcast.18, bf16[27,32,64]{2,1,0:T(8,128)(2,1)} %bitcast.19), custom_call_target="tpu_custom_call" | custom-call | tf_op jit(solution)/shard_map/gather/pallas_call | solution.py:293
  1.8 3.5 %collective-permute-start = (bf16[20,16,128]{2,1,0:T(8,128)(2,1)S(1)}, bf16[20,16,128]{2,1,0:T(8,128)(2,1)S(1)}, u32[]{:S(2)}, u32[]{:S(2)}) collective-permute-start(bf16[20,16,128]{2,1,0:T(8,128)(2,1)S(1)} %get-tuple-element.15), channel_id=1, source_target_pairs={{0,8},{2,10},{4,12},{6,14},{8,16},{10,18},{12,20},{14,22},{16,24},... | collective-permute-start | bytes 245768 | tf_op jit(solution)/shard_map/ppermute | solution.py:19
  5.3 5.5 %collective-permute-start.1 = (bf16[20,16,128]{2,1,0:T(8,128)(2,1)S(1)}, bf16[20,16,128]{2,1,0:T(8,128)(2,1)S(1)}, u32[]{:S(2)}, u32[]{:S(2)}) collective-permute-start(bf16[20,16,128]{2,1,0:T(8,128)(2,1)S(1)} %get-tuple-element.15), channel_id=1, source_target_pairs={{8,0},{10,2},{12,4},{14,6},{16,8},{18,10},{20,12},{22,14},{24,16},... | collective-permute-start | bytes 245768 | tf_op jit(solution)/shard_map/ppermute | solution.py:19
  10.8 0.4 collective-permute-done
  11.3 1.5 %collective-permute-done.1 = bf16[20,16,128]{2,1,0:T(8,128)(2,1)S(1)} collective-permute-done((bf16[20,16,128]{2,1,0:T(8,128)(2,1)S(1)}, bf16[20,16,128]{2,1,0:T(8,128)(2,1)S(1)}, u32[]{:S(2)}, u32[]{:S(2)}) %collective-permute-start.1) | collective-permute-done | bytes 81952 | tf_op jit(solution)/shard_map/ppermute | solution.py:19
  12.8 0.1 dynamic-slice_bitcast_fusion.3
  13.0 0.1 pad_maximum_fusion
  13.1 12.3 %all_to_all.20.own = bf16[4,40,16,128]{3,2,1,0:T(8,128)(2,1)S(1)} all-to-all(bf16[4,40,16,128]{3,2,1,0:T(8,128)(2,1)S(1)} %pad_maximum_fusion), channel_id=1, replica_groups=mesh['z'=8,'y'=8,'x'=4,'chan'=2] {'x'}, dimensions={0} | all-to-all | bytes 1310720 | tf_op jit(solution)/shard_map/all_to_all | solution.py:439
  25.4 1.9 %collective-permute-start.2 = (bf16[4,40,16,128]{3,2,1,0:T(8,128)(2,1)S(1)}, bf16[4,40,16,128]{3,2,1,0:T(8,128)(2,1)S(1)}, u32[]{:S(2)}, u32[]{:S(2)}) collective-permute-start(bf16[4,40,16,128]{3,2,1,0:T(8,128)(2,1)S(1)} %all_to_all.20.own), channel_id=1, source_target_pairs={{0,1},{1,0},{2,3},{3,2},{4,5},{5,4},{6,7},{7,6},{8,9},{9,8},{10,11... | collective-permute-start | bytes 1966088 | tf_op jit(solution)/shard_map/ppermute | solution.py:440
  27.3 1.2 %bands.1 = (bf16[256,2304]{1,0:T(8,128)(2,1)S(1)}, bf16[128,2304]{1,0:T(8,128)(2,1)S(1)}, bf16[256,1152]{1,0:T(8,128)(2,1)S(1)}, bf16[128,2304]{1,0:T(8,128)(2,1)S(1)}) custom-call(bf16[27,32,32]{2,1,0:T(8,128)(2,1)S(1)} %get-tuple-element.16.w1, bf16[27,32,64]{2,1,0:T(8,128)(2,1)S(1)} %get-tuple-element.17.w2), custom_call_target="tpu_custom_call" | custom-call | flops 1000000000 | bytes 4000000 | tf_op jit(solution)/shard_map/bands/pallas_call | solution.py:315
  28.6 0.8 collective-permute-done.2.oth
  29.4 5.1 %levels.1 = (bf16[16,2,8,128]{3,2,1,0:T(8,128)(2,1)S(1)}, bf16[384,128]{1,0:T(8,128)(2,1)S(1)}) custom-call(bf16[4,40,16,128]{3,2,1,0:T(8,128)(2,1)S(1)} %all_to_all.20.own, bf16[4,40,16,128]{3,2,1,0:T(8,128)(2,1)S(1)} %collective-permute-done.2.oth, bf16[256,2304]{1,0:T(8,128)(2,1)S(1)} %get-tuple-element.18.t1, ...), custom_call_target="tpu_custom_call" | custom-call | flops 10000000000 | bytes 8000000 | tf_op jit(solution)/shard_map/levels/pallas_call | solution.py:342
  34.5 11.6 %all_to_all.21 = bf16[16,24,128]{2,1,0:T(8,128)(2,1)S(1)} all-to-all(bf16[16,24,128]{2,1,0:T(8,128)(2,1)S(1)} %bitcast.17), channel_id=1, replica_groups={{0,64,8,72,2,66,10,74,4,68,12,76,6,70,14,78},{16,80,24,88,18,82,26,90,2..., dimensions={0} | all-to-all | bytes 196608 | tf_op jit(solution)/shard_map/all_to_all | solution.py:360
  46.1 23.7 %all_to_all.22 = bf16[16,24,128]{2,1,0:T(8,128)(2,1)S(1)} all-to-all(bf16[16,24,128]{2,1,0:T(8,128)(2,1)S(1)} %broadcast_in_dim.6), channel_id=1, replica_groups={{0,16,40,56,128,144,168,184,320,336,360,376,448,464,488,504},{64,80,104..., dimensions={0} | all-to-all | bytes 196608 | tf_op jit(solution)/shard_map/all_to_all | solution.py:360
  69.9 11.4 %all_to_all.23.total = bf16[16,24,128]{2,1,0:T(8,128)(2,1)S(1)} all-to-all(bf16[16,24,128]{2,1,0:T(8,128)(2,1)S(1)} %broadcast_in_dim.7), channel_id=1, replica_groups={{0,64,8,72,2,66,10,74,4,68,12,76,6,70,14,78},{16,80,24,88,18,82,26,90,2..., dimensions={0} | all-to-all | bytes 196608 | tf_op jit(solution)/shard_map/all_to_all | solution.py:360
  81.3 0.9 %split.1 = (f32[432,32]{1,0:T(8,128)}, f32[432,64]{1,0:T(8,128)}, bf16[16,2,8,128]{3,2,1,0:T(8,128)(2,1)}) custom-call(bf16[16,24,128]{2,1,0:T(8,128)(2,1)S(1)} %all_to_all.23.total, bf16[16,2,8,128]{3,2,1,0:T(8,128)(2,1)S(1)} %get-tuple-element.23.gf), custom_call_target="tpu_custom_call" | custom-call | tf_op jit(solution)/shard_map/split/pallas_call | solution.py:406
  (7 shorter events, 0.1 us)
Async XLA Ops:
  1.8 9.5 %collective-permute-start = (bf16[20,16,128]{2,1,0:T(8,128)(2,1)S(1)}, bf16[20,16,128]{2,1,0:T(8,128)(2,1)S(1)}, u32[]{:S(2)}, u32[]{:S(2)}) collective-permute-start(bf16[20,16,128]{2,1,0:T(8,128)(2,1)S(1)} %get-tuple-element.15), channel_id=1, source_target_pairs={{0,8},{2,10},{4,12},{6,14},{8,16},{10,18},{12,20},{14,22},{16,24},... | collective-permute-start | bytes 245768 | tf_op jit(solution)/shard_map/ppermute | solution.py:19
  5.3 7.6 %collective-permute-start.1 = (bf16[20,16,128]{2,1,0:T(8,128)(2,1)S(1)}, bf16[20,16,128]{2,1,0:T(8,128)(2,1)S(1)}, u32[]{:S(2)}, u32[]{:S(2)}) collective-permute-start(bf16[20,16,128]{2,1,0:T(8,128)(2,1)S(1)} %get-tuple-element.15), channel_id=1, source_target_pairs={{8,0},{10,2},{12,4},{14,6},{16,8},{18,10},{20,12},{22,14},{24,16},... | collective-permute-start | bytes 245768 | tf_op jit(solution)/shard_map/ppermute | solution.py:19
  25.4 4.0 %collective-permute-start.2 = (bf16[4,40,16,128]{3,2,1,0:T(8,128)(2,1)S(1)}, bf16[4,40,16,128]{3,2,1,0:T(8,128)(2,1)S(1)}, u32[]{:S(2)}, u32[]{:S(2)}) collective-permute-start(bf16[4,40,16,128]{3,2,1,0:T(8,128)(2,1)S(1)} %all_to_all.20.own), channel_id=1, source_target_pairs={{0,1},{1,0},{2,3},{3,2},{4,5},{5,4},{6,7},{7,6},{8,9},{9,8},{10,11... | collective-permute-start | bytes 1966088 | tf_op jit(solution)/shard_map/ppermute | solution.py:440

commit v9 on v8

--- a/solution.py
+++ b/solution.py
@@ -65,15 +65,23 @@
         copy.wait()
 
 
-def band_kernel(w1, w2, t1, t1t, t2, t2t, rows_one):
+def band_kernel(w1, w2, t1_own, t1_oth, t1t, t2, t2t, rows_one):
     turn = position()[0] * 16
     half = pl.multiple_of(turn, 16)
 
-    def marks_of(width, lanes, sign, turn):
+    def marks_of(width, lanes, sign):
         row = lax.broadcasted_iota(jnp.int32, (3 * width, lanes), 0)
         lane = lax.broadcasted_iota(jnp.int32, (3 * width, lanes), 1)
-        base = lane - (sign * (row // width - 1) * width + (row + turn) % width)
+        base = lane - (sign * (row // width - 1) * width + row % width)
         return lambda h: jnp.where(base == h * width, 1.0, 0.0).astype(BF16)
+
+    def marks_by_core():
+        row = lax.broadcasted_iota(jnp.int32, (96, 256), 0)
+        lane = lax.broadcasted_iota(jnp.int32, (96, 256), 1)
+        chan = (row + turn) % 32
+        fits = (lane // 128 == chan // 16) & (lane % 16 == chan % 16)
+        base = jnp.where(fits, lane % 128 // 16 - (row // 32 - 1), -1)
+        return lambda h: jnp.where(base == h, 1.0, 0.0).astype(BF16)
 
     def taps_of(ref, flip):
         order = [(2 - a, 2 - c) if flip else (a, c) for a in range(3) for c in range(3)]
@@ -111,10 +119,17 @@
                 h, pl.ds(tap * 32 + half, 16), :
             ]
 
-    straight(w1, False, marks_of(32, 256, 1, turn), 8, into(t1, 32, 256))
-    crossed(w1, True, marks_of(32, 256, -1, 0), 8, put_half)
-    crossed(w2, False, marks_of(32, 128, 1, 0), 4, into(t2, 64, 128))
-    straight(w2, True, marks_of(64, 256, -1, 0), 4, into(t2t, 32, 256))
+    def put_both(h, bands):
+        for tap in range(9):
+            for side, out in ((0, t1_own), (128, t1_oth)):
+                out[h * 32 : (h + 1) * 32, tap * 128 : (tap + 1) * 128] = bands[
+                    tap * 32 : (tap + 1) * 32, side : side + 128
+                ]
+
+    straight(w1, False, marks_by_core(), 8, put_both)
+    crossed(w1, True, marks_of(32, 256, -1), 8, put_half)
+    crossed(w2, False, marks_of(32, 128, 1), 4, into(t2, 64, 128))
+    straight(w2, True, marks_of(64, 256, -1), 4, into(t2t, 32, 256))
 
 
 def shifted(value, step):
@@ -125,8 +140,49 @@
     return low.astype(BF16), value.astype(BF16), high.astype(BF16)
 
 
+def plane_tiles(x):
+    def slot(delta):
+        return lax.rem(x + delta + 4, 4)
+
+    planes = [(slot(0), 0)]
+    planes += [(slot(delta), 8 * p) for delta in (-3, -2, -1) for p in range(2)]
+    planes += [(slot(0), 12), (slot(0), 20)]
+    planes += [(slot(delta), 20 + 8 * p) for delta in (1, 2, 3) for p in range(2)]
+    return planes + [(slot(0), 32)]
+
+
+def convolve_half(tiles, bands, fields, use):
+    planes = plane_tiles(lax.rem(position()[1], 4))
+
+    def load_plane(j):
+        at, start = planes[j]
+        plane = tiles[at, start : start + 8].reshape(128, 128)
+        for c, part in enumerate(shifted(plane.astype(F32), 1)):
+            if j <= 8:
+                fields[j, c, :, :128] = part
+            if j >= 7:
+                fields[j - 7, c, :, 128:] = part
+
+    for j in (0, 1, 7, 8):
+        load_plane(j)
+    for k in range(7):
+        for j in (k + 2, k + 9):
+            if j not in (7, 8) and j < 16:
+                load_plane(j)
+        field = fields[k : k + 3].reshape(1152, 256)
+        use(k, jnp.dot(bands[...], field, preferred_element_type=F32))
+
+
+def own_kernel(own, t1_own, fields, sums):
+    def use(k, part):
+        sums[k] = part
+
+    convolve_half(own, t1_own, fields, use)
+
+
 def main_kernel(
-    own, oth, t1, t1t, t2, t2t, gf, wg, XP, PS, SL, QP, GP, HP, CT, FS, FP, G1, G2
+    own, oth, own_fields, own_sums, t1_oth, t1t, t2, t2t, gf, wg,
+    XP, PS, SL, QP, GP, HP, CT, FS, FP, G1, G2,
 ):
     member, place = position()
     x = lax.rem(place, 4)
@@ -135,31 +191,8 @@
     def slot(delta):
         return lax.rem(x + delta + 4, 4)
 
-    planes = [(slot(0), 0)]
-    planes += [(slot(delta), 8 * p) for delta in (-3, -2, -1) for p in range(2)]
-    planes += [(slot(0), 12), (slot(0), 20)]
-    planes += [(slot(delta), 20 + 8 * p) for delta in (1, 2, 3) for p in range(2)]
-    planes += [(slot(0), 32)]
-
-    def load_plane(j):
-        at, start = planes[j]
-        plane = jnp.concatenate(
-            [own[at, start : start + 8], oth[at, start : start + 8]], axis=1
-        ).reshape(256, 128)
-        for c, part in enumerate(shifted(plane.astype(F32), 1)):
-            if j <= 8:
-                XP[j, c, :, :128] = part
-            if j >= 7:
-                XP[j - 7, c, :, 128:] = part
-
-    for j in (0, 1, 7, 8):
-        load_plane(j)
-
-    for k in range(7):
-        for j in (k + 2, k + 9):
-            if j not in (7, 8) and j < 16:
-                load_plane(j)
-        pre = jnp.dot(t1[...], XP[k : k + 3].reshape(2304, 256), preferred_element_type=F32)
+    def use(k, part):
+        pre = part + own_sums[k]
         act = (pre * jax.nn.sigmoid(pre)).astype(BF16).astype(F32).reshape(4, 2, 32, 256)
         rows = (act[:, 0] + act[:, 1]).reshape(128, 256)
         PS[k] = rows[:, :128]
@@ -168,6 +201,8 @@
             SL[k - 5] = slope(pre[:, :128])
         if k <= 1:
             SL[k + 2] = slope(pre[:, 128:])
+
+    convolve_half(oth, t1_oth, XP, use)
 
     lane = lax.broadcasted_iota(jnp.int32, (128, 128), 1)
     even = lane % 2 == 0
@@ -266,8 +301,8 @@
             m, side = (j + 6, 0) if j <= 2 else (2, 128)
             to = (j * 3 + c) * 16
             for h in range(8):
-                FS[to : to + 16, h * 128 : (h + 1) * 128] = XP[
-                    m, c, h * 32 : h * 32 + 16, side : side + 128
+                FS[to : to + 16, h * 128 : (h + 1) * 128] = own_fields[
+                    m, c, h * 16 : h * 16 + 16, side : side + 128
                 ]
         for a in range(3):
             to = (a * 3 + c) * 16
@@ -311,11 +346,11 @@
 
 def band_weights(w1, w2):
     vmem = pl.BlockSpec(memory_space=pltpu.VMEM)
-    shapes = [(256, 2304), (128, 2304), (256, 1152), (128, 2304)]
+    shapes = [(256, 1152), (256, 1152), (128, 2304), (256, 1152), (128, 2304)]
     return pl.pallas_call(
         band_kernel,
         in_specs=[vmem] * 2,
-        out_specs=[vmem] * 4,
+        out_specs=[vmem] * 5,
         scratch_shapes=[pltpu.VMEM((8, 288, 256), BF16)],
         out_shape=[jax.ShapeDtypeStruct(shape, BF16) for shape in shapes],
         cost_estimate=pl.CostEstimate(flops=10**9, bytes_accessed=4 * 10**6, transcendentals=0),
@@ -324,10 +359,26 @@
     )(w1, w2)
 
 
-def levels(own, oth, bands):
+def own_half(own, t1_own):
+    vmem = pl.BlockSpec(memory_space=pltpu.VMEM)
+    return pl.pallas_call(
+        own_kernel,
+        in_specs=[vmem, vmem],
+        out_specs=[vmem, vmem],
+        out_shape=[
+            jax.ShapeDtypeStruct((9, 3, 128, 256), BF16),
+            jax.ShapeDtypeStruct((7, 256, 256), F32),
+        ],
+        cost_estimate=pl.CostEstimate(flops=10**9, bytes_accessed=5 * 10**6, transcendentals=0),
+        compiler_params=pltpu.CompilerParams(vmem_limit_bytes=12 * 2**20),
+        name="half",
+    )(own, t1_own)
+
+
+def levels(fields, bands):
     vmem = pl.BlockSpec(memory_space=pltpu.VMEM)
     scratch = [
-        ((9, 3, 256, 256), BF16),
+        ((9, 3, 128, 256), BF16),
         ((14, 128, 128), F32),
         ((4, 256, 128), F32),
         ((5, 3, 128, 256), BF16),
@@ -341,7 +392,7 @@
     ]
     return pl.pallas_call(
         main_kernel,
-        in_specs=[vmem] * 6,
+        in_specs=[vmem] * 8,
         out_specs=[vmem, vmem],
         out_shape=[
             jax.ShapeDtypeStruct((16, 2, 8, 128), BF16),
@@ -353,7 +404,7 @@
         ),
         compiler_params=pltpu.CompilerParams(vmem_limit_bytes=28 * 2**20),
         name="levels",
-    )(own, oth, *bands)
+    )(*fields, *bands)
 
 
 def exchange(pieces, groups):
@@ -438,7 +489,8 @@
     ]
     own = lax.all_to_all(jnp.stack(slots, 0), "x", 0, 0, tiled=True)
     oth = lax.ppermute(own, "chan", [(0, 1), (1, 0)])
-    grad_feats, part = levels(own, oth, bands)
+    own_fields, own_sums = own_half(own, bands[0])
+    grad_feats, part = levels((own, oth, own_fields, own_sums), bands[1:])
     one, two, grad_feats = split_total(total_over_depth(part), grad_feats)
     grad_weight_one = jnp.transpose(one.reshape(27, 16, 32), (2, 1, 0))
     grad_weight_two = jnp.transpose(two.reshape(27, 16, 64), (2, 1, 0))

time: 82.5 us -> 82.1 us (level)
    pallas_call x2 -> x3, Pallas kernels: 6.37 us -> 6.75 us  [the longest x1 3.87 us: levels(): pl.pallas_call(main_kernel, in_specs=[vmem] * 8, out_specs=[vmem, vmem],...]
  transfers between devices with their start and end apart: 3 -> 3, of which waited for: 3 -> 2; matrix products, arithmetic and copies ran while one was open for 0% -> 0% of each run, Pallas kernels for 2% -> 4%
where the time goes in v9:
time: 82.1 us; the launch traced here: 81.8 us
  blocking collectives  59.1 us (72%)
  starting transfers between devices  10.9 us (13%)
  Pallas kernels  8.77 us (11%)
  waiting for transfers between devices  1.99 us (2%)
    all_to_all x3, blocking collectives, exchange(): lax.all_to_all(pieces, DEPTH, 0, 0, axis_index_groups=groups, tiled=True)  46.7 us
    all_to_all x1, blocking collectives, shards(): own = lax.all_to_all(jnp.stack(slots, 0), 'x', 0, 0, tiled=True)  12.3 us
    ppermute x2, starting transfers between devices, depth_shift(): return lax.ppermute(block, DEPTH, pairs)  9 us
    pallas_call x1, Pallas kernels, levels(): pl.pallas_call(main_kernel, in_specs=[vmem] * 8, out_specs=[vmem, vmem],...  3.87 us
    ppermute x2, waiting for transfers between devices, depth_shift(): return lax.ppermute(block, DEPTH, pairs)  1.98 us
    ppermute x1, starting transfers between devices, shards(): oth = lax.ppermute(own, 'chan', [(0, 1), (1, 0)])  1.91 us
  transfers between devices with their start and end apart: 3, of which 2 were waited for; matrix products, arithmetic and copies ran while one was open for 0% of the time, Pallas kernels for 4%

profile of v9, /device:TPU:8, one launch (start us, length us, event | category | flops | bytes accessed | tf_op | source)
XLA Modules:
  0.0 81.8 jit_solution(18373446946399419367)
XLA Ops:
  0.6 1.1 %gather.1 = (bf16[20,16,128]{2,1,0:T(8,128)(2,1)S(1)}, bf16[27,32,32]{2,1,0:T(8,128)(2,1)S(1)}, bf16[27,32,64]{2,1,0:T(8,128)(2,1)S(1)}) custom-call(bf16[16,2,8,128]{3,2,1,0:T(8,128)(2,1)} %feats_far.1, bf16[32,1,4,64]{3,2,1,0:T(4,128)(2,1)} %cot_far.1, bf16[27,32,32]{2,1,0:T(8,128)(2,1)} %bitcast.18, bf16[27,32,64]{2,1,0:T(8,128)(2,1)} %bitcast.19), custom_call_target="tpu_custom_call" | custom-call | tf_op jit(solution)/shard_map/gather/pallas_call | solution.py:328
  1.8 3.5 %collective-permute-start = (bf16[20,16,128]{2,1,0:T(8,128)(2,1)S(1)}, bf16[20,16,128]{2,1,0:T(8,128)(2,1)S(1)}, u32[]{:S(2)}, u32[]{:S(2)}) collective-permute-start(bf16[20,16,128]{2,1,0:T(8,128)(2,1)S(1)} %get-tuple-element.18), channel_id=1, source_target_pairs={{0,8},{2,10},{4,12},{6,14},{8,16},{10,18},{12,20},{14,22},{16,24},... | collective-permute-start | bytes 245768 | tf_op jit(solution)/shard_map/ppermute | solution.py:19
  5.3 5.5 %collective-permute-start.1 = (bf16[20,16,128]{2,1,0:T(8,128)(2,1)S(1)}, bf16[20,16,128]{2,1,0:T(8,128)(2,1)S(1)}, u32[]{:S(2)}, u32[]{:S(2)}) collective-permute-start(bf16[20,16,128]{2,1,0:T(8,128)(2,1)S(1)} %get-tuple-element.18), channel_id=1, source_target_pairs={{8,0},{10,2},{12,4},{14,6},{16,8},{18,10},{20,12},{22,14},{24,16},... | collective-permute-start | bytes 245768 | tf_op jit(solution)/shard_map/ppermute | solution.py:19
  10.8 0.4 collective-permute-done
  11.3 1.5 %collective-permute-done.1 = bf16[20,16,128]{2,1,0:T(8,128)(2,1)S(1)} collective-permute-done((bf16[20,16,128]{2,1,0:T(8,128)(2,1)S(1)}, bf16[20,16,128]{2,1,0:T(8,128)(2,1)S(1)}, u32[]{:S(2)}, u32[]{:S(2)}) %collective-permute-start.1) | collective-permute-done | bytes 81952 | tf_op jit(solution)/shard_map/ppermute | solution.py:19
  12.8 0.1 dynamic-slice_bitcast_fusion.3
  13.0 0.1 pad_maximum_fusion
  13.1 12.3 %all_to_all.20.own = bf16[4,40,16,128]{3,2,1,0:T(8,128)(2,1)S(1)} all-to-all(bf16[4,40,16,128]{3,2,1,0:T(8,128)(2,1)S(1)} %pad_maximum_fusion), channel_id=1, replica_groups=mesh['z'=8,'y'=8,'x'=4,'chan'=2] {'x'}, dimensions={0} | all-to-all | bytes 1310720 | tf_op jit(solution)/shard_map/all_to_all | solution.py:490
  25.4 1.9 %collective-permute-start.2 = (bf16[4,40,16,128]{3,2,1,0:T(8,128)(2,1)S(1)}, bf16[4,40,16,128]{3,2,1,0:T(8,128)(2,1)S(1)}, u32[]{:S(2)}, u32[]{:S(2)}) collective-permute-start(bf16[4,40,16,128]{3,2,1,0:T(8,128)(2,1)S(1)} %all_to_all.20.own), channel_id=1, source_target_pairs={{0,1},{1,0},{2,3},{3,2},{4,5},{5,4},{6,7},{7,6},{8,9},{9,8},{10,11... | collective-permute-start | bytes 1966088 | tf_op jit(solution)/shard_map/ppermute | solution.py:491
  27.3 1.4 %bands.1 = (bf16[256,1152]{1,0:T(8,128)(2,1)S(1)}, bf16[256,1152]{1,0:T(8,128)(2,1)S(1)}, bf16[128,2304]{1,0:T(8,128)(2,1)S(1)}, bf16[256,1152]{1,0:T(8,128)(2,1)S(1)}, bf16[128,2304]{1,0:T(8,128)(2,1)S(1)}) custom-call(bf16[27,32,32]{2,1,0:T(8,128)(2,1)S(1)} %get-tuple-element.19.w1, bf16[27,32,64]{2,1,0:T(8,128)(2,1)S(1)} %get-tuple-element.20.w2), custom_call_target="tpu_custom_call" | custom-call | flops 1000000000 | bytes 4000000 | tf_op jit(solution)/shard_map/bands/pallas_call | solution.py:350
  28.7 1.5 %half.1 = (bf16[9,3,128,256]{3,2,1,0:T(8,128)(2,1)S(1)}, f32[7,256,256]{2,1,0:T(8,128)S(1)}) custom-call(bf16[4,40,16,128]{3,2,1,0:T(8,128)(2,1)S(1)} %all_to_all.20.own, bf16[256,1152]{1,0:T(8,128)(2,1)S(1)} %get-tuple-element.21.t1_own), custom_call_target="tpu_custom_call" | custom-call | flops 1000000000 | bytes 5000000 | tf_op jit(solution)/shard_map/half/pallas_call | solution.py:364
  30.2 0.0 collective-permute-done.2.oth
  30.2 3.9 %levels.1 = (bf16[16,2,8,128]{3,2,1,0:T(8,128)(2,1)S(1)}, bf16[384,128]{1,0:T(8,128)(2,1)S(1)}) custom-call(bf16[4,40,16,128]{3,2,1,0:T(8,128)(2,1)S(1)} %all_to_all.20.own, bf16[4,40,16,128]{3,2,1,0:T(8,128)(2,1)S(1)} %collective-permute-done.2.oth, bf16[9,3,128,256]{3,2,1,0:T(8,128)(2,1)S(1)} %get-tuple-element.22.own_fields, ...), custom_call_target="tpu_custom_call" | custom-call | flops 10000000000 | bytes 8000000 | tf_op jit(solution)/shard_map/levels/pallas_call | solution.py:393
  34.1 11.5 %all_to_all.21 = bf16[16,24,128]{2,1,0:T(8,128)(2,1)S(1)} all-to-all(bf16[16,24,128]{2,1,0:T(8,128)(2,1)S(1)} %bitcast.17), channel_id=1, replica_groups={{0,64,8,72,2,66,10,74,4,68,12,76,6,70,14,78},{16,80,24,88,18,82,26,90,2..., dimensions={0} | all-to-all | bytes 196608 | tf_op jit(solution)/shard_map/all_to_all | solution.py:411
  45.7 23.7 %all_to_all.22 = bf16[16,24,128]{2,1,0:T(8,128)(2,1)S(1)} all-to-all(bf16[16,24,128]{2,1,0:T(8,128)(2,1)S(1)} %broadcast_in_dim.6), channel_id=1, replica_groups={{0,16,40,56,128,144,168,184,320,336,360,376,448,464,488,504},{64,80,104..., dimensions={0} | all-to-all | bytes 196608 | tf_op jit(solution)/shard_map/all_to_all | solution.py:411
  69.4 11.5 %all_to_all.23.total = bf16[16,24,128]{2,1,0:T(8,128)(2,1)S(1)} all-to-all(bf16[16,24,128]{2,1,0:T(8,128)(2,1)S(1)} %broadcast_in_dim.7), channel_id=1, replica_groups={{0,64,8,72,2,66,10,74,4,68,12,76,6,70,14,78},{16,80,24,88,18,82,26,90,2..., dimensions={0} | all-to-all | bytes 196608 | tf_op jit(solution)/shard_map/all_to_all | solution.py:411
  80.9 0.9 %split.1 = (f32[432,32]{1,0:T(8,128)}, f32[432,64]{1,0:T(8,128)}, bf16[16,2,8,128]{3,2,1,0:T(8,128)(2,1)}) custom-call(bf16[16,24,128]{2,1,0:T(8,128)(2,1)S(1)} %all_to_all.23.total, bf16[16,2,8,128]{3,2,1,0:T(8,128)(2,1)S(1)} %get-tuple-element.29.gf), custom_call_target="tpu_custom_call" | custom-call | tf_op jit(solution)/shard_map/split/pallas_call | solution.py:457
  (7 shorter events, 0.1 us)
Async XLA Ops:
  1.8 9.5 %collective-permute-start = (bf16[20,16,128]{2,1,0:T(8,128)(2,1)S(1)}, bf16[20,16,128]{2,1,0:T(8,128)(2,1)S(1)}, u32[]{:S(2)}, u32[]{:S(2)}) collective-permute-start(bf16[20,16,128]{2,1,0:T(8,128)(2,1)S(1)} %get-tuple-element.18), channel_id=1, source_target_pairs={{0,8},{2,10},{4,12},{6,14},{8,16},{10,18},{12,20},{14,22},{16,24},... | collective-permute-start | bytes 245768 | tf_op jit(solution)/shard_map/ppermute | solution.py:19
  5.3 7.6 %collective-permute-start.1 = (bf16[20,16,128]{2,1,0:T(8,128)(2,1)S(1)}, bf16[20,16,128]{2,1,0:T(8,128)(2,1)S(1)}, u32[]{:S(2)}, u32[]{:S(2)}) collective-permute-start(bf16[20,16,128]{2,1,0:T(8,128)(2,1)S(1)} %get-tuple-element.18), channel_id=1, source_target_pairs={{8,0},{10,2},{12,4},{14,6},{16,8},{18,10},{20,12},{22,14},{24,16},... | collective-permute-start | bytes 245768 | tf_op jit(solution)/shard_map/ppermute | solution.py:19
  25.4 4.8 %collective-permute-start.2 = (bf16[4,40,16,128]{3,2,1,0:T(8,128)(2,1)S(1)}, bf16[4,40,16,128]{3,2,1,0:T(8,128)(2,1)S(1)}, u32[]{:S(2)}, u32[]{:S(2)}) collective-permute-start(bf16[4,40,16,128]{3,2,1,0:T(8,128)(2,1)S(1)} %all_to_all.20.own), channel_id=1, source_target_pairs={{0,1},{1,0},{2,3},{3,2},{4,5},{5,4},{6,7},{7,6},{8,9},{9,8},{10,11... | collective-permute-start | bytes 1966088 | tf_op jit(solution)/shard_map/ppermute | solution.py:491

commit v10 on v9

--- a/solution.py
+++ b/solution.py
@@ -44,8 +44,8 @@
     return lax.axis_index("chan"), place
 
 
-def gather_kernel(feats_far, cot_far, w1, w2, block, w1_near, w2_near, feats, cot, sems):
-    pairs = ((feats_far, feats), (cot_far, cot), (w1, w1_near), (w2, w2_near))
+def gather_kernel(feats_far, cot_far, block, feats, cot, sems):
+    pairs = ((feats_far, feats), (cot_far, cot))
     copies = [
         pltpu.make_async_copy(source, target, sems.at[index])
         for index, (source, target) in enumerate(pairs)
@@ -61,11 +61,16 @@
     for high in range(2):
         pair = jnp.concatenate([rows[2 * high], rows[2 * high + 1]], axis=1)
         block[16 + 2 * high : 18 + 2 * high] = pair.astype(BF16).reshape(2, 16, 128)
-    for copy in copies[2:]:
-        copy.wait()
-
-
-def band_kernel(w1, w2, t1_own, t1_oth, t1t, t2, t2t, rows_one):
+
+
+def band_kernel(w1_far, w2_far, t1_own, t1_oth, t1t, t2, t2t, rows_one, w1, w2, sems):
+    pairs = ((w1_far, w1), (w2_far, w2))
+    copies = [
+        pltpu.make_async_copy(source, target, sems.at[index])
+        for index, (source, target) in enumerate(pairs)
+    ]
+    for copy in copies:
+        copy.start()
     turn = position()[0] * 16
     half = pl.multiple_of(turn, 16)
 
@@ -126,18 +131,23 @@
                     tap * 32 : (tap + 1) * 32, side : side + 128
                 ]
 
+    copies[0].wait()
     straight(w1, False, marks_by_core(), 8, put_both)
     crossed(w1, True, marks_of(32, 256, -1), 8, put_half)
+    copies[1].wait()
     crossed(w2, False, marks_of(32, 128, 1), 4, into(t2, 64, 128))
     straight(w2, True, marks_of(64, 256, -1), 4, into(t2t, 32, 256))
 
 
 def shifted(value, step):
+    value = value.astype(BF16)
     lanes = value.shape[-1]
-    lane = lax.broadcasted_iota(jnp.int32, value.shape, 1)
-    low = jnp.where(lane < step, 0.0, pltpu.roll(value, step, 1))
-    high = jnp.where(lane >= lanes - step, 0.0, pltpu.roll(value, lanes - step, 1))
-    return low.astype(BF16), value.astype(BF16), high.astype(BF16)
+    lane = lax.broadcasted_iota(jnp.int32, (1, lanes), 1)
+    inner = jnp.where(lane < step, 0.0, 1.0).astype(BF16)
+    outer = jnp.where(lane >= lanes - step, 0.0, 1.0).astype(BF16)
+    low = pltpu.roll(value, step, 1) * inner
+    high = pltpu.roll(value, lanes - step, 1) * outer
+    return low, value, high
 
 
 def plane_tiles(x):
@@ -152,12 +162,12 @@
 
 
 def convolve_half(tiles, bands, fields, use):
-    planes = plane_tiles(lax.rem(position()[1], 4))
+    planes = plane_tiles(lax.rem(position()[1], ROW))
 
     def load_plane(j):
         at, start = planes[j]
         plane = tiles[at, start : start + 8].reshape(128, 128)
-        for c, part in enumerate(shifted(plane.astype(F32), 1)):
+        for c, part in enumerate(shifted(plane, 1)):
             if j <= 8:
                 fields[j, c, :, :128] = part
             if j >= 7:
@@ -213,7 +223,7 @@
         total = total + jnp.where(even, pltpu.roll(total, 127, 1), pltpu.roll(total, 1, 1))
         at = place + (j - 3)
         factor = jnp.where((at >= 0) & (at < SLABS), 0.125, 0.0)
-        pooled = (total * factor).astype(BF16).astype(F32)
+        pooled = (total * factor).astype(BF16)
         for c, part in enumerate(shifted(pooled, 2)):
             if j <= 4:
                 QP[j, c, :, :128] = part
@@ -250,15 +260,15 @@
                 ],
                 axis=0,
             )
-            grad = (cots_of * side).astype(BF16).astype(F32)
+            grad = (cots_of * side).astype(BF16)
             for c, part in enumerate(shifted(grad, 2)):
                 for m in range(3):
                     n = plane - m
                     if 0 <= n <= 2:
                         GP[m, c, :, n * 128 : (n + 1) * 128] = part
             if plane == 2:
-                lanes = lax.broadcasted_iota(jnp.int32, (256, 128), 1)
-                kept = jnp.where(lanes % 2 == 0, grad, 0.0).astype(BF16)
+                lanes = lax.broadcasted_iota(jnp.int32, (1, 128), 1)
+                kept = grad * jnp.where(lanes % 2 == 0, 1.0, 0.0).astype(BF16)
                 for b in range(3):
                     for at in range(4):
                         h = at + 1 - b
@@ -273,7 +283,7 @@
         factor = jnp.where((at >= 0) & (at < SLABS), 0.125, 0.0)
         part = (back[:, f * 128 : (f + 1) * 128] * factor).reshape(4, 1, 32, 128)
         wide = jnp.concatenate([part, part], axis=1).reshape(256, 128)
-        grad = (wide * SL[q]).astype(BF16).astype(F32)
+        grad = (wide * SL[q]).astype(BF16)
         for c, piece in enumerate(shifted(grad, 1)):
             if q <= 2:
                 HP[q, c, :, :128] = piece
@@ -322,41 +332,45 @@
     wg[336:] = jnp.zeros((48, 128), BF16)
 
 
-def own_block(feats, cot, w1, w2):
-    vmem = pl.BlockSpec(memory_space=pltpu.VMEM)
+def far_operands(*arrays):
+    return [pltpu.with_memory_space_constraint(array, pltpu.HBM) for array in arrays]
+
+
+def own_block(feats, cot):
     hbm = pl.BlockSpec(memory_space=pltpu.MemorySpace.HBM)
     return pl.pallas_call(
         gather_kernel,
-        in_specs=[hbm] * 4,
-        out_specs=[vmem] * 3,
-        out_shape=[
-            jax.ShapeDtypeStruct((20, 16, 128), BF16),
-            jax.ShapeDtypeStruct(w1.shape, BF16),
-            jax.ShapeDtypeStruct(w2.shape, BF16),
-        ],
+        in_specs=[hbm] * 2,
+        out_specs=pl.BlockSpec(memory_space=pltpu.VMEM),
+        out_shape=jax.ShapeDtypeStruct((20, 16, 128), BF16),
         scratch_shapes=[
             pltpu.VMEM(feats.shape, BF16),
             pltpu.VMEM(cot.shape, BF16),
-            pltpu.SemaphoreType.DMA((4,)),
+            pltpu.SemaphoreType.DMA((2,)),
         ],
         compiler_params=pltpu.CompilerParams(vmem_limit_bytes=4 * 2**20),
         name="gather",
-    )(*[pltpu.with_memory_space_constraint(array, pltpu.HBM) for array in (feats, cot, w1, w2)])
+    )(*far_operands(feats, cot))
 
 
 def band_weights(w1, w2):
-    vmem = pl.BlockSpec(memory_space=pltpu.VMEM)
+    hbm = pl.BlockSpec(memory_space=pltpu.MemorySpace.HBM)
     shapes = [(256, 1152), (256, 1152), (128, 2304), (256, 1152), (128, 2304)]
     return pl.pallas_call(
         band_kernel,
-        in_specs=[vmem] * 2,
-        out_specs=[vmem] * 5,
-        scratch_shapes=[pltpu.VMEM((8, 288, 256), BF16)],
+        in_specs=[hbm] * 2,
+        out_specs=[pl.BlockSpec(memory_space=pltpu.VMEM)] * 5,
         out_shape=[jax.ShapeDtypeStruct(shape, BF16) for shape in shapes],
+        scratch_shapes=[
+            pltpu.VMEM((8, 288, 256), BF16),
+            pltpu.VMEM(w1.shape, BF16),
+            pltpu.VMEM(w2.shape, BF16),
+            pltpu.SemaphoreType.DMA((2,)),
+        ],
         cost_estimate=pl.CostEstimate(flops=10**9, bytes_accessed=4 * 10**6, transcendentals=0),
         compiler_params=pltpu.CompilerParams(vmem_limit_bytes=16 * 2**20),
         name="bands",
-    )(w1, w2)
+    )(*far_operands(w1, w2))
 
 
 def own_half(own, t1_own):
@@ -469,16 +483,13 @@
 
 def shards(feats, weight_one, weight_two, cotangent):
     x = lax.axis_index("x")
-    block, w1, w2 = own_block(
-        feats,
-        cotangent,
-        jnp.transpose(weight_one, (2, 0, 1)),
-        jnp.transpose(weight_two, (2, 1, 0)),
-    )
+    block = own_block(feats, cotangent)
     up = depth_shift(block, ROW)
     down = depth_shift(block, -ROW)
 
-    bands = band_weights(w1, w2)
+    bands = band_weights(
+        jnp.transpose(weight_one, (2, 0, 1)), jnp.transpose(weight_two, (2, 1, 0))
+    )
 
     three = jnp.concatenate([up, block, down], axis=0)
     slots = [

time: 82.1 us -> 83.1 us (1.012)
  Pallas kernels: 8.77 us -> 9.72 us
    pallas_call x2, Pallas kernels: 2.53 us -> 3.44 us  [the longest x1 2.46 us: band_weights(): pl.pallas_call(band_kernel, in_specs=[hbm] * 2, out_specs=[pl.BlockSpec(m...]
  transfers between devices with their start and end apart: 3 -> 3, of which waited for: 2 -> 2; matrix products, arithmetic and copies ran while one was open for 0% -> 0% of each run, Pallas kernels for 4% -> 5%
where the time goes in v10:
time: 83.1 us; the launch traced here: 82.8 us
  blocking collectives  59.1 us (71%)
  starting transfers between devices  10.9 us (13%)
  Pallas kernels  9.72 us (12%)
  waiting for transfers between devices  2.01 us (2%)
    all_to_all x3, blocking collectives, exchange(): lax.all_to_all(pieces, DEPTH, 0, 0, axis_index_groups=groups, tiled=True)  46.7 us
    all_to_all x1, blocking collectives, shards(): own = lax.all_to_all(jnp.stack(slots, 0), 'x', 0, 0, tiled=True)  12.3 us
    ppermute x2, starting transfers between devices, depth_shift(): return lax.ppermute(block, DEPTH, pairs)  9 us
    pallas_call x1, Pallas kernels, levels(): pl.pallas_call(main_kernel, in_specs=[vmem] * 8, out_specs=[vmem, vmem],...  3.9 us
    pallas_call x1, Pallas kernels, band_weights(): pl.pallas_call(band_kernel, in_specs=[hbm] * 2, out_specs=[pl.BlockSpec(m...  2.46 us
    ppermute x2, waiting for transfers between devices, depth_shift(): return lax.ppermute(block, DEPTH, pairs)  2 us
    ppermute x1, starting transfers between devices, shards(): oth = lax.ppermute(own, 'chan', [(0, 1), (1, 0)])  1.91 us
  transfers between devices with their start and end apart: 3, of which 2 were waited for; matrix products, arithmetic and copies ran while one was open for 0% of the time, Pallas kernels for 5%

profile of v10, /device:TPU:8, one launch (start us, length us, event | category | flops | bytes accessed | tf_op | source)
XLA Modules:
  0.0 82.8 jit_solution(15122650867545654959)
XLA Ops:
  0.6 1.0 %gather.1 = bf16[20,16,128]{2,1,0:T(8,128)(2,1)S(1)} custom-call(bf16[16,2,8,128]{3,2,1,0:T(8,128)(2,1)} %feats_far.1, bf16[32,1,4,64]{3,2,1,0:T(4,128)(2,1)} %cot_far.1), custom_call_target="tpu_custom_call" | custom-call | tf_op jit(solution)/shard_map/gather/pallas_call | solution.py:341
  1.6 3.5 %collective-permute-start = (bf16[20,16,128]{2,1,0:T(8,128)(2,1)S(1)}, bf16[20,16,128]{2,1,0:T(8,128)(2,1)S(1)}, u32[]{:S(2)}, u32[]{:S(2)}) collective-permute-start(bf16[20,16,128]{2,1,0:T(8,128)(2,1)S(1)} %gather.1), channel_id=1, source_target_pairs={{0,8},{2,10},{4,12},{6,14},{8,16},{10,18},{12,20},{14,22},{16,24},... | collective-permute-start | bytes 245768 | tf_op jit(solution)/shard_map/ppermute | solution.py:19
  5.1 5.5 %collective-permute-start.1 = (bf16[20,16,128]{2,1,0:T(8,128)(2,1)S(1)}, bf16[20,16,128]{2,1,0:T(8,128)(2,1)S(1)}, u32[]{:S(2)}, u32[]{:S(2)}) collective-permute-start(bf16[20,16,128]{2,1,0:T(8,128)(2,1)S(1)} %gather.1), channel_id=1, source_target_pairs={{8,0},{10,2},{12,4},{14,6},{16,8},{18,10},{20,12},{22,14},{24,16},... | collective-permute-start | bytes 245768 | tf_op jit(solution)/shard_map/ppermute | solution.py:19
  10.7 0.4 collective-permute-done
  11.1 1.6 %collective-permute-done.1 = bf16[20,16,128]{2,1,0:T(8,128)(2,1)S(1)} collective-permute-done((bf16[20,16,128]{2,1,0:T(8,128)(2,1)S(1)}, bf16[20,16,128]{2,1,0:T(8,128)(2,1)S(1)}, u32[]{:S(2)}, u32[]{:S(2)}) %collective-permute-start.1) | collective-permute-done | bytes 81952 | tf_op jit(solution)/shard_map/ppermute | solution.py:19
  12.7 0.1 dynamic-slice_bitcast_fusion.3
  12.8 0.1 pad_maximum_fusion
  12.9 12.3 %all_to_all.20.own = bf16[4,40,16,128]{3,2,1,0:T(8,128)(2,1)S(1)} all-to-all(bf16[4,40,16,128]{3,2,1,0:T(8,128)(2,1)S(1)} %pad_maximum_fusion), channel_id=1, replica_groups=mesh['z'=8,'y'=8,'x'=4,'chan'=2] {'x'}, dimensions={0} | all-to-all | bytes 1310720 | tf_op jit(solution)/shard_map/all_to_all | solution.py:501
  25.3 1.9 %collective-permute-start.2 = (bf16[4,40,16,128]{3,2,1,0:T(8,128)(2,1)S(1)}, bf16[4,40,16,128]{3,2,1,0:T(8,128)(2,1)S(1)}, u32[]{:S(2)}, u32[]{:S(2)}) collective-permute-start(bf16[4,40,16,128]{3,2,1,0:T(8,128)(2,1)S(1)} %all_to_all.20.own), channel_id=1, source_target_pairs={{0,1},{1,0},{2,3},{3,2},{4,5},{5,4},{6,7},{7,6},{8,9},{9,8},{10,11... | collective-permute-start | bytes 1966088 | tf_op jit(solution)/shard_map/ppermute | solution.py:502
  27.2 2.5 %bands.1 = (bf16[256,1152]{1,0:T(8,128)(2,1)S(1)}, bf16[256,1152]{1,0:T(8,128)(2,1)S(1)}, bf16[128,2304]{1,0:T(8,128)(2,1)S(1)}, bf16[256,1152]{1,0:T(8,128)(2,1)S(1)}, bf16[128,2304]{1,0:T(8,128)(2,1)S(1)}) custom-call(bf16[27,32,32]{2,1,0:T(8,128)(2,1)} %bitcast.18, bf16[27,32,64]{2,1,0:T(8,128)(2,1)} %bitcast.19), custom_call_target="tpu_custom_call" | custom-call | flops 1000000000 | bytes 4000000 | tf_op jit(solution)/shard_map/bands/pallas_call | solution.py:359
  29.6 1.5 %half.1 = (bf16[9,3,128,256]{3,2,1,0:T(8,128)(2,1)S(1)}, f32[7,256,256]{2,1,0:T(8,128)S(1)}) custom-call(bf16[4,40,16,128]{3,2,1,0:T(8,128)(2,1)S(1)} %all_to_all.20.own, bf16[256,1152]{1,0:T(8,128)(2,1)S(1)} %get-tuple-element.15.t1_own), custom_call_target="tpu_custom_call" | custom-call | flops 1000000000 | bytes 5000000 | tf_op jit(solution)/shard_map/half/pallas_call | solution.py:378
  31.1 0.0 collective-permute-done.2.oth
  31.2 3.9 %levels.1 = (bf16[16,2,8,128]{3,2,1,0:T(8,128)(2,1)S(1)}, bf16[384,128]{1,0:T(8,128)(2,1)S(1)}) custom-call(bf16[4,40,16,128]{3,2,1,0:T(8,128)(2,1)S(1)} %all_to_all.20.own, bf16[4,40,16,128]{3,2,1,0:T(8,128)(2,1)S(1)} %collective-permute-done.2.oth, bf16[9,3,128,256]{3,2,1,0:T(8,128)(2,1)S(1)} %get-tuple-element.16.own_fields, ...), custom_call_target="tpu_custom_call" | custom-call | flops 10000000000 | bytes 8000000 | tf_op jit(solution)/shard_map/levels/pallas_call | solution.py:407
  35.1 11.5 %all_to_all.21 = bf16[16,24,128]{2,1,0:T(8,128)(2,1)S(1)} all-to-all(bf16[16,24,128]{2,1,0:T(8,128)(2,1)S(1)} %bitcast.17), channel_id=1, replica_groups={{0,64,8,72,2,66,10,74,4,68,12,76,6,70,14,78},{16,80,24,88,18,82,26,90,2..., dimensions={0} | all-to-all | bytes 196608 | tf_op jit(solution)/shard_map/all_to_all | solution.py:425
  46.6 23.7 %all_to_all.22 = bf16[16,24,128]{2,1,0:T(8,128)(2,1)S(1)} all-to-all(bf16[16,24,128]{2,1,0:T(8,128)(2,1)S(1)} %broadcast_in_dim.6), channel_id=1, replica_groups={{0,16,40,56,128,144,168,184,320,336,360,376,448,464,488,504},{64,80,104..., dimensions={0} | all-to-all | bytes 196608 | tf_op jit(solution)/shard_map/all_to_all | solution.py:425
  70.4 11.5 %all_to_all.23.total = bf16[16,24,128]{2,1,0:T(8,128)(2,1)S(1)} all-to-all(bf16[16,24,128]{2,1,0:T(8,128)(2,1)S(1)} %broadcast_in_dim.7), channel_id=1, replica_groups={{0,64,8,72,2,66,10,74,4,68,12,76,6,70,14,78},{16,80,24,88,18,82,26,90,2..., dimensions={0} | all-to-all | bytes 196608 | tf_op jit(solution)/shard_map/all_to_all | solution.py:425
  81.9 0.9 %split.1 = (f32[432,32]{1,0:T(8,128)}, f32[432,64]{1,0:T(8,128)}, bf16[16,2,8,128]{3,2,1,0:T(8,128)(2,1)}) custom-call(bf16[16,24,128]{2,1,0:T(8,128)(2,1)S(1)} %all_to_all.23.total, bf16[16,2,8,128]{3,2,1,0:T(8,128)(2,1)S(1)} %get-tuple-element.23.gf), custom_call_target="tpu_custom_call" | custom-call | tf_op jit(solution)/shard_map/split/pallas_call | solution.py:471
  (5 shorter events, 0.1 us)
Async XLA Ops:
  1.6 9.5 %collective-permute-start = (bf16[20,16,128]{2,1,0:T(8,128)(2,1)S(1)}, bf16[20,16,128]{2,1,0:T(8,128)(2,1)S(1)}, u32[]{:S(2)}, u32[]{:S(2)}) collective-permute-start(bf16[20,16,128]{2,1,0:T(8,128)(2,1)S(1)} %gather.1), channel_id=1, source_target_pairs={{0,8},{2,10},{4,12},{6,14},{8,16},{10,18},{12,20},{14,22},{16,24},... | collective-permute-start | bytes 245768 | tf_op jit(solution)/shard_map/ppermute | solution.py:19
  5.1 7.6 %collective-permute-start.1 = (bf16[20,16,128]{2,1,0:T(8,128)(2,1)S(1)}, bf16[20,16,128]{2,1,0:T(8,128)(2,1)S(1)}, u32[]{:S(2)}, u32[]{:S(2)}) collective-permute-start(bf16[20,16,128]{2,1,0:T(8,128)(2,1)S(1)} %gather.1), channel_id=1, source_target_pairs={{8,0},{10,2},{12,4},{14,6},{16,8},{18,10},{20,12},{22,14},{24,16},... | collective-permute-start | bytes 245768 | tf_op jit(solution)/shard_map/ppermute | solution.py:19
  25.3 5.9 %collective-permute-start.2 = (bf16[4,40,16,128]{3,2,1,0:T(8,128)(2,1)S(1)}, bf16[4,40,16,128]{3,2,1,0:T(8,128)(2,1)S(1)}, u32[]{:S(2)}, u32[]{:S(2)}) collective-permute-start(bf16[4,40,16,128]{3,2,1,0:T(8,128)(2,1)S(1)} %all_to_all.20.own), channel_id=1, source_target_pairs={{0,1},{1,0},{2,3},{3,2},{4,5},{5,4},{6,7},{7,6},{8,9},{9,8},{10,11... | collective-permute-start | bytes 1966088 | tf_op jit(solution)/shard_map/ppermute | solution.py:502

commit v11 on v9

--- a/solution.py
+++ b/solution.py
@@ -14,8 +14,12 @@
 F32 = jnp.float32
 
 
-def depth_shift(block, steps):
-    pairs = [(i, i + steps) for i in range(SLABS) if 0 <= i + steps < SLABS]
+def row_swap(block, first):
+    pairs = []
+    for low in range(first, SLABS // ROW - 1, 2):
+        for x in range(ROW):
+            here, there = low * ROW + x, (low + 1) * ROW + x
+            pairs += [(here, there), (there, here)]
     return lax.ppermute(block, DEPTH, pairs)
 
 
@@ -475,8 +479,10 @@
         jnp.transpose(weight_one, (2, 0, 1)),
         jnp.transpose(weight_two, (2, 1, 0)),
     )
-    up = depth_shift(block, ROW)
-    down = depth_shift(block, -ROW)
+    even = row_swap(block, 0)
+    odd = row_swap(block, 1)
+    upper = lax.axis_index("y") % 2 == 1
+    up, down = jnp.where(upper, even, odd), jnp.where(upper, odd, even)
 
     bands = band_weights(w1, w2)
 

time: 82.1 us -> 82.2 us (level)
  blocking collectives: 59.1 us -> 56.1 us
  waiting for transfers between devices: 1.99 us -> 4.37 us
    ppermute x2, waiting for transfers between devices: 1.98 us -> 4.36 us  [row_swap(): return lax.ppermute(block, DEPTH, pairs)]
    all_to_all x3, blocking collectives: 46.7 us -> 44.9 us  [exchange(): lax.all_to_all(pieces, DEPTH, 0, 0, axis_index_groups=groups, tiled=True)]
    all_to_all x1, blocking collectives: 12.3 us -> 11.2 us  [shards(): own = lax.all_to_all(jnp.stack(slots, 0), 'x', 0, 0, tiled=True)]
where the time goes in v11:
time: 82.2 us; the launch traced here: 81.9 us
  blocking collectives  56.1 us (68%)
  starting transfers between devices  11.5 us (14%)
  Pallas kernels  8.76 us (11%)
  waiting for transfers between devices  4.37 us (5%)
    all_to_all x3, blocking collectives, exchange(): lax.all_to_all(pieces, DEPTH, 0, 0, axis_index_groups=groups, tiled=True)  44.9 us
    all_to_all x1, blocking collectives, shards(): own = lax.all_to_all(jnp.stack(slots, 0), 'x', 0, 0, tiled=True)  11.2 us
    ppermute x2, starting transfers between devices, row_swap(): return lax.ppermute(block, DEPTH, pairs)  9.62 us
    ppermute x2, waiting for transfers between devices, row_swap(): return lax.ppermute(block, DEPTH, pairs)  4.36 us
    pallas_call x1, Pallas kernels, levels(): pl.pallas_call(main_kernel, in_specs=[vmem] * 8, out_specs=[vmem, vmem],...  3.87 us
    ppermute x1, starting transfers between devices, shards(): oth = lax.ppermute(own, 'chan', [(0, 1), (1, 0)])  1.91 us
  transfers between devices with their start and end apart: 3, of which 2 were waited for; matrix products, arithmetic and copies ran while one was open for 0% of the time, Pallas kernels for 4%

profile of v11, /device:TPU:8, one launch (start us, length us, event | category | flops | bytes accessed | tf_op | source)
XLA Modules:
  0.0 81.9 jit_solution(8058883709599840877)
XLA Ops:
  0.6 1.1 %gather.1 = (bf16[20,16,128]{2,1,0:T(8,128)(2,1)S(1)}, bf16[27,32,32]{2,1,0:T(8,128)(2,1)S(1)}, bf16[27,32,64]{2,1,0:T(8,128)(2,1)S(1)}) custom-call(bf16[16,2,8,128]{3,2,1,0:T(8,128)(2,1)} %feats_far.1, bf16[32,1,4,64]{3,2,1,0:T(4,128)(2,1)} %cot_far.1, bf16[27,32,32]{2,1,0:T(8,128)(2,1)} %bitcast.18, bf16[27,32,64]{2,1,0:T(8,128)(2,1)} %bitcast.19), custom_call_target="tpu_custom_call" | custom-call | tf_op jit(solution)/shard_map/gather/pallas_call | solution.py:332
  1.8 7.7 %collective-permute-start = (bf16[20,16,128]{2,1,0:T(8,128)(2,1)S(1)}, bf16[20,16,128]{2,1,0:T(8,128)(2,1)S(1)}, u32[]{:S(2)}, u32[]{:S(2)}) collective-permute-start(bf16[20,16,128]{2,1,0:T(8,128)(2,1)S(1)} %get-tuple-element.18), channel_id=1, source_target_pairs={{0,8},{8,0},{2,10},{10,2},{4,12},{12,4},{6,14},{14,6},{16,24},{24,... | collective-permute-start | bytes 245768 | tf_op jit(solution)/shard_map/ppermute | solution.py:23
  9.5 1.9 %collective-permute-start.1 = (bf16[20,16,128]{2,1,0:T(8,128)(2,1)S(1)}, bf16[20,16,128]{2,1,0:T(8,128)(2,1)S(1)}, u32[]{:S(2)}, u32[]{:S(2)}) collective-permute-start(bf16[20,16,128]{2,1,0:T(8,128)(2,1)S(1)} %get-tuple-element.18), channel_id=1, source_target_pairs={{8,16},{16,8},{10,18},{18,10},{12,20},{20,12},{14,22},{22,14},{24,... | collective-permute-start | bytes 245768 | tf_op jit(solution)/shard_map/ppermute | solution.py:23
  11.5 0.4 collective-permute-done
  11.9 3.9 %collective-permute-done.1 = bf16[20,16,128]{2,1,0:T(8,128)(2,1)S(1)} collective-permute-done((bf16[20,16,128]{2,1,0:T(8,128)(2,1)S(1)}, bf16[20,16,128]{2,1,0:T(8,128)(2,1)S(1)}, u32[]{:S(2)}, u32[]{:S(2)}) %collective-permute-start.1) | collective-permute-done | bytes 81952 | tf_op jit(solution)/shard_map/ppermute | solution.py:23
  15.9 0.1 dynamic-slice_bitcast_fusion.3
  16.0 0.1 pad_maximum_fusion
  16.1 11.2 %all_to_all.20.own = bf16[4,40,16,128]{3,2,1,0:T(8,128)(2,1)S(1)} all-to-all(bf16[4,40,16,128]{3,2,1,0:T(8,128)(2,1)S(1)} %pad_maximum_fusion), channel_id=1, replica_groups=mesh['z'=8,'y'=8,'x'=4,'chan'=2] {'x'}, dimensions={0} | all-to-all | bytes 1310720 | tf_op jit(solution)/shard_map/all_to_all | solution.py:496
  27.3 1.9 %collective-permute-start.2 = (bf16[4,40,16,128]{3,2,1,0:T(8,128)(2,1)S(1)}, bf16[4,40,16,128]{3,2,1,0:T(8,128)(2,1)S(1)}, u32[]{:S(2)}, u32[]{:S(2)}) collective-permute-start(bf16[4,40,16,128]{3,2,1,0:T(8,128)(2,1)S(1)} %all_to_all.20.own), channel_id=1, source_target_pairs={{0,1},{1,0},{2,3},{3,2},{4,5},{5,4},{6,7},{7,6},{8,9},{9,8},{10,11... | collective-permute-start | bytes 1966088 | tf_op jit(solution)/shard_map/ppermute | solution.py:497
  29.2 1.4 %bands.1 = (bf16[256,1152]{1,0:T(8,128)(2,1)S(1)}, bf16[256,1152]{1,0:T(8,128)(2,1)S(1)}, bf16[128,2304]{1,0:T(8,128)(2,1)S(1)}, bf16[256,1152]{1,0:T(8,128)(2,1)S(1)}, bf16[128,2304]{1,0:T(8,128)(2,1)S(1)}) custom-call(bf16[27,32,32]{2,1,0:T(8,128)(2,1)S(1)} %get-tuple-element.19.w1, bf16[27,32,64]{2,1,0:T(8,128)(2,1)S(1)} %get-tuple-element.20.w2), custom_call_target="tpu_custom_call" | custom-call | flops 1000000000 | bytes 4000000 | tf_op jit(solution)/shard_map/bands/pallas_call | solution.py:354
  30.6 1.5 %half.1 = (bf16[9,3,128,256]{3,2,1,0:T(8,128)(2,1)S(1)}, f32[7,256,256]{2,1,0:T(8,128)S(1)}) custom-call(bf16[4,40,16,128]{3,2,1,0:T(8,128)(2,1)S(1)} %all_to_all.20.own, bf16[256,1152]{1,0:T(8,128)(2,1)S(1)} %get-tuple-element.21.t1_own), custom_call_target="tpu_custom_call" | custom-call | flops 1000000000 | bytes 5000000 | tf_op jit(solution)/shard_map/half/pallas_call | solution.py:368
  32.1 0.0 collective-permute-done.2.oth
  32.1 3.9 %levels.1 = (bf16[16,2,8,128]{3,2,1,0:T(8,128)(2,1)S(1)}, bf16[384,128]{1,0:T(8,128)(2,1)S(1)}) custom-call(bf16[4,40,16,128]{3,2,1,0:T(8,128)(2,1)S(1)} %all_to_all.20.own, bf16[4,40,16,128]{3,2,1,0:T(8,128)(2,1)S(1)} %collective-permute-done.2.oth, bf16[9,3,128,256]{3,2,1,0:T(8,128)(2,1)S(1)} %get-tuple-element.22.own_fields, ...), custom_call_target="tpu_custom_call" | custom-call | flops 10000000000 | bytes 8000000 | tf_op jit(solution)/shard_map/levels/pallas_call | solution.py:397
  36.0 10.8 %all_to_all.21 = bf16[16,24,128]{2,1,0:T(8,128)(2,1)S(1)} all-to-all(bf16[16,24,128]{2,1,0:T(8,128)(2,1)S(1)} %bitcast.17), channel_id=1, replica_groups={{0,64,8,72,2,66,10,74,4,68,12,76,6,70,14,78},{16,80,24,88,18,82,26,90,2..., dimensions={0} | all-to-all | bytes 196608 | tf_op jit(solution)/shard_map/all_to_all | solution.py:415
  46.8 23.0 %all_to_all.22 = bf16[16,24,128]{2,1,0:T(8,128)(2,1)S(1)} all-to-all(bf16[16,24,128]{2,1,0:T(8,128)(2,1)S(1)} %broadcast_in_dim.6), channel_id=1, replica_groups={{0,16,40,56,128,144,168,184,320,336,360,376,448,464,488,504},{64,80,104..., dimensions={0} | all-to-all | bytes 196608 | tf_op jit(solution)/shard_map/all_to_all | solution.py:415
  69.9 11.1 %all_to_all.23.total = bf16[16,24,128]{2,1,0:T(8,128)(2,1)S(1)} all-to-all(bf16[16,24,128]{2,1,0:T(8,128)(2,1)S(1)} %broadcast_in_dim.7), channel_id=1, replica_groups={{0,64,8,72,2,66,10,74,4,68,12,76,6,70,14,78},{16,80,24,88,18,82,26,90,2..., dimensions={0} | all-to-all | bytes 196608 | tf_op jit(solution)/shard_map/all_to_all | solution.py:415
  81.0 0.9 %split.1 = (f32[432,32]{1,0:T(8,128)}, f32[432,64]{1,0:T(8,128)}, bf16[16,2,8,128]{3,2,1,0:T(8,128)(2,1)}) custom-call(bf16[16,24,128]{2,1,0:T(8,128)(2,1)S(1)} %all_to_all.23.total, bf16[16,2,8,128]{3,2,1,0:T(8,128)(2,1)S(1)} %get-tuple-element.29.gf), custom_call_target="tpu_custom_call" | custom-call | tf_op jit(solution)/shard_map/split/pallas_call | solution.py:461
  (6 shorter events, 0.1 us)
Async XLA Ops:
  1.8 10.1 %collective-permute-start = (bf16[20,16,128]{2,1,0:T(8,128)(2,1)S(1)}, bf16[20,16,128]{2,1,0:T(8,128)(2,1)S(1)}, u32[]{:S(2)}, u32[]{:S(2)}) collective-permute-start(bf16[20,16,128]{2,1,0:T(8,128)(2,1)S(1)} %get-tuple-element.18), channel_id=1, source_target_pairs={{0,8},{8,0},{2,10},{10,2},{4,12},{12,4},{6,14},{14,6},{16,24},{24,... | collective-permute-start | bytes 245768 | tf_op jit(solution)/shard_map/ppermute | solution.py:23
  9.5 6.3 %collective-permute-start.1 = (bf16[20,16,128]{2,1,0:T(8,128)(2,1)S(1)}, bf16[20,16,128]{2,1,0:T(8,128)(2,1)S(1)}, u32[]{:S(2)}, u32[]{:S(2)}) collective-permute-start(bf16[20,16,128]{2,1,0:T(8,128)(2,1)S(1)} %get-tuple-element.18), channel_id=1, source_target_pairs={{8,16},{16,8},{10,18},{18,10},{12,20},{20,12},{14,22},{22,14},{24,... | collective-permute-start | bytes 245768 | tf_op jit(solution)/shard_map/ppermute | solution.py:23
  27.3 4.8 %collective-permute-start.2 = (bf16[4,40,16,128]{3,2,1,0:T(8,128)(2,1)S(1)}, bf16[4,40,16,128]{3,2,1,0:T(8,128)(2,1)S(1)}, u32[]{:S(2)}, u32[]{:S(2)}) collective-permute-start(bf16[4,40,16,128]{3,2,1,0:T(8,128)(2,1)S(1)} %all_to_all.20.own), channel_id=1, source_target_pairs={{0,1},{1,0},{2,3},{3,2},{4,5},{5,4},{6,7},{7,6},{8,9},{9,8},{10,11... | collective-permute-start | bytes 1966088 | tf_op jit(solution)/shard_map/ppermute | solution.py:497

commit v12 on v11

--- a/solution.py
+++ b/solution.py
@@ -363,6 +363,30 @@
     )(w1, w2)
 
 
+def slot_kernel(even, block, odd, slots, rows):
+    for at, part in enumerate((even, block, odd, block, even)):
+        rows[at * 20 : (at + 1) * 20] = part[...]
+    place = position()[1]
+    x = lax.rem(place, ROW)
+    first = jnp.where(lax.rem(place // ROW, 2) == 1, 0, 40)
+    for t in range(4):
+        at = first + jnp.where(x > t, 0, jnp.where(x == t, 8, 20))
+        slots[t] = rows[pl.ds(at, 40)]
+
+
+def row_slots(even, block, odd):
+    vmem = pl.BlockSpec(memory_space=pltpu.VMEM)
+    return pl.pallas_call(
+        slot_kernel,
+        in_specs=[vmem] * 3,
+        out_specs=vmem,
+        out_shape=jax.ShapeDtypeStruct((4, 40, 16, 128), BF16),
+        scratch_shapes=[pltpu.VMEM((100, 16, 128), BF16)],
+        compiler_params=pltpu.CompilerParams(vmem_limit_bytes=4 * 2**20),
+        name="slots",
+    )(even, block, odd)
+
+
 def own_half(own, t1_own):
     vmem = pl.BlockSpec(memory_space=pltpu.VMEM)
     return pl.pallas_call(
@@ -472,7 +496,6 @@
 
 
 def shards(feats, weight_one, weight_two, cotangent):
-    x = lax.axis_index("x")
     block, w1, w2 = own_block(
         feats,
         cotangent,
@@ -481,19 +504,10 @@
     )
     even = row_swap(block, 0)
     odd = row_swap(block, 1)
-    upper = lax.axis_index("y") % 2 == 1
-    up, down = jnp.where(upper, even, odd), jnp.where(upper, odd, even)
 
     bands = band_weights(w1, w2)
 
-    three = jnp.concatenate([up, block, down], axis=0)
-    slots = [
-        lax.dynamic_slice_in_dim(
-            three, jnp.where(x > t, 0, jnp.where(x == t, 8, 20)).astype(jnp.int32), 40, 0
-        )
-        for t in range(4)
-    ]
-    own = lax.all_to_all(jnp.stack(slots, 0), "x", 0, 0, tiled=True)
+    own = lax.all_to_all(row_slots(even, block, odd), "x", 0, 0, tiled=True)
     oth = lax.ppermute(own, "chan", [(0, 1), (1, 0)])
     own_fields, own_sums = own_half(own, bands[0])
     grad_feats, part = levels((own, oth, own_fields, own_sums), bands[1:])

time: 82.2 us -> 82 us (level)
  no operation moved by 1% of the time
where the time goes in v12:
time: 82 us; the launch traced here: 81.7 us
  blocking collectives  56.1 us (68%)
  starting transfers between devices  11.5 us (14%)
  Pallas kernels  8.87 us (11%)
  waiting for transfers between devices  4.41 us (5%)
    all_to_all x3, blocking collectives, exchange(): lax.all_to_all(pieces, DEPTH, 0, 0, axis_index_groups=groups, tiled=True)  44.9 us
    all_to_all x1, blocking collectives, shards(): own = lax.all_to_all(row_slots(even, block, odd), 'x', 0, 0, tiled=True)  11.2 us
    ppermute x2, starting transfers between devices, row_swap(): return lax.ppermute(block, DEPTH, pairs)  9.62 us
    ppermute x2, waiting for transfers between devices, row_swap(): return lax.ppermute(block, DEPTH, pairs)  4.41 us
    pallas_call x1, Pallas kernels, levels(): pl.pallas_call(main_kernel, in_specs=[vmem] * 8, out_specs=[vmem, vmem],...  3.87 us
    ppermute x1, starting transfers between devices, shards(): oth = lax.ppermute(own, 'chan', [(0, 1), (1, 0)])  1.91 us
  transfers between devices with their start and end apart: 3, of which 2 were waited for; matrix products, arithmetic and copies ran while one was open for 0% of the time, Pallas kernels for 4%

profile of v12, /device:TPU:8, one launch (start us, length us, event | category | flops | bytes accessed | tf_op | source)
XLA Modules:
  0.0 81.7 jit_solution(15093145399932301054)
XLA Ops:
  0.6 1.1 %gather.1 = (bf16[20,16,128]{2,1,0:T(8,128)(2,1)S(1)}, bf16[27,32,32]{2,1,0:T(8,128)(2,1)S(1)}, bf16[27,32,64]{2,1,0:T(8,128)(2,1)S(1)}) custom-call(bf16[16,2,8,128]{3,2,1,0:T(8,128)(2,1)} %feats_far.1, bf16[32,1,4,64]{3,2,1,0:T(4,128)(2,1)} %cot_far.1, bf16[27,32,32]{2,1,0:T(8,128)(2,1)} %bitcast.10, bf16[27,32,64]{2,1,0:T(8,128)(2,1)} %bitcast.11), custom_call_target="tpu_custom_call" | custom-call | tf_op jit(solution)/shard_map/gather/pallas_call | solution.py:332
  1.8 7.7 %collective-permute-start = (bf16[20,16,128]{2,1,0:T(8,128)(2,1)S(1)}, bf16[20,16,128]{2,1,0:T(8,128)(2,1)S(1)}, u32[]{:S(2)}, u32[]{:S(2)}) collective-permute-start(bf16[20,16,128]{2,1,0:T(8,128)(2,1)S(1)} %get-tuple-element.18.block), channel_id=1, source_target_pairs={{0,8},{8,0},{2,10},{10,2},{4,12},{12,4},{6,14},{14,6},{16,24},{24,... | collective-permute-start | bytes 245768 | tf_op jit(solution)/shard_map/ppermute | solution.py:23
  9.5 1.9 %collective-permute-start.1 = (bf16[20,16,128]{2,1,0:T(8,128)(2,1)S(1)}, bf16[20,16,128]{2,1,0:T(8,128)(2,1)S(1)}, u32[]{:S(2)}, u32[]{:S(2)}) collective-permute-start(bf16[20,16,128]{2,1,0:T(8,128)(2,1)S(1)} %get-tuple-element.18.block), channel_id=1, source_target_pairs={{8,16},{16,8},{10,18},{18,10},{12,20},{20,12},{14,22},{22,14},{24,... | collective-permute-start | bytes 245768 | tf_op jit(solution)/shard_map/ppermute | solution.py:23
  11.4 0.5 collective-permute-done.even
  11.9 3.9 %collective-permute-done.1.odd = bf16[20,16,128]{2,1,0:T(8,128)(2,1)S(1)} collective-permute-done((bf16[20,16,128]{2,1,0:T(8,128)(2,1)S(1)}, bf16[20,16,128]{2,1,0:T(8,128)(2,1)S(1)}, u32[]{:S(2)}, u32[]{:S(2)}) %collective-permute-start.1) | collective-permute-done | bytes 81952 | tf_op jit(solution)/shard_map/ppermute | solution.py:23
  15.8 0.1 slots.1
  15.9 11.2 %all_to_all.20.own = bf16[4,40,16,128]{3,2,1,0:T(8,128)(2,1)S(1)} all-to-all(bf16[4,40,16,128]{3,2,1,0:T(8,128)(2,1)S(1)} %slots.1), channel_id=1, replica_groups=mesh['z'=8,'y'=8,'x'=4,'chan'=2] {'x'}, dimensions={0} | all-to-all | bytes 1310720 | tf_op jit(solution)/shard_map/all_to_all | solution.py:510
  27.1 1.9 %collective-permute-start.2 = (bf16[4,40,16,128]{3,2,1,0:T(8,128)(2,1)S(1)}, bf16[4,40,16,128]{3,2,1,0:T(8,128)(2,1)S(1)}, u32[]{:S(2)}, u32[]{:S(2)}) collective-permute-start(bf16[4,40,16,128]{3,2,1,0:T(8,128)(2,1)S(1)} %all_to_all.20.own), channel_id=1, source_target_pairs={{0,1},{1,0},{2,3},{3,2},{4,5},{5,4},{6,7},{7,6},{8,9},{9,8},{10,11... | collective-permute-start | bytes 1966088 | tf_op jit(solution)/shard_map/ppermute | solution.py:511
  29.0 1.4 %bands.1 = (bf16[256,1152]{1,0:T(8,128)(2,1)S(1)}, bf16[256,1152]{1,0:T(8,128)(2,1)S(1)}, bf16[128,2304]{1,0:T(8,128)(2,1)S(1)}, bf16[256,1152]{1,0:T(8,128)(2,1)S(1)}, bf16[128,2304]{1,0:T(8,128)(2,1)S(1)}) custom-call(bf16[27,32,32]{2,1,0:T(8,128)(2,1)S(1)} %get-tuple-element.19.w1, bf16[27,32,64]{2,1,0:T(8,128)(2,1)S(1)} %get-tuple-element.20.w2), custom_call_target="tpu_custom_call" | custom-call | flops 1000000000 | bytes 4000000 | tf_op jit(solution)/shard_map/bands/pallas_call | solution.py:354
  30.4 1.5 %half.1 = (bf16[9,3,128,256]{3,2,1,0:T(8,128)(2,1)S(1)}, f32[7,256,256]{2,1,0:T(8,128)S(1)}) custom-call(bf16[4,40,16,128]{3,2,1,0:T(8,128)(2,1)S(1)} %all_to_all.20.own, bf16[256,1152]{1,0:T(8,128)(2,1)S(1)} %get-tuple-element.21.t1_own), custom_call_target="tpu_custom_call" | custom-call | flops 1000000000 | bytes 5000000 | tf_op jit(solution)/shard_map/half/pallas_call | solution.py:392
  31.9 0.0 collective-permute-done.2.oth
  31.9 3.9 %levels.1 = (bf16[16,2,8,128]{3,2,1,0:T(8,128)(2,1)S(1)}, bf16[384,128]{1,0:T(8,128)(2,1)S(1)}) custom-call(bf16[4,40,16,128]{3,2,1,0:T(8,128)(2,1)S(1)} %all_to_all.20.own, bf16[4,40,16,128]{3,2,1,0:T(8,128)(2,1)S(1)} %collective-permute-done.2.oth, bf16[9,3,128,256]{3,2,1,0:T(8,128)(2,1)S(1)} %get-tuple-element.22.own_fields, ...), custom_call_target="tpu_custom_call" | custom-call | flops 10000000000 | bytes 8000000 | tf_op jit(solution)/shard_map/levels/pallas_call | solution.py:421
  35.8 10.8 %all_to_all.21 = bf16[16,24,128]{2,1,0:T(8,128)(2,1)S(1)} all-to-all(bf16[16,24,128]{2,1,0:T(8,128)(2,1)S(1)} %bitcast.9), channel_id=1, replica_groups={{0,64,8,72,2,66,10,74,4,68,12,76,6,70,14,78},{16,80,24,88,18,82,26,90,2..., dimensions={0} | all-to-all | bytes 196608 | tf_op jit(solution)/shard_map/all_to_all | solution.py:439
  46.6 23.0 %all_to_all.22 = bf16[16,24,128]{2,1,0:T(8,128)(2,1)S(1)} all-to-all(bf16[16,24,128]{2,1,0:T(8,128)(2,1)S(1)} %broadcast_in_dim.6), channel_id=1, replica_groups={{0,16,40,56,128,144,168,184,320,336,360,376,448,464,488,504},{64,80,104..., dimensions={0} | all-to-all | bytes 196608 | tf_op jit(solution)/shard_map/all_to_all | solution.py:439
  69.7 11.1 %all_to_all.23.total = bf16[16,24,128]{2,1,0:T(8,128)(2,1)S(1)} all-to-all(bf16[16,24,128]{2,1,0:T(8,128)(2,1)S(1)} %broadcast_in_dim.7), channel_id=1, replica_groups={{0,64,8,72,2,66,10,74,4,68,12,76,6,70,14,78},{16,80,24,88,18,82,26,90,2..., dimensions={0} | all-to-all | bytes 196608 | tf_op jit(solution)/shard_map/all_to_all | solution.py:439
  80.8 0.9 %split.1 = (f32[432,32]{1,0:T(8,128)}, f32[432,64]{1,0:T(8,128)}, bf16[16,2,8,128]{3,2,1,0:T(8,128)(2,1)}) custom-call(bf16[16,24,128]{2,1,0:T(8,128)(2,1)S(1)} %all_to_all.23.total, bf16[16,2,8,128]{3,2,1,0:T(8,128)(2,1)S(1)} %get-tuple-element.29.gf), custom_call_target="tpu_custom_call" | custom-call | tf_op jit(solution)/shard_map/split/pallas_call | solution.py:485
  (4 shorter events, 0.1 us)
Async XLA Ops:
  1.8 10.1 %collective-permute-start = (bf16[20,16,128]{2,1,0:T(8,128)(2,1)S(1)}, bf16[20,16,128]{2,1,0:T(8,128)(2,1)S(1)}, u32[]{:S(2)}, u32[]{:S(2)}) collective-permute-start(bf16[20,16,128]{2,1,0:T(8,128)(2,1)S(1)} %get-tuple-element.18.block), channel_id=1, source_target_pairs={{0,8},{8,0},{2,10},{10,2},{4,12},{12,4},{6,14},{14,6},{16,24},{24,... | collective-permute-start | bytes 245768 | tf_op jit(solution)/shard_map/ppermute | solution.py:23
  9.5 6.3 %collective-permute-start.1 = (bf16[20,16,128]{2,1,0:T(8,128)(2,1)S(1)}, bf16[20,16,128]{2,1,0:T(8,128)(2,1)S(1)}, u32[]{:S(2)}, u32[]{:S(2)}) collective-permute-start(bf16[20,16,128]{2,1,0:T(8,128)(2,1)S(1)} %get-tuple-element.18.block), channel_id=1, source_target_pairs={{8,16},{16,8},{10,18},{18,10},{12,20},{20,12},{14,22},{22,14},{24,... | collective-permute-start | bytes 245768 | tf_op jit(solution)/shard_map/ppermute | solution.py:23
  27.1 4.8 %collective-permute-start.2 = (bf16[4,40,16,128]{3,2,1,0:T(8,128)(2,1)S(1)}, bf16[4,40,16,128]{3,2,1,0:T(8,128)(2,1)S(1)}, u32[]{:S(2)}, u32[]{:S(2)}) collective-permute-start(bf16[4,40,16,128]{3,2,1,0:T(8,128)(2,1)S(1)} %all_to_all.20.own), channel_id=1, source_target_pairs={{0,1},{1,0},{2,3},{3,2},{4,5},{5,4},{6,7},{7,6},{8,9},{9,8},{10,11... | collective-permute-start | bytes 1966088 | tf_op jit(solution)/shard_map/ppermute | solution.py:511

commit v13 on v12

--- a/solution.py
+++ b/solution.py
@@ -137,11 +137,14 @@
 
 
 def shifted(value, step):
+    value = value.astype(BF16)
     lanes = value.shape[-1]
-    lane = lax.broadcasted_iota(jnp.int32, value.shape, 1)
-    low = jnp.where(lane < step, 0.0, pltpu.roll(value, step, 1))
-    high = jnp.where(lane >= lanes - step, 0.0, pltpu.roll(value, lanes - step, 1))
-    return low.astype(BF16), value.astype(BF16), high.astype(BF16)
+    lane = lax.broadcasted_iota(jnp.int32, (1, lanes), 1)
+    inner = jnp.where(lane < step, 0.0, 1.0).astype(BF16)
+    outer = jnp.where(lane >= lanes - step, 0.0, 1.0).astype(BF16)
+    low = pltpu.roll(value, step, 1) * inner
+    high = pltpu.roll(value, lanes - step, 1) * outer
+    return low, value, high
 
 
 def plane_tiles(x):
@@ -161,7 +164,7 @@
     def load_plane(j):
         at, start = planes[j]
         plane = tiles[at, start : start + 8].reshape(128, 128)
-        for c, part in enumerate(shifted(plane.astype(F32), 1)):
+        for c, part in enumerate(shifted(plane, 1)):
             if j <= 8:
                 fields[j, c, :, :128] = part
             if j >= 7:
@@ -217,7 +220,7 @@
         total = total + jnp.where(even, pltpu.roll(total, 127, 1), pltpu.roll(total, 1, 1))
         at = place + (j - 3)
         factor = jnp.where((at >= 0) & (at < SLABS), 0.125, 0.0)
-        pooled = (total * factor).astype(BF16).astype(F32)
+        pooled = (total * factor).astype(BF16)
         for c, part in enumerate(shifted(pooled, 2)):
             if j <= 4:
                 QP[j, c, :, :128] = part
@@ -277,7 +280,7 @@
         factor = jnp.where((at >= 0) & (at < SLABS), 0.125, 0.0)
         part = (back[:, f * 128 : (f + 1) * 128] * factor).reshape(4, 1, 32, 128)
         wide = jnp.concatenate([part, part], axis=1).reshape(256, 128)
-        grad = (wide * SL[q]).astype(BF16).astype(F32)
+        grad = (wide * SL[q]).astype(BF16)
         for c, piece in enumerate(shifted(grad, 1)):
             if q <= 2:
                 HP[q, c, :, :128] = piece

time: 82 us -> 82.1 us (level)
  no operation moved by 1% of the time
where the time goes in v13:
time: 82.1 us; the launch traced here: 81.7 us
  blocking collectives  56.1 us (68%)
  starting transfers between devices  11.5 us (14%)
  Pallas kernels  8.92 us (11%)
  waiting for transfers between devices  4.41 us (5%)
    all_to_all x3, blocking collectives, exchange(): lax.all_to_all(pieces, DEPTH, 0, 0, axis_index_groups=groups, tiled=True)  44.9 us
    all_to_all x1, blocking collectives, shards(): own = lax.all_to_all(row_slots(even, block, odd), 'x', 0, 0, tiled=True)  11.2 us
    ppermute x2, starting transfers between devices, row_swap(): return lax.ppermute(block, DEPTH, pairs)  9.62 us
    ppermute x2, waiting for transfers between devices, row_swap(): return lax.ppermute(block, DEPTH, pairs)  4.41 us
    pallas_call x1, Pallas kernels, levels(): pl.pallas_call(main_kernel, in_specs=[vmem] * 8, out_specs=[vmem, vmem],...  3.9 us
    ppermute x1, starting transfers between devices, shards(): oth = lax.ppermute(own, 'chan', [(0, 1), (1, 0)])  1.91 us
  transfers between devices with their start and end apart: 3, of which 2 were waited for; matrix products, arithmetic and copies ran while one was open for 0% of the time, Pallas kernels for 4%

profile of v13, /device:TPU:8, one launch (start us, length us, event | category | flops | bytes accessed | tf_op | source)
XLA Modules:
  0.0 81.7 jit_solution(10557124036181726237)
XLA Ops:
  0.6 1.1 %gather.1 = (bf16[20,16,128]{2,1,0:T(8,128)(2,1)S(1)}, bf16[27,32,32]{2,1,0:T(8,128)(2,1)S(1)}, bf16[27,32,64]{2,1,0:T(8,128)(2,1)S(1)}) custom-call(bf16[16,2,8,128]{3,2,1,0:T(8,128)(2,1)} %feats_far.1, bf16[32,1,4,64]{3,2,1,0:T(4,128)(2,1)} %cot_far.1, bf16[27,32,32]{2,1,0:T(8,128)(2,1)} %bitcast.10, bf16[27,32,64]{2,1,0:T(8,128)(2,1)} %bitcast.11), custom_call_target="tpu_custom_call" | custom-call | tf_op jit(solution)/shard_map/gather/pallas_call | solution.py:335
  1.8 7.7 %collective-permute-start = (bf16[20,16,128]{2,1,0:T(8,128)(2,1)S(1)}, bf16[20,16,128]{2,1,0:T(8,128)(2,1)S(1)}, u32[]{:S(2)}, u32[]{:S(2)}) collective-permute-start(bf16[20,16,128]{2,1,0:T(8,128)(2,1)S(1)} %get-tuple-element.18.block), channel_id=1, source_target_pairs={{0,8},{8,0},{2,10},{10,2},{4,12},{12,4},{6,14},{14,6},{16,24},{24,... | collective-permute-start | bytes 245768 | tf_op jit(solution)/shard_map/ppermute | solution.py:23
  9.5 1.9 %collective-permute-start.1 = (bf16[20,16,128]{2,1,0:T(8,128)(2,1)S(1)}, bf16[20,16,128]{2,1,0:T(8,128)(2,1)S(1)}, u32[]{:S(2)}, u32[]{:S(2)}) collective-permute-start(bf16[20,16,128]{2,1,0:T(8,128)(2,1)S(1)} %get-tuple-element.18.block), channel_id=1, source_target_pairs={{8,16},{16,8},{10,18},{18,10},{12,20},{20,12},{14,22},{22,14},{24,... | collective-permute-start | bytes 245768 | tf_op jit(solution)/shard_map/ppermute | solution.py:23
  11.4 0.5 collective-permute-done.even
  11.9 3.9 %collective-permute-done.1.odd = bf16[20,16,128]{2,1,0:T(8,128)(2,1)S(1)} collective-permute-done((bf16[20,16,128]{2,1,0:T(8,128)(2,1)S(1)}, bf16[20,16,128]{2,1,0:T(8,128)(2,1)S(1)}, u32[]{:S(2)}, u32[]{:S(2)}) %collective-permute-start.1) | collective-permute-done | bytes 81952 | tf_op jit(solution)/shard_map/ppermute | solution.py:23
  15.8 0.1 slots.1
  15.9 11.2 %all_to_all.20.own = bf16[4,40,16,128]{3,2,1,0:T(8,128)(2,1)S(1)} all-to-all(bf16[4,40,16,128]{3,2,1,0:T(8,128)(2,1)S(1)} %slots.1), channel_id=1, replica_groups=mesh['z'=8,'y'=8,'x'=4,'chan'=2] {'x'}, dimensions={0} | all-to-all | bytes 1310720 | tf_op jit(solution)/shard_map/all_to_all | solution.py:513
  27.1 1.9 %collective-permute-start.2 = (bf16[4,40,16,128]{3,2,1,0:T(8,128)(2,1)S(1)}, bf16[4,40,16,128]{3,2,1,0:T(8,128)(2,1)S(1)}, u32[]{:S(2)}, u32[]{:S(2)}) collective-permute-start(bf16[4,40,16,128]{3,2,1,0:T(8,128)(2,1)S(1)} %all_to_all.20.own), channel_id=1, source_target_pairs={{0,1},{1,0},{2,3},{3,2},{4,5},{5,4},{6,7},{7,6},{8,9},{9,8},{10,11... | collective-permute-start | bytes 1966088 | tf_op jit(solution)/shard_map/ppermute | solution.py:514
  29.0 1.4 %bands.1 = (bf16[256,1152]{1,0:T(8,128)(2,1)S(1)}, bf16[256,1152]{1,0:T(8,128)(2,1)S(1)}, bf16[128,2304]{1,0:T(8,128)(2,1)S(1)}, bf16[256,1152]{1,0:T(8,128)(2,1)S(1)}, bf16[128,2304]{1,0:T(8,128)(2,1)S(1)}) custom-call(bf16[27,32,32]{2,1,0:T(8,128)(2,1)S(1)} %get-tuple-element.19.w1, bf16[27,32,64]{2,1,0:T(8,128)(2,1)S(1)} %get-tuple-element.20.w2), custom_call_target="tpu_custom_call" | custom-call | flops 1000000000 | bytes 4000000 | tf_op jit(solution)/shard_map/bands/pallas_call | solution.py:357
  30.4 1.5 %half.1 = (bf16[9,3,128,256]{3,2,1,0:T(8,128)(2,1)S(1)}, f32[7,256,256]{2,1,0:T(8,128)S(1)}) custom-call(bf16[4,40,16,128]{3,2,1,0:T(8,128)(2,1)S(1)} %all_to_all.20.own, bf16[256,1152]{1,0:T(8,128)(2,1)S(1)} %get-tuple-element.21.t1_own), custom_call_target="tpu_custom_call" | custom-call | flops 1000000000 | bytes 5000000 | tf_op jit(solution)/shard_map/half/pallas_call | solution.py:395
  32.0 0.0 collective-permute-done.2.oth
  32.0 3.9 %levels.1 = (bf16[16,2,8,128]{3,2,1,0:T(8,128)(2,1)S(1)}, bf16[384,128]{1,0:T(8,128)(2,1)S(1)}) custom-call(bf16[4,40,16,128]{3,2,1,0:T(8,128)(2,1)S(1)} %all_to_all.20.own, bf16[4,40,16,128]{3,2,1,0:T(8,128)(2,1)S(1)} %collective-permute-done.2.oth, bf16[9,3,128,256]{3,2,1,0:T(8,128)(2,1)S(1)} %get-tuple-element.22.own_fields, ...), custom_call_target="tpu_custom_call" | custom-call | flops 10000000000 | bytes 8000000 | tf_op jit(solution)/shard_map/levels/pallas_call | solution.py:424
  35.9 10.8 %all_to_all.21 = bf16[16,24,128]{2,1,0:T(8,128)(2,1)S(1)} all-to-all(bf16[16,24,128]{2,1,0:T(8,128)(2,1)S(1)} %bitcast.9), channel_id=1, replica_groups={{0,64,8,72,2,66,10,74,4,68,12,76,6,70,14,78},{16,80,24,88,18,82,26,90,2..., dimensions={0} | all-to-all | bytes 196608 | tf_op jit(solution)/shard_map/all_to_all | solution.py:442
  46.7 23.0 %all_to_all.22 = bf16[16,24,128]{2,1,0:T(8,128)(2,1)S(1)} all-to-all(bf16[16,24,128]{2,1,0:T(8,128)(2,1)S(1)} %broadcast_in_dim.6), channel_id=1, replica_groups={{0,16,40,56,128,144,168,184,320,336,360,376,448,464,488,504},{64,80,104..., dimensions={0} | all-to-all | bytes 196608 | tf_op jit(solution)/shard_map/all_to_all | solution.py:442
  69.8 11.1 %all_to_all.23.total = bf16[16,24,128]{2,1,0:T(8,128)(2,1)S(1)} all-to-all(bf16[16,24,128]{2,1,0:T(8,128)(2,1)S(1)} %broadcast_in_dim.7), channel_id=1, replica_groups={{0,64,8,72,2,66,10,74,4,68,12,76,6,70,14,78},{16,80,24,88,18,82,26,90,2..., dimensions={0} | all-to-all | bytes 196608 | tf_op jit(solution)/shard_map/all_to_all | solution.py:442
  80.9 0.9 %split.1 = (f32[432,32]{1,0:T(8,128)}, f32[432,64]{1,0:T(8,128)}, bf16[16,2,8,128]{3,2,1,0:T(8,128)(2,1)}) custom-call(bf16[16,24,128]{2,1,0:T(8,128)(2,1)S(1)} %all_to_all.23.total, bf16[16,2,8,128]{3,2,1,0:T(8,128)(2,1)S(1)} %get-tuple-element.29.gf), custom_call_target="tpu_custom_call" | custom-call | tf_op jit(solution)/shard_map/split/pallas_call | solution.py:488
  (4 shorter events, 0.1 us)
Async XLA Ops:
  1.8 10.1 %collective-permute-start = (bf16[20,16,128]{2,1,0:T(8,128)(2,1)S(1)}, bf16[20,16,128]{2,1,0:T(8,128)(2,1)S(1)}, u32[]{:S(2)}, u32[]{:S(2)}) collective-permute-start(bf16[20,16,128]{2,1,0:T(8,128)(2,1)S(1)} %get-tuple-element.18.block), channel_id=1, source_target_pairs={{0,8},{8,0},{2,10},{10,2},{4,12},{12,4},{6,14},{14,6},{16,24},{24,... | collective-permute-start | bytes 245768 | tf_op jit(solution)/shard_map/ppermute | solution.py:23
  9.5 6.3 %collective-permute-start.1 = (bf16[20,16,128]{2,1,0:T(8,128)(2,1)S(1)}, bf16[20,16,128]{2,1,0:T(8,128)(2,1)S(1)}, u32[]{:S(2)}, u32[]{:S(2)}) collective-permute-start(bf16[20,16,128]{2,1,0:T(8,128)(2,1)S(1)} %get-tuple-element.18.block), channel_id=1, source_target_pairs={{8,16},{16,8},{10,18},{18,10},{12,20},{20,12},{14,22},{22,14},{24,... | collective-permute-start | bytes 245768 | tf_op jit(solution)/shard_map/ppermute | solution.py:23
  27.1 4.8 %collective-permute-start.2 = (bf16[4,40,16,128]{3,2,1,0:T(8,128)(2,1)S(1)}, bf16[4,40,16,128]{3,2,1,0:T(8,128)(2,1)S(1)}, u32[]{:S(2)}, u32[]{:S(2)}) collective-permute-start(bf16[4,40,16,128]{3,2,1,0:T(8,128)(2,1)S(1)} %all_to_all.20.own), channel_id=1, source_target_pairs={{0,1},{1,0},{2,3},{3,2},{4,5},{5,4},{6,7},{7,6},{8,9},{9,8},{10,11... | collective-permute-start | bytes 1966088 | tf_op jit(solution)/shard_map/ppermute | solution.py:514
